TPU v7x, 128 devices: a whole 4x4x4 slice. The times are simulated.
128 devices in a mesh: gx: 4 (over x), gy: 4 (over y_lo, core), gz: 8 (over z, y_hi).
Axes of the slice: x: 4, y: 4 (y_hi: 2, y_lo: 2; y = y_hi * 2 + y_lo), z: 4, core: 2. Of those that a mesh axis runs over, the one named last changes fastest.
Arguments:
- layer_input: bfloat16 [4096, 4096], P('gz', ('gx', 'gy')), may hold values from -6 to 6
- modality: int32 [4096], P('gz'), may hold values 0 or 1
- image_spans: int32 [2, 8], replicated, may hold values from 0 to 4096, as said below
- norm_gain: float32 [2, 4096], P(None, ('gx', 'gy')), may hold values from 0.1 to 1.9
- w_qkv: bfloat16 [3, 4096, 2048], P(None, 'gz', ('gx', 'gy')), as said below
- w_out: bfloat16 [2048, 4096], P(('gx', 'gy'), 'gz'), may hold values from -0.125 to 0.125
- grad_out: bfloat16 [4096, 4096], P('gz', ('gx', 'gy')), may hold values from -6 to 6
Outputs:
- attn_out: bfloat16 [4096, 4096], P('gz', ('gx', 'gy'))
- grad_in: bfloat16 [4096, 4096], P('gz', ('gx', 'gy'))
- grad_qkv: float32 [3, 4096, 2048], P(None, 'gz', ('gx', 'gy'))
- grad_wout: float32 [2048, 4096], P(('gx', 'gy'), 'gz')
- grad_gain: float32 [2, 4096], P(None, ('gx', 'gy'))
Inputs may be any that keep to these rules, and one draw needn't show every extreme that they name: `image_spans`: row 0 holds the first position of each of 8 image spans, in increasing order, and row 1 one past its last; spans are disjoint and none is empty. `w_qkv`: entries are at most 20 * 4096 ** -0.5 in magnitude.
All inputs are finite; a program needn't handle non-finite values. No bound on the sum of `modality` on one device may be relied on, other than what follows from the above.
Results may differ from a plain program's by a relative error of at most 0.035.
The roundings to bfloat16 on the way count: a program that leaves them out, or rounds other values in their place, can miss the bound.
Values may be sent and summed in bfloat16 or wider, within the bound.
No kernel may reach another device: no remote copies, remote signals or barrier semaphores. Data moves between devices by JAX's collectives and lax.ppermute only.
A program may use at most 128 MiB of HBM per device.

v0:
```python
import math

import jax
import jax.numpy as jnp
from jax import lax
from jax.experimental import pallas as pl
from jax.experimental.pallas import tpu as pltpu
from jax.sharding import Mesh
from jax.sharding import PartitionSpec as P


epsilon = 1e-05
masked_low = -1e30
GROUP = ("x", "h", "c")
TOKENS_AXES = ("z", "u")
F32 = jnp.float32
BF16 = jnp.bfloat16
TURNS = (0, 1, 3, 2)
NT = (((1,), (1,)), ((), ()))
TN = (((0,), (0,)), ((), ()))
SMEM = pl.BlockSpec(memory_space=pltpu.SMEM)
PARAMS = pltpu.CompilerParams(vmem_limit_bytes=60 * 1024 * 1024)


def swap(a, axis):
    return lax.ppermute(a, axis, [(0, 1), (1, 0)])


def turn(a, d):
    return lax.ppermute(a, "x", [(i, (i + d) % 4) for i in range(4)])


def spread(block):
    pair = jnp.stack([block, swap(block, "h")])
    own = [pair] + [turn(pair, d) for d in TURNS[1:]]
    return own + [swap(a, "c") for a in own]


def exchange(blocks, axis):
    return lax.all_to_all(blocks, axis, 0, 0, tiled=True)


def copies(x, count):
    return jnp.broadcast_to(x[None], (count, *x.shape))


def three_parts(g):
    high = lax.reduce_precision(g, 8, 7)
    rest = g - high
    mid = lax.reduce_precision(rest, 8, 7)
    return high, mid, rest - mid


def dot(a, b, dims=(((1,), (0,)), ((), ()))):
    return lax.dot_general(a, b, dims, preferred_element_type=F32)


def shape(dims, kind=BF16):
    return jax.ShapeDtypeStruct(dims, kind)


def fixed(*dims):
    return pl.BlockSpec(dims, lambda *i: (0,) * len(dims))


def pack_kernel(w, out):
    for m in range(3):
        block = w[m].T
        for k in range(8):
            out[k, 0, m * 128 : (m + 1) * 128, :] = block


def pack_weights(w):
    return pl.pallas_call(
        pack_kernel,
        name="pack_weights",
        grid=(2,),
        in_specs=[pl.BlockSpec((3, 256, 128), lambda s: (0, s, 0))],
        out_specs=pl.BlockSpec((8, 1, 384, 256), lambda s: (0, s, 0, 0)),
        out_shape=shape((8, 2, 384, 256)),
        compiler_params=PARAMS,
    )(w)


def normalize_kernel(idx, *refs):
    xs, gains = refs[:8], refs[8:16]
    mod, normed, inv_out = refs[16:]
    rows = mod.shape[0]
    squares = jnp.zeros((rows, 256), F32)
    for a in xs:
        for s in range(2):
            xb = a[s].astype(F32)
            squares = squares + xb * xb
    inv = lax.rsqrt(jnp.sum(squares, axis=1, keepdims=True) / 4096 + epsilon)
    inv_out[...] = inv
    second = mod[...] == 1
    for n in range(16):
        a, s = n // 2, n % 2
        g = gains[a][s].astype(F32)
        g0 = (g[0:1] + g[2:3]) + g[4:5]
        g1 = (g[1:2] + g[3:4]) + g[5:6]
        scaled = xs[a][s].astype(F32) * inv
        normed[idx[n]] = (scaled * jnp.where(second, g1, g0)).astype(BF16)


def normalize(idx, xs, modality):
    tile = 128
    rows = lambda cols: pl.BlockSpec((tile, cols), lambda i: (i, 0))
    return pl.pallas_call(
        normalize_kernel,
        name="normalize",
        grid=(512 // tile,),
        in_specs=[SMEM]
        + [pl.BlockSpec((2, tile, 256), lambda i: (0, i, 0))] * 8
        + [pl.BlockSpec((2, 16, 256), lambda i: (0, 32, 0))] * 8
        + [rows(1)],
        out_specs=[pl.BlockSpec((16, tile, 256), lambda i: (0, i, 0)), rows(1)],
        out_shape=[shape((16, 512, 256)), shape((512, 1), F32)],
        compiler_params=PARAMS,
    )(idx, *xs, *xs, modality[:, None])


def project_kernel(normed, w, q, kv, kv_copies, acc):
    step = pl.program_id(0)
    total = dot(normed[0], w[0], NT)
    for k in range(1, 8):
        total = total + dot(normed[k], w[k], NT)

    @pl.when(step == 0)
    def _():
        acc[...] = total

    @pl.when(step == 1)
    def _():
        both = (acc[...] + total).astype(BF16)
        q[...] = both[:, 0:128]
        kv[...] = both[:, 128:384]
        for k in range(8):
            kv_copies[k] = both[:, 128:384]


def project(normed, w_t):
    return pl.pallas_call(
        project_kernel,
        name="project",
        grid=(2,),
        in_specs=[
            pl.BlockSpec((8, 512, 256), lambda j: (j, 0, 0)),
            pl.BlockSpec((8, 384, 256), lambda j: (j, 0, 0)),
        ],
        out_specs=[fixed(512, 128), fixed(512, 256), fixed(8, 512, 256)],
        out_shape=[shape((512, 128)), shape((512, 256)), shape((8, 512, 256))],
        scratch_shapes=[pltpu.VMEM((512, 384), F32)],
        compiler_params=PARAMS,
    )(normed, w_t)


def upstream_kernel(idx, *refs):
    gs, w, out, ordered = refs[:8], refs[8], refs[9], refs[10]
    acc = jnp.zeros(out.shape, F32)
    for n in range(16):
        g = gs[n // 2][n % 2]
        ordered[idx[n]] = g
        acc = acc + dot(g, w[idx[n]], NT)
    out[...] = acc.astype(BF16)


def upstream(idx, gs, wo):
    tile = 128
    return pl.pallas_call(
        upstream_kernel,
        name="upstream",
        grid=(512 // tile,),
        in_specs=[SMEM]
        + [pl.BlockSpec((2, tile, 256), lambda i: (0, i, 0))] * 8
        + [fixed(16, 128, 256)],
        out_specs=[
            pl.BlockSpec((tile, 128), lambda i: (i, 0)),
            pl.BlockSpec((16, tile, 256), lambda i: (0, i, 0)),
        ],
        out_shape=[shape((512, 128)), shape((16, 512, 256))],
        compiler_params=PARAMS,
    )(idx, *gs, wo)


KEY_BLOCK = 512
SCALE = 1.0 / math.sqrt(128)
TO_BASE2 = SCALE * math.log2(math.e)


def masked_scores(b, kv, q, edge):
    s = dot(kv[pl.ds(b * KEY_BLOCK, KEY_BLOCK), 0:128], q[...], NT) * TO_BASE2
    pos = lax.broadcasted_iota(jnp.int32, s.shape, 0) + b * KEY_BLOCK
    return jnp.where(pos < edge, s, masked_low)


def forward_kernel(limit, q, kv, att, att_t, lse, s_all):
    count = kv.shape[0] // KEY_BLOCK
    cols = q.shape[0]
    edge = limit[...]

    def scores(b, top):
        s = masked_scores(b, kv, q, edge)
        s_all[pl.ds(b * KEY_BLOCK, KEY_BLOCK), :] = s
        return jnp.maximum(top, jnp.max(s, axis=0, keepdims=True))

    top = lax.fori_loop(0, count, scores, jnp.full((1, cols), masked_low, F32))

    def sums(b, total):
        at = pl.ds(b * KEY_BLOCK, KEY_BLOCK)
        e = jnp.exp2(s_all[at, :] - top)
        s_all[at, :] = e
        return total + jnp.sum(e, axis=0, keepdims=True)

    total = lax.fori_loop(0, count, sums, jnp.zeros((1, cols), F32))
    inv = 1.0 / total
    lse[...] = top + jnp.log2(total)

    def attend(b, acc):
        at = pl.ds(b * KEY_BLOCK, KEY_BLOCK)
        return acc + dot(kv[at, 128:256], (s_all[at, :] * inv).astype(BF16), TN)

    out_t = lax.fori_loop(0, count, attend, jnp.zeros((128, cols), F32)).astype(BF16)
    att_t[...] = out_t
    att[...] = out_t.T


def forward(limit, q, kv):
    return pl.pallas_call(
        forward_kernel,
        name="forward",
        out_shape=[shape((512, 128)), shape((128, 512)), shape((1, 512), F32)],
        scratch_shapes=[pltpu.VMEM((4096, 512), F32)],
        compiler_params=PARAMS,
    )(limit, q, kv)


def backward_kernel(limit, lse, q, kv, da, att_t, dq, dkv):
    count = kv.shape[0] // KEY_BLOCK
    edge = limit[...]
    da_t = da[...].T
    row_dots = jnp.sum(att_t[...].astype(F32) * da_t.astype(F32), axis=0, keepdims=True)

    def back(b, acc):
        at = pl.ds(b * KEY_BLOCK, KEY_BLOCK)
        p = jnp.exp2(masked_scores(b, kv, q, edge) - lse[...])
        d_probs = dot(kv[at, 128:256], da[...], NT)
        ds = (p * (d_probs - row_dots) * SCALE).astype(BF16)
        dkv[at, 0:128] = dot(ds, q[...]).astype(BF16)
        dkv[at, 128:256] = dot(p.astype(BF16), da[...]).astype(BF16)
        return acc + dot(kv[at, 0:128], ds, TN)

    dq_t = lax.fori_loop(0, count, back, jnp.zeros((128, q.shape[0]), F32))
    dq[...] = dq_t.astype(BF16).T


def backward(limit, lse, q, kv, da, att_t):
    return pl.pallas_call(
        backward_kernel,
        name="backward",
        out_shape=[shape((512, 128)), shape((4096, 256))],
        compiler_params=PARAMS,
    )(limit, lse, q, kv, da, att_t)


def split_rows(dots):
    rows = []
    for p in (dots[:, 0:256], dots[:, 256:512]):
        high = p.astype(BF16).astype(F32)
        mid = (p - high).astype(BF16).astype(F32)
        rows.append((high, mid, p - high - mid))
    kind = lax.broadcasted_iota(jnp.int32, (16, 256), 0)
    both = jnp.zeros((16, 256), F32)
    for r in range(6):
        both = jnp.where(kind == r, rows[r % 2][r // 2], both)
    return both.astype(BF16)


def joined_rows(block):
    t = block.astype(F32)
    return (t[0:2] + t[2:4]) + t[4:6]


def collect_kernel(dkv, dq, q, kv, g_out, g_t, dots):
    total = dkv[0].astype(F32)
    for k in range(1, 8):
        total = total + dkv[k].astype(F32)
    g = jnp.concatenate([dq[...], total.astype(BF16)], axis=1)
    g_out[...] = g
    g_t[...] = g.T
    gf = g.astype(F32)
    prod = gf[:, 0:128] * q[...].astype(F32)
    prod = prod + gf[:, 128:256] * kv[:, 0:128].astype(F32)
    prod = prod + gf[:, 256:384] * kv[:, 128:256].astype(F32)
    dots[...] = lax.dot_general(
        jnp.ones((8, 128), F32), prod, NT, precision=lax.Precision.HIGHEST, preferred_element_type=F32
    )


def collect(dkv, dq, q, kv):
    return pl.pallas_call(
        collect_kernel,
        name="collect",
        out_shape=[shape((512, 384)), shape((384, 512)), shape((8, 512), F32)],
        compiler_params=PARAMS,
    )(dkv, dq, q, kv)


def input_grad_kernel(idx, g, g2, w, w2, dots, dots2, *outs):
    rows = split_rows(dots[0:1] + dots2[0:1])
    for n in range(8):
        out, at = outs[n // 2], idx[n]
        both = dot(g[...], w[at]) + dot(g2[...], w2[at])
        out[n % 2, 0:512, :] = both.astype(BF16)
        out[n % 2, 512:528, :] = rows


def input_grad(idx, g, g2, w, w2, dots, dots2):
    vmem = pl.BlockSpec(memory_space=pltpu.VMEM)
    return pl.pallas_call(
        input_grad_kernel,
        name="input_grad",
        in_specs=[SMEM] + [vmem] * 6,
        out_shape=[shape((2, 528, 256))] * 4,
        compiler_params=PARAMS,
    )(idx, g, g2, w, w2, dots, dots2)


def weight_grad_kernel(left, right, out):
    for k in range(right.shape[0]):
        out[k] = dot(left[...], right[k]).astype(BF16)


def weight_grad(left, right):
    rows = left.shape[0]
    return pl.pallas_call(
        weight_grad_kernel,
        name="weight_grad",
        grid=(2,),
        in_specs=[fixed(rows, 512), pl.BlockSpec((8, 512, 256), lambda j: (j, 0, 0))],
        out_specs=pl.BlockSpec((8, rows, 256), lambda j: (j, 0, 0)),
        out_shape=shape((16, rows, 256)),
        compiler_params=PARAMS,
    )(left, right)


def add_up_kernel(*refs):
    terms, out = refs[:-1], refs[-1]
    total = terms[0][0, 0:512].astype(F32)
    dots = joined_rows(terms[0][0, 512:528])
    for t in terms[1:]:
        total = total + t[0, 0:512].astype(F32)
        dots = dots + joined_rows(t[0, 512:528])
    out[0:512] = total.astype(BF16)
    out[512:528] = split_rows(jnp.concatenate([dots[0:1], dots[1:2]], axis=1))


def add_up(terms):
    return pl.pallas_call(
        add_up_kernel,
        name="add_up",
        grid=(1,),
        in_specs=[pl.BlockSpec((1, 528, 256), lambda i: (1, 0, 0))] * len(terms),
        out_specs=fixed(528, 256),
        out_shape=shape((528, 256)),
        compiler_params=PARAMS,
    )(*terms)


def finish_kernel(*refs):
    terms, (last, x, inv, mod, gain, grad_in, local_gain) = refs[:4], refs[4:]
    gn = last[0:512].astype(F32)
    dots = joined_rows(last[512:528])
    for t in terms:
        gn = gn + t[0, 0:512].astype(F32)
        dots = dots + joined_rows(t[0, 512:528])
    columns = [jnp.broadcast_to(dots[r : r + 1], (128, 256)).T[:, 0:1] for r in range(2)]
    mean = jnp.concatenate(columns, axis=0) / 4096
    second = mod[...] == 1
    scaled = x[...].astype(F32) * inv[...]
    up = gn * jnp.where(second, gain[1:2], gain[0:1])
    grad_in[...] = (inv[...] * (up - scaled * mean)).astype(BF16)
    each = gn * scaled
    sums = [jnp.sum(jnp.where(second, b, a), axis=0, keepdims=True) for a, b in ((each, 0.0), (0.0, each))]
    for k in range(8):
        local_gain[k, 0:1] = sums[0]
        local_gain[k, 1:2] = sums[1]


def finish(terms, last, x, inv, modality, gain):
    return pl.pallas_call(
        finish_kernel,
        name="finish",
        grid=(1,),
        in_specs=[pl.BlockSpec((1, 528, 256), lambda i: (0, 0, 0))] * 4
        + [fixed(528, 256), fixed(512, 256), fixed(512, 1), fixed(512, 1), fixed(2, 256)],
        out_specs=[fixed(512, 256), fixed(8, 2, 256)],
        out_shape=[shape((512, 256)), shape((8, 2, 256), F32)],
        compiler_params=PARAMS,
    )(*terms, last, x, inv, modality[:, None], gain)


def output_kernel(idx, *refs):
    atts, rows, out = refs[:8], refs[8], refs[9]
    total = jnp.zeros(out.shape, F32)
    for n in range(16):
        total = total + dot(atts[n // 2][n % 2], rows[idx[n]]).astype(BF16).astype(F32)
    out[...] = total.astype(BF16)


def output(idx, atts, rows):
    tile = 128
    return pl.pallas_call(
        output_kernel,
        name="output",
        grid=(512 // tile,),
        in_specs=[SMEM]
        + [pl.BlockSpec((2, tile, 128), lambda i: (0, i, 0))] * 8
        + [fixed(16, 128, 256)],
        out_specs=pl.BlockSpec((tile, 256), lambda i: (i, 0)),
        out_shape=shape((512, 256)),
        compiler_params=PARAMS,
    )(idx, *atts, rows)


def sum_qkv_kernel(parts, out):
    total = parts[0, 0].astype(F32)
    for k in range(1, 8):
        total = total + parts[k, 0].astype(F32)
    for m in range(3):
        out[m] = total[m * 128 : (m + 1) * 128].T


def sum_qkv(parts):
    return pl.pallas_call(
        sum_qkv_kernel,
        name="sum_qkv",
        grid=(2,),
        in_specs=[pl.BlockSpec((8, 1, 384, 256), lambda s: (0, s, 0, 0))],
        out_specs=pl.BlockSpec((3, 256, 128), lambda s: (0, s, 0)),
        out_shape=shape((3, 512, 128), F32),
        compiler_params=PARAMS,
    )(parts)


def sum_out_kernel(parts, out):
    total = parts[0].astype(F32)
    for k in range(1, 8):
        total = total + parts[k].astype(F32)
    out[:, 0:256] = total[0]
    out[:, 256:512] = total[1]


def sum_out(parts):
    return pl.pallas_call(
        sum_out_kernel,
        name="sum_out",
        out_shape=shape((128, 512), F32),
        compiler_params=PARAMS,
    )(parts)


def sublayer(layer_input, modality, image_spans, norm_gain, w_qkv, w_out, grad_out):
    x, h, c = (lax.axis_index(a) for a in GROUP)
    blocks = [((x - d) % 4, h ^ s, c ^ k) for k in range(2) for d in TURNS for s in range(2)]
    idx = jnp.stack([a * 4 + b * 2 + e for a, b, e in blocks]).astype(jnp.int32)
    places = jnp.stack([((x + d) % 4) * 2 + (h ^ s) for d in range(4) for s in range(2)]).astype(jnp.int32)

    gain_rows = jnp.concatenate(three_parts(norm_gain), axis=0).astype(BF16)
    gain_rows = jnp.concatenate([gain_rows, jnp.zeros((10, 256), BF16)], axis=0)
    xs = spread(jnp.concatenate([layer_input, gain_rows], axis=0))
    gs = spread(grad_out)

    w_t = exchange(pack_weights(w_qkv), TOKENS_AXES).reshape(16, 384, 256)
    wo_half = jnp.stack([w_out[:, 0:256], w_out[:, 256:512]])
    wo = exchange(copies(wo_half, 8), TOKENS_AXES).reshape(16, 128, 256)

    normed, inv = normalize(idx, xs, modality)
    q, kv, kv_copies = project(normed, w_t)
    all_kv = exchange(kv_copies, TOKENS_AXES).reshape(4096, 256)
    da, g_all = upstream(idx, gs, wo)
    w_pairs = w_t.reshape(8, 2, 384, 256)
    w_kept = lax.dynamic_index_in_dim(w_pairs, c, 1, keepdims=False)
    w_sent = lax.dynamic_index_in_dim(w_pairs, 1 - c, 1, keepdims=False)
    w_other = swap(w_sent, "c")

    pos = lax.axis_index(TOKENS_AXES) * 512 + jnp.arange(512, dtype=jnp.int32)
    inside = (pos[:, None] >= image_spans[0][None]) & (pos[:, None] < image_spans[1][None])
    ends = jnp.max(jnp.where(inside, image_spans[1][None], 0), axis=1)
    limit = jnp.maximum(pos + 1, ends)[None, :]

    out_rows = exchange(wo, GROUP)
    att, att_t, lse = forward(limit, q, all_kv)
    wo_parts = weight_grad(att_t, g_all).reshape(8, 2, 128, 256)
    wo_parts = exchange(wo_parts, TOKENS_AXES)
    dq, dkv = backward(limit, lse, q, all_kv, da, att_t)
    dkv_parts = exchange(dkv.reshape(8, 512, 256), TOKENS_AXES)

    atts = spread(att)
    attn_out = output(idx, atts, out_rows)
    grad_wout = sum_out(wo_parts)

    g, g_t, dots = collect(dkv_parts, dq, q, kv)
    g2, dots2 = swap(g, "c"), swap(dots, "c")
    w_parts = weight_grad(g_t, normed).reshape(8, 2, 384, 256)
    w_parts = exchange(w_parts, TOKENS_AXES)
    terms = input_grad(places, g, g2, w_kept, w_other, dots, dots2)
    terms = [turn(t, d) if d else t for d, t in enumerate(terms)]
    line = add_up(terms)
    last = swap(line, "h")
    grad_in, local_gain = finish(terms, last, layer_input, inv, modality, norm_gain)
    grad_qkv = sum_qkv(w_parts)
    grad_gain = jnp.sum(exchange(local_gain, TOKENS_AXES), axis=0)
    return (attn_out, grad_in, grad_qkv, grad_wout, grad_gain)


def solution(mesh):
    fine = Mesh(mesh.devices.reshape(4, 2, 2, 4, 2), ("x", "h", "c", "z", "u"))
    tok, feat = TOKENS_AXES, GROUP
    in_specs = (P(tok, feat), P(tok), P(), P(None, feat), P(None, tok, feat), P(feat, tok), P(tok, feat))
    out_specs = (P(tok, feat), P(tok, feat), P(None, tok, feat), P(feat, tok), P(None, feat))
    return jax.shard_map(sublayer, mesh=fine, in_specs=in_specs, out_specs=out_specs, check_vma=False)
```

profile of v0, /device:TPU:0, one launch (start us, length us, event | category | flops | bytes accessed | tf_op | source)
XLA Modules:
  0.0 384.7 jit_solution(14440421842329217773)
XLA Ops:
  3.4 8.2 %all-to-all-start = ((bf16[8,2,384,256]{3,2,1,0:T(8,128)(2,1)}), bf16[8,2,384,256]{3,2,1,0:T(8,128)(2,1)S(1)}, u32[]{:S(2)}, u32[]{:S(2)}) async-start(bf16[8,2,384,256]{3,2,1,0:T(8,128)(2,1)} %pack_weights.1), calls=%async_computation | async-start | bytes 6291456 | tf_op jit(solution)/shard_map/all_to_all | solution.py:40
  14.7 37.8 %collective-permute-done = bf16[528,256]{1,0:T(8,128)(2,1)S(1)} collective-permute-done((bf16[528,256]{1,0:T(8,128)(2,1)S(1)}, bf16[528,256]{1,0:T(8,128)(2,1)S(1)}, u32[]{:S(2)}, u32[]{:S(2)}) %collective-permute-start) | collective-permute-done | bytes 270368 | tf_op jit(solution)/shard_map/ppermute | solution.py:26
  53.4 3.0 collective-permute-start.3
  59.7 7.9 %all-to-all-start.2 = ((bf16[8,2,128,256]{3,2,1,0:T(8,128)(2,1)}), bf16[8,2,128,256]{3,2,1,0:T(8,128)(2,1)}, u32[]{:S(2)}, u32[]{:S(2)}) async-start(bf16[8,2,128,256]{3,2,1,0:T(8,128)(2,1)} %broadcast_in_dim.29), calls=%async_computation.2 | async-start | bytes 2097152 | tf_op jit(solution)/shard_map/all_to_all | solution.py:40
  70.4 9.7 %collective-permute-done.2.refs_2_.refs_10_ = bf16[2,528,256]{2,1,0:T(8,128)(2,1)} collective-permute-done((bf16[2,528,256]{2,1,0:T(8,128)(2,1)}, bf16[2,528,256]{2,1,0:T(8,128)(2,1)}, u32[]{:S(2)}, u32[]{:S(2)}) %collective-permute-start.2) | collective-permute-done | bytes 540704 | tf_op jit(solution)/shard_map/ppermute | solution.py:30
  83.1 6.2 %normalize.1 = (bf16[16,512,256]{2,1,0:T(8,128)(2,1)}, f32[512,1]{1,0:T(8,128)}) custom-call(s32[16]{0:T(128)} %stack.130.idx, bf16[2,528,256]{2,1,0:T(8,128)(2,1)} %pad_maximum_fusion.refs_0_.refs_8_, bf16[2,528,256]{2,1,0:T(8,128)(2,1)} %collective-permute-done.1.refs_1_.refs_9_, bf16[2,528,256]{2,1,0:T(8,128)(2,1)} %collective-permute-done.2.refs_2_.refs_10_, ...), custom_call_target="tpu_custom_call" | custom-call | tf_op jit(solution)/shard_map/normalize/pallas_call | solution.py:109
  89.3 6.3 %project.1 = (bf16[512,128]{1,0:T(8,128)(2,1)}, bf16[512,256]{1,0:T(8,128)(2,1)}, bf16[8,512,256]{2,1,0:T(8,128)(2,1)}) custom-call(bf16[16,512,256]{2,1,0:T(8,128)(2,1)} %get-tuple-element.26.normed.right, bf16[16,384,256]{2,1,0:T(8,128)(2,1)} %bitcast.50), custom_call_target="tpu_custom_call" | custom-call | tf_op jit(solution)/shard_map/project/pallas_call | solution.py:143
  95.6 7.8 %all-to-all-start.1 = ((bf16[8,512,256]{2,1,0:T(8,128)(2,1)}), bf16[8,512,256]{2,1,0:T(8,128)(2,1)S(1)}, u32[]{:S(2)}, u32[]{:S(2)}) async-start(bf16[8,512,256]{2,1,0:T(8,128)(2,1)} %get-tuple-element.28), calls=%async_computation.1 | async-start | bytes 4194304 | tf_op jit(solution)/shard_map/all_to_all | solution.py:40
  103.7 29.1 %collective-permute-done.16 = bf16[512,256]{1,0:T(8,128)(2,1)S(1)} collective-permute-done((bf16[512,256]{1,0:T(8,128)(2,1)S(1)}, bf16[512,256]{1,0:T(8,128)(2,1)S(1)}, u32[]{:S(2)}, u32[]{:S(2)}) %collective-permute-start.16) | collective-permute-done | bytes 262176 | tf_op jit(solution)/shard_map/ppermute | solution.py:26
  137.1 12.2 %collective-permute-done.19.refs_3_ = bf16[2,512,256]{2,1,0:T(8,128)(2,1)S(1)} collective-permute-done((bf16[2,512,256]{2,1,0:T(8,128)(2,1)S(1)}, bf16[2,512,256]{2,1,0:T(8,128)(2,1)S(1)}, u32[]{:S(2)}, u32[]{:S(2)}) %collective-permute-start.19) | collective-permute-done | bytes 524320 | tf_op jit(solution)/shard_map/ppermute | solution.py:30
  149.3 9.6 %collective-permute-done.18.refs_2_ = bf16[2,512,256]{2,1,0:T(8,128)(2,1)} collective-permute-done((bf16[2,512,256]{2,1,0:T(8,128)(2,1)S(1)}, bf16[2,512,256]{2,1,0:T(8,128)(2,1)}, u32[]{:S(2)}, u32[]{:S(2)}) %collective-permute-start.18) | collective-permute-done | bytes 524320 | tf_op jit(solution)/shard_map/ppermute | solution.py:30
  162.6 6.3 %upstream.1 = (bf16[512,128]{1,0:T(8,128)(2,1)}, bf16[16,512,256]{2,1,0:T(8,128)(2,1)}) custom-call(s32[16]{0:T(128)} %stack.130.idx, bf16[2,512,256]{2,1,0:T(8,128)(2,1)} %copy-done.9, bf16[2,512,256]{2,1,0:T(8,128)(2,1)} %collective-permute-done.17.refs_1_, bf16[2,512,256]{2,1,0:T(8,128)(2,1)} %collective-permute-done.18.refs_2_, ...), custom_call_target="tpu_custom_call" | custom-call | tf_op jit(solution)/shard_map/upstream/pallas_call | solution.py:170
  170.2 8.4 %forward.1 = (bf16[512,128]{1,0:T(8,128)(2,1)}, bf16[128,512]{1,0:T(8,128)(2,1)}, f32[1,512]{1,0:T(1,128)}) custom-call(s32[1,512]{1,0:T(1,128)} %add_maximum_fusion.limit, bf16[512,128]{1,0:T(8,128)(2,1)} %get-tuple-element.27.q, bf16[4096,256]{1,0:T(8,128)(2,1)} %bitcast.51), custom_call_target="tpu_custom_call" | custom-call | tf_op jit(solution)/shard_map/forward/pallas_call | solution.py:229
  178.6 10.1 %backward.1 = (bf16[512,128]{1,0:T(8,128)(2,1)}, bf16[4096,256]{1,0:T(8,128)(2,1)}) custom-call(s32[1,512]{1,0:T(1,128)} %add_maximum_fusion.limit, f32[1,512]{1,0:T(1,128)} %get-tuple-element.30.lse, bf16[512,128]{1,0:T(8,128)(2,1)} %get-tuple-element.27.q, bf16[4096,256]{1,0:T(8,128)(2,1)} %bitcast.52, bf16[512,128]{1,0:T(8,128)(2,1)} %get-tuple-element.31.da, ...), custom_call_target="tpu_custom_call" | custom-call | tf_op jit(solution)/shard_map/backward/pallas_call | solution.py:258
  188.7 7.9 %all-to-all-start.4 = ((bf16[8,512,256]{2,1,0:T(8,128)(2,1)}), bf16[8,512,256]{2,1,0:T(8,128)(2,1)}, u32[]{:S(2)}, u32[]{:S(2)}) async-start(bf16[8,512,256]{2,1,0:T(8,128)(2,1)} %bitcast.55), calls=%async_computation.4 | async-start | bytes 4194304 | tf_op jit(solution)/shard_map/all_to_all | solution.py:40
  198.5 27.0 %all-to-all-done.4.dkv = bf16[8,512,256]{2,1,0:T(8,128)(2,1)} async-done(((bf16[8,512,256]{2,1,0:T(8,128)(2,1)}), bf16[8,512,256]{2,1,0:T(8,128)(2,1)}, u32[]{:S(2)}, u32[]{:S(2)}) %all-to-all-start.4) | async-done | bytes 2097184 | tf_op jit(solution)/shard_map/all_to_all | solution.py:40
  225.5 4.1 %all-to-all-start.3 = ((bf16[16,128,256]{2,1,0:T(8,128)(2,1)}), bf16[16,128,256]{2,1,0:T(8,128)(2,1)S(1)}, u32[]{:S(2)}, u32[]{:S(2)}) async-start(bf16[16,128,256]{2,1,0:T(8,128)(2,1)} %bitcast.28.refs_8_), calls=%async_computation.3 | async-start | bytes 2097152 | tf_op jit(solution)/shard_map/all_to_all | solution.py:40
  229.6 3.1 collect.1
  233.1 3.5 weight_grad.3
  236.6 9.5 %all-to-all-done.3.refs_8_ = bf16[16,128,256]{2,1,0:T(8,128)(2,1)S(1)} async-done(((bf16[16,128,256]{2,1,0:T(8,128)(2,1)}), bf16[16,128,256]{2,1,0:T(8,128)(2,1)S(1)}, u32[]{:S(2)}, u32[]{:S(2)}) %all-to-all-start.3) | async-done | bytes 1048608 | tf_op jit(solution)/shard_map/all_to_all | solution.py:40
  247.1 3.6 all-to-all-start.6
  252.8 5.7 %input_grad.1 = (bf16[2,528,256]{2,1,0:T(8,128)(2,1)}, bf16[2,528,256]{2,1,0:T(8,128)(2,1)}, bf16[2,528,256]{2,1,0:T(8,128)(2,1)}, bf16[2,528,256]{2,1,0:T(8,128)(2,1)}) custom-call(s32[8]{0:T(128)} %stack.148.idx, bf16[512,384]{1,0:T(8,128)(2,1)} %get-tuple-element.36.g, bf16[512,384]{1,0:T(8,128)(2,1)} %copy-done.17, ...), custom_call_target="tpu_custom_call" | custom-call | tf_op jit(solution)/shard_map/input_grad/pallas_call | solution.py:320
  262.3 23.8 %collective-permute-done.27.refs_1_ = bf16[2,528,256]{2,1,0:T(8,128)(2,1)S(1)} collective-permute-done((bf16[2,528,256]{2,1,0:T(8,128)(2,1)}, bf16[2,528,256]{2,1,0:T(8,128)(2,1)S(1)}, u32[]{:S(2)}, u32[]{:S(2)}) %collective-permute-start.27) | collective-permute-done | bytes 540704 | tf_op jit(solution)/shard_map/ppermute | solution.py:30
  289.9 7.6 %collective-permute-done.30.refs_4_ = bf16[528,256]{1,0:T(8,128)(2,1)S(1)} collective-permute-done((bf16[528,256]{1,0:T(8,128)(2,1)}, bf16[528,256]{1,0:T(8,128)(2,1)S(1)}, u32[]{:S(2)}, u32[]{:S(2)}) %collective-permute-start.30) | collective-permute-done | bytes 270368 | tf_op jit(solution)/shard_map/ppermute | solution.py:26
  301.0 7.1 %all-to-all-start.7 = ((f32[8,2,256]{2,1,0:T(2,128)}), f32[8,2,256]{2,1,0:T(2,128)S(1)}, u32[]{:S(2)}, u32[]{:S(2)}) async-start(f32[8,2,256]{2,1,0:T(2,128)} %get-tuple-element.46), calls=%async_computation.7 | async-start | bytes 32768 | tf_op jit(solution)/shard_map/all_to_all | solution.py:40
  308.1 4.8 %weight_grad.2 = bf16[16,384,256]{2,1,0:T(8,128)(2,1)} custom-call(bf16[384,512]{1,0:T(8,128)(2,1)} %get-tuple-element.44.left, bf16[16,512,256]{2,1,0:T(8,128)(2,1)} %get-tuple-element.26.normed.right), custom_call_target="tpu_custom_call" | custom-call | tf_op jit(solution)/shard_map/weight_grad/pallas_call | solution.py:336
  315.8 4.5 %all-to-all-start.5 = ((bf16[8,2,384,256]{3,2,1,0:T(8,128)(2,1)}), bf16[8,2,384,256]{3,2,1,0:T(8,128)(2,1)S(1)}, u32[]{:S(2)}, u32[]{:S(2)}) async-start(bf16[8,2,384,256]{3,2,1,0:T(8,128)(2,1)} %bitcast.53), calls=%async_computation.5 | async-start | bytes 6291456 | tf_op jit(solution)/shard_map/all_to_all | solution.py:40
  320.6 35.1 %collective-permute-done.8 = bf16[512,128]{1,0:T(8,128)(2,1)S(1)} collective-permute-done((bf16[512,128]{1,0:T(8,128)(2,1)S(1)}, bf16[512,128]{1,0:T(8,128)(2,1)S(1)}, u32[]{:S(2)}, u32[]{:S(2)}) %collective-permute-start.8) | collective-permute-done | bytes 131104 | tf_op jit(solution)/shard_map/ppermute | solution.py:26
  357.7 3.7 collective-permute-start.10
  361.5 4.9 %collective-permute-done.11.refs_3_ = bf16[2,512,128]{2,1,0:T(8,128)(2,1)S(1)} collective-permute-done((bf16[2,512,128]{2,1,0:T(8,128)(2,1)S(1)}, bf16[2,512,128]{2,1,0:T(8,128)(2,1)S(1)}, u32[]{:S(2)}, u32[]{:S(2)}) %collective-permute-start.11) | collective-permute-done | bytes 262176 | tf_op jit(solution)/shard_map/ppermute | solution.py:30
  366.4 4.2 %collective-permute-done.10.refs_2_ = bf16[2,512,128]{2,1,0:T(8,128)(2,1)S(1)} collective-permute-done((bf16[2,512,128]{2,1,0:T(8,128)(2,1)S(1)}, bf16[2,512,128]{2,1,0:T(8,128)(2,1)S(1)}, u32[]{:S(2)}, u32[]{:S(2)}) %collective-permute-start.10) | collective-permute-done | bytes 262176 | tf_op jit(solution)/shard_map/ppermute | solution.py:30
  372.8 4.7 %output.1 = bf16[512,256]{1,0:T(8,128)(2,1)} custom-call(s32[16]{0:T(128)} %stack.130.idx, bf16[2,512,128]{2,1,0:T(8,128)(2,1)} %copy-done.11, bf16[2,512,128]{2,1,0:T(8,128)(2,1)} %copy-done.21, bf16[2,512,128]{2,1,0:T(8,128)(2,1)} %copy-done.20, bf16[2,512,128]{2,1,0:T(8,128)(2,1)} %copy-done.19, bf16[2,512,128]{2,1,0:T(8,128)(2,1)} %copy-done.22, ...), custom_call_target="tpu_custom_call" | custom-call | tf_op jit(solution)/shard_map/output/pallas_call | solution.py:413
  (145 shorter events, 56.5 us)
Async XLA Ops:
  3.4 55.1 %all-to-all-start = ((bf16[8,2,384,256]{3,2,1,0:T(8,128)(2,1)}), bf16[8,2,384,256]{3,2,1,0:T(8,128)(2,1)S(1)}, u32[]{:S(2)}, u32[]{:S(2)}) async-start(bf16[8,2,384,256]{3,2,1,0:T(8,128)(2,1)} %pack_weights.1), calls=%async_computation | async-start | bytes 6291456 | tf_op jit(solution)/shard_map/all_to_all | solution.py:40
  14.0 38.6 %collective-permute-start = (bf16[528,256]{1,0:T(8,128)(2,1)S(1)}, bf16[528,256]{1,0:T(8,128)(2,1)S(1)}, u32[]{:S(2)}, u32[]{:S(2)}) collective-permute-start(bf16[528,256]{1,0:T(8,128)(2,1)S(1)} %concatenate.6), channel_id=1, source_target_pairs={{0,16},{16,0},{1,17},{17,1},{2,18},{18,2},{3,19},{19,3},{4,20},{20... | collective-permute-start | bytes 811016 | tf_op jit(solution)/shard_map/ppermute | solution.py:26
  53.4 17.0 %collective-permute-start.3 = (bf16[2,528,256]{2,1,0:T(8,128)(2,1)}, bf16[2,528,256]{2,1,0:T(8,128)(2,1)}, u32[]{:S(2)}, u32[]{:S(2)}) collective-permute-start(bf16[2,528,256]{2,1,0:T(8,128)(2,1)} %pad_maximum_fusion.refs_0_.refs_8_), channel_id=1, source_target_pairs={{0,64},{32,96},{64,0},{96,32},{1,65},{33,97},{65,1},{97,33},{2,66}... | collective-permute-start | bytes 1622024 | tf_op jit(solution)/shard_map/ppermute | solution.py:30
  56.4 23.7 %collective-permute-start.2 = (bf16[2,528,256]{2,1,0:T(8,128)(2,1)}, bf16[2,528,256]{2,1,0:T(8,128)(2,1)}, u32[]{:S(2)}, u32[]{:S(2)}) collective-permute-start(bf16[2,528,256]{2,1,0:T(8,128)(2,1)} %pad_maximum_fusion.refs_0_.refs_8_), channel_id=1, source_target_pairs={{0,96},{32,0},{64,32},{96,64},{1,97},{33,1},{65,33},{97,65},{2,98}... | collective-permute-start | bytes 1622024 | tf_op jit(solution)/shard_map/ppermute | solution.py:30
  57.6 22.5 %collective-permute-start.1 = (bf16[2,528,256]{2,1,0:T(8,128)(2,1)}, bf16[2,528,256]{2,1,0:T(8,128)(2,1)}, u32[]{:S(2)}, u32[]{:S(2)}) collective-permute-start(bf16[2,528,256]{2,1,0:T(8,128)(2,1)} %pad_maximum_fusion.refs_0_.refs_8_), channel_id=1, source_target_pairs={{0,32},{32,64},{64,96},{96,0},{1,33},{33,65},{65,97},{97,1},{2,34}... | collective-permute-start | bytes 1622024 | tf_op jit(solution)/shard_map/ppermute | solution.py:30
  59.7 35.9 %all-to-all-start.2 = ((bf16[8,2,128,256]{3,2,1,0:T(8,128)(2,1)}), bf16[8,2,128,256]{3,2,1,0:T(8,128)(2,1)}, u32[]{:S(2)}, u32[]{:S(2)}) async-start(bf16[8,2,128,256]{3,2,1,0:T(8,128)(2,1)} %broadcast_in_dim.29), calls=%async_computation.2 | async-start | bytes 2097152 | tf_op jit(solution)/shard_map/all_to_all | solution.py:40
  67.6 14.5 %collective-permute-start.4 = (bf16[2,528,256]{2,1,0:T(8,128)(2,1)}, bf16[2,528,256]{2,1,0:T(8,128)(2,1)}, u32[]{:S(2)}, u32[]{:S(2)}) collective-permute-start(bf16[2,528,256]{2,1,0:T(8,128)(2,1)} %pad_maximum_fusion.refs_0_.refs_8_), channel_id=1, source_target_pairs={{0,8},{8,0},{1,9},{9,1},{2,10},{10,2},{3,11},{11,3},{4,12},{12,4},... | collective-permute-start | bytes 1622024 | tf_op jit(solution)/shard_map/ppermute | solution.py:26
  70.4 11.8 %collective-permute-start.7 = (bf16[2,528,256]{2,1,0:T(8,128)(2,1)}, bf16[2,528,256]{2,1,0:T(8,128)(2,1)}, u32[]{:S(2)}, u32[]{:S(2)}) collective-permute-start(bf16[2,528,256]{2,1,0:T(8,128)(2,1)} %collective-permute-done.3.refs_3_.refs_11_), channel_id=1, source_target_pairs={{0,8},{8,0},{1,9},{9,1},{2,10},{10,2},{3,11},{11,3},{4,12},{12,4},... | collective-permute-start | bytes 1622024 | tf_op jit(solution)/shard_map/ppermute | solution.py:26
  95.6 73.3 %all-to-all-start.1 = ((bf16[8,512,256]{2,1,0:T(8,128)(2,1)}), bf16[8,512,256]{2,1,0:T(8,128)(2,1)S(1)}, u32[]{:S(2)}, u32[]{:S(2)}) async-start(bf16[8,512,256]{2,1,0:T(8,128)(2,1)} %get-tuple-element.28), calls=%async_computation.1 | async-start | bytes 4194304 | tf_op jit(solution)/shard_map/all_to_all | solution.py:40
  103.4 29.3 %collective-permute-start.16 = (bf16[512,256]{1,0:T(8,128)(2,1)S(1)}, bf16[512,256]{1,0:T(8,128)(2,1)S(1)}, u32[]{:S(2)}, u32[]{:S(2)}) collective-permute-start(bf16[512,256]{1,0:T(8,128)(2,1)S(1)} %copy-done.25), channel_id=1, source_target_pairs={{0,16},{16,0},{1,17},{17,1},{2,18},{18,2},{3,19},{19,3},{4,20},{20... | collective-permute-start | bytes 786440 | tf_op jit(solution)/shard_map/ppermute | solution.py:26
  132.8 16.4 %collective-permute-start.19 = (bf16[2,512,256]{2,1,0:T(8,128)(2,1)S(1)}, bf16[2,512,256]{2,1,0:T(8,128)(2,1)S(1)}, u32[]{:S(2)}, u32[]{:S(2)}) collective-permute-start(bf16[2,512,256]{2,1,0:T(8,128)(2,1)S(1)} %pad_maximum_fusion.1.refs_0_), channel_id=1, source_target_pairs={{0,64},{32,96},{64,0},{96,32},{1,65},{33,97},{65,1},{97,33},{2,66}... | collective-permute-start | bytes 1572872 | tf_op jit(solution)/shard_map/ppermute | solution.py:30
  135.0 23.8 %collective-permute-start.18 = (bf16[2,512,256]{2,1,0:T(8,128)(2,1)S(1)}, bf16[2,512,256]{2,1,0:T(8,128)(2,1)}, u32[]{:S(2)}, u32[]{:S(2)}) collective-permute-start(bf16[2,512,256]{2,1,0:T(8,128)(2,1)S(1)} %pad_maximum_fusion.1.refs_0_), channel_id=1, source_target_pairs={{0,96},{32,0},{64,32},{96,64},{1,97},{33,1},{65,33},{97,65},{2,98}... | collective-permute-start | bytes 1572872 | tf_op jit(solution)/shard_map/ppermute | solution.py:30
  136.9 21.9 %collective-permute-start.17 = (bf16[2,512,256]{2,1,0:T(8,128)(2,1)S(1)}, bf16[2,512,256]{2,1,0:T(8,128)(2,1)}, u32[]{:S(2)}, u32[]{:S(2)}) collective-permute-start(bf16[2,512,256]{2,1,0:T(8,128)(2,1)S(1)} %pad_maximum_fusion.1.refs_0_), channel_id=1, source_target_pairs={{0,32},{32,64},{64,96},{96,0},{1,33},{33,65},{65,97},{97,1},{2,34}... | collective-permute-start | bytes 1572872 | tf_op jit(solution)/shard_map/ppermute | solution.py:30
  137.1 23.0 %collective-permute-start.20 = (bf16[2,512,256]{2,1,0:T(8,128)(2,1)S(1)}, bf16[2,512,256]{2,1,0:T(8,128)(2,1)S(1)}, u32[]{:S(2)}, u32[]{:S(2)}) collective-permute-start(bf16[2,512,256]{2,1,0:T(8,128)(2,1)S(1)} %pad_maximum_fusion.1.refs_0_), channel_id=1, source_target_pairs={{0,8},{8,0},{1,9},{9,1},{2,10},{10,2},{3,11},{11,3},{4,12},{12,4},... | collective-permute-start | bytes 1572872 | tf_op jit(solution)/shard_map/ppermute | solution.py:26
  149.3 10.8 %collective-permute-start.23 = (bf16[2,512,256]{2,1,0:T(8,128)(2,1)S(1)}, bf16[2,512,256]{2,1,0:T(8,128)(2,1)S(1)}, u32[]{:S(2)}, u32[]{:S(2)}) collective-permute-start(bf16[2,512,256]{2,1,0:T(8,128)(2,1)S(1)} %collective-permute-done.19.refs_3_), channel_id=1, source_target_pairs={{0,8},{8,0},{1,9},{9,1},{2,10},{10,2},{3,11},{11,3},{4,12},{12,4},... | collective-permute-start | bytes 1572872 | tf_op jit(solution)/shard_map/ppermute | solution.py:26
  188.7 36.8 %all-to-all-start.4 = ((bf16[8,512,256]{2,1,0:T(8,128)(2,1)}), bf16[8,512,256]{2,1,0:T(8,128)(2,1)}, u32[]{:S(2)}, u32[]{:S(2)}) async-start(bf16[8,512,256]{2,1,0:T(8,128)(2,1)} %bitcast.55), calls=%async_computation.4 | async-start | bytes 4194304 | tf_op jit(solution)/shard_map/all_to_all | solution.py:40
  198.5 53.0 %collective-permute-start.25 = (bf16[8,384,256]{2,1,0:T(8,128)(2,1)}, bf16[8,384,256]{2,1,0:T(8,128)(2,1)S(1)}, u32[]{:S(2)}, u32[]{:S(2)}) collective-permute-start(bf16[8,384,256]{2,1,0:T(8,128)(2,1)} %get-tuple-element.47), channel_id=1, source_target_pairs={{0,8},{8,0},{1,9},{9,1},{2,10},{10,2},{3,11},{11,3},{4,12},{12,4},... | collective-permute-start | bytes 4718600 | tf_op jit(solution)/shard_map/ppermute | solution.py:26
  225.5 20.6 %all-to-all-start.3 = ((bf16[16,128,256]{2,1,0:T(8,128)(2,1)}), bf16[16,128,256]{2,1,0:T(8,128)(2,1)S(1)}, u32[]{:S(2)}, u32[]{:S(2)}) async-start(bf16[16,128,256]{2,1,0:T(8,128)(2,1)} %bitcast.28.refs_8_), calls=%async_computation.3 | async-start | bytes 2097152 | tf_op jit(solution)/shard_map/all_to_all | solution.py:40
  232.7 19.3 %collective-permute-start.24 = (bf16[512,384]{1,0:T(8,128)(2,1)}, bf16[512,384]{1,0:T(8,128)(2,1)S(1)}, u32[]{:S(2)}, u32[]{:S(2)}) collective-permute-start(bf16[512,384]{1,0:T(8,128)(2,1)} %get-tuple-element.36.g), channel_id=1, source_target_pairs={{0,8},{8,0},{1,9},{9,1},{2,10},{10,2},{3,11},{11,3},{4,12},{12,4},... | collective-permute-start | bytes 1179656 | tf_op jit(solution)/shard_map/ppermute | solution.py:26
  247.1 53.9 %all-to-all-start.6 = ((bf16[8,2,128,256]{3,2,1,0:T(8,128)(2,1)}), bf16[8,2,128,256]{3,2,1,0:T(8,128)(2,1)S(1)}, u32[]{:S(2)}, u32[]{:S(2)}) async-start(bf16[8,2,128,256]{3,2,1,0:T(8,128)(2,1)} %bitcast.54), calls=%async_computation.6 | async-start | bytes 2097152 | tf_op jit(solution)/shard_map/all_to_all | solution.py:40
  258.5 27.6 %collective-permute-start.27 = (bf16[2,528,256]{2,1,0:T(8,128)(2,1)}, bf16[2,528,256]{2,1,0:T(8,128)(2,1)S(1)}, u32[]{:S(2)}, u32[]{:S(2)}) collective-permute-start(bf16[2,528,256]{2,1,0:T(8,128)(2,1)} %get-tuple-element.39), channel_id=1, source_target_pairs={{0,32},{32,64},{64,96},{96,0},{1,33},{33,65},{65,97},{97,1},{2,34}... | collective-permute-start | bytes 1622024 | tf_op jit(solution)/shard_map/ppermute | solution.py:30
  258.5 27.6 %collective-permute-start.28 = (bf16[2,528,256]{2,1,0:T(8,128)(2,1)}, bf16[2,528,256]{2,1,0:T(8,128)(2,1)S(1)}, u32[]{:S(2)}, u32[]{:S(2)}) collective-permute-start(bf16[2,528,256]{2,1,0:T(8,128)(2,1)} %get-tuple-element.40), channel_id=1, source_target_pairs={{0,64},{32,96},{64,0},{96,32},{1,65},{33,97},{65,1},{97,33},{2,66}... | collective-permute-start | bytes 1622024 | tf_op jit(solution)/shard_map/ppermute | solution.py:30
  260.9 25.8 %collective-permute-start.29 = (bf16[2,528,256]{2,1,0:T(8,128)(2,1)}, bf16[2,528,256]{2,1,0:T(8,128)(2,1)S(1)}, u32[]{:S(2)}, u32[]{:S(2)}) collective-permute-start(bf16[2,528,256]{2,1,0:T(8,128)(2,1)} %get-tuple-element.41), channel_id=1, source_target_pairs={{0,96},{32,0},{64,32},{96,64},{1,97},{33,1},{65,33},{97,65},{2,98}... | collective-permute-start | bytes 1622024 | tf_op jit(solution)/shard_map/ppermute | solution.py:30
  289.6 7.9 %collective-permute-start.30 = (bf16[528,256]{1,0:T(8,128)(2,1)}, bf16[528,256]{1,0:T(8,128)(2,1)S(1)}, u32[]{:S(2)}, u32[]{:S(2)}) collective-permute-start(bf16[528,256]{1,0:T(8,128)(2,1)} %add_up.1), channel_id=1, source_target_pairs={{0,16},{16,0},{1,17},{17,1},{2,18},{18,2},{3,19},{19,3},{4,20},{20... | collective-permute-start | bytes 811016 | tf_op jit(solution)/shard_map/ppermute | solution.py:26
  301.0 14.8 %all-to-all-start.7 = ((f32[8,2,256]{2,1,0:T(2,128)}), f32[8,2,256]{2,1,0:T(2,128)S(1)}, u32[]{:S(2)}, u32[]{:S(2)}) async-start(f32[8,2,256]{2,1,0:T(2,128)} %get-tuple-element.46), calls=%async_computation.7 | async-start | bytes 32768 | tf_op jit(solution)/shard_map/all_to_all | solution.py:40
  315.8 64.4 %all-to-all-start.5 = ((bf16[8,2,384,256]{3,2,1,0:T(8,128)(2,1)}), bf16[8,2,384,256]{3,2,1,0:T(8,128)(2,1)S(1)}, u32[]{:S(2)}, u32[]{:S(2)}) async-start(bf16[8,2,384,256]{3,2,1,0:T(8,128)(2,1)} %bitcast.53), calls=%async_computation.5 | async-start | bytes 6291456 | tf_op jit(solution)/shard_map/all_to_all | solution.py:40
  320.2 35.5 %collective-permute-start.8 = (bf16[512,128]{1,0:T(8,128)(2,1)S(1)}, bf16[512,128]{1,0:T(8,128)(2,1)S(1)}, u32[]{:S(2)}, u32[]{:S(2)}) collective-permute-start(bf16[512,128]{1,0:T(8,128)(2,1)S(1)} %copy-done.27), channel_id=1, source_target_pairs={{0,16},{16,0},{1,17},{17,1},{2,18},{18,2},{3,19},{19,3},{4,20},{20... | collective-permute-start | bytes 393224 | tf_op jit(solution)/shard_map/ppermute | solution.py:26
  355.8 10.6 %collective-permute-start.11 = (bf16[2,512,128]{2,1,0:T(8,128)(2,1)S(1)}, bf16[2,512,128]{2,1,0:T(8,128)(2,1)S(1)}, u32[]{:S(2)}, u32[]{:S(2)}) collective-permute-start(bf16[2,512,128]{2,1,0:T(8,128)(2,1)S(1)} %pad_maximum_fusion.2.refs_0_), channel_id=1, source_target_pairs={{0,64},{32,96},{64,0},{96,32},{1,65},{33,97},{65,1},{97,33},{2,66}... | collective-permute-start | bytes 786440 | tf_op jit(solution)/shard_map/ppermute | solution.py:30
  357.7 12.8 %collective-permute-start.10 = (bf16[2,512,128]{2,1,0:T(8,128)(2,1)S(1)}, bf16[2,512,128]{2,1,0:T(8,128)(2,1)S(1)}, u32[]{:S(2)}, u32[]{:S(2)}) collective-permute-start(bf16[2,512,128]{2,1,0:T(8,128)(2,1)S(1)} %pad_maximum_fusion.2.refs_0_), channel_id=1, source_target_pairs={{0,96},{32,0},{64,32},{96,64},{1,97},{33,1},{65,33},{97,65},{2,98}... | collective-permute-start | bytes 786440 | tf_op jit(solution)/shard_map/ppermute | solution.py:30
  361.4 9.1 %collective-permute-start.9 = (bf16[2,512,128]{2,1,0:T(8,128)(2,1)S(1)}, bf16[2,512,128]{2,1,0:T(8,128)(2,1)S(1)}, u32[]{:S(2)}, u32[]{:S(2)}) collective-permute-start(bf16[2,512,128]{2,1,0:T(8,128)(2,1)S(1)} %pad_maximum_fusion.2.refs_0_), channel_id=1, source_target_pairs={{0,32},{32,64},{64,96},{96,0},{1,33},{33,65},{65,97},{97,1},{2,34}... | collective-permute-start | bytes 786440 | tf_op jit(solution)/shard_map/ppermute | solution.py:30
  361.5 9.6 %collective-permute-start.12 = (bf16[2,512,128]{2,1,0:T(8,128)(2,1)S(1)}, bf16[2,512,128]{2,1,0:T(8,128)(2,1)S(1)}, u32[]{:S(2)}, u32[]{:S(2)}) collective-permute-start(bf16[2,512,128]{2,1,0:T(8,128)(2,1)S(1)} %pad_maximum_fusion.2.refs_0_), channel_id=1, source_target_pairs={{0,8},{8,0},{1,9},{9,1},{2,10},{10,2},{3,11},{11,3},{4,12},{12,4},... | collective-permute-start | bytes 786440 | tf_op jit(solution)/shard_map/ppermute | solution.py:26
  366.4 4.7 %collective-permute-start.15 = (bf16[2,512,128]{2,1,0:T(8,128)(2,1)S(1)}, bf16[2,512,128]{2,1,0:T(8,128)(2,1)S(1)}, u32[]{:S(2)}, u32[]{:S(2)}) collective-permute-start(bf16[2,512,128]{2,1,0:T(8,128)(2,1)S(1)} %collective-permute-done.11.refs_3_), channel_id=1, source_target_pairs={{0,8},{8,0},{1,9},{9,1},{2,10},{10,2},{3,11},{11,3},{4,12},{12,4},... | collective-permute-start | bytes 786440 | tf_op jit(solution)/shard_map/ppermute | solution.py:26
  (40 other events, 334.7 us)
where the time goes:
time: 387 us; the launch traced here: 385 us
  waiting for transfers between devices  219 us (57%)
  starting transfers between devices  73.4 us (19%)
  Pallas kernels  71.5 us (18%)
  local copies, waits for them, and re-layouts  16.6 us (4%)
    ppermute x19, waiting for transfers between devices, swap(): return lax.ppermute(a, axis, [(0, 1), (1, 0)])  112 us
    ppermute x12, waiting for transfers between devices, turn(): return lax.ppermute(a, 'x', [(i, (i + d) % 4) for i in range(4)])  67.8 us
    all_to_all x8, starting transfers between devices, exchange(): return lax.all_to_all(blocks, axis, 0, 0, tiled=True)  51 us
    all_to_all x8, waiting for transfers between devices, exchange(): return lax.all_to_all(blocks, axis, 0, 0, tiled=True)  39.4 us
    ppermute x12, starting transfers between devices, turn(): return lax.ppermute(a, 'x', [(i, (i + d) % 4) for i in range(4)])  18.8 us
    pallas_call x1, Pallas kernels, backward(): pl.pallas_call(backward_kernel, name='backward', out_shape=[shape((512, 1...  10.1 us
    unnamed x66, local copies, waits for them, and re-layouts  9.53 us
    pallas_call x1, Pallas kernels, forward(): pl.pallas_call(forward_kernel, name='forward', out_shape=[shape((512, 128...  8.39 us
  transfers between devices with their start and end apart: 39, of which 20 were waited for; matrix products, arithmetic and copies ran while one was open for 3% of the time, Pallas kernels for 12%

commit v1 on v0

v1 whole, which is shorter than its diff:
```python
import math

import jax
import jax.numpy as jnp
from jax import lax
from jax.experimental import pallas as pl
from jax.experimental.pallas import tpu as pltpu
from jax.sharding import Mesh
from jax.sharding import PartitionSpec as P


epsilon = 1e-05
masked_low = -1e30
GROUP = ("x", "h", "c")
TOKENS_AXES = ("z", "u")
F32 = jnp.float32
BF16 = jnp.bfloat16
TURNS = (0, 1, 3, 2)
NT = (((1,), (1,)), ((), ()))
TN = (((0,), (0,)), ((), ()))
SMEM = pl.BlockSpec(memory_space=pltpu.SMEM)
PARAMS = pltpu.CompilerParams(vmem_limit_bytes=60 * 1024 * 1024)


def swap(a, axis):
    return lax.ppermute(a, axis, [(0, 1), (1, 0)])


def turn(a, d, axis="x"):
    return lax.ppermute(a, axis, [(i, (i + d) % 4) for i in range(4)])


def turns(a, axis="x"):
    return [a] + [turn(a, d, axis) for d in TURNS[1:]]


def spread(block):
    row = turns(block) + turns(swap(block, "h"))
    return row + [swap(a, "c") for a in row]


def gather_tokens_axes(block):
    return turns(block, "z") + turns(swap(block, "u"), "z")


def exchange(blocks, axis):
    return lax.all_to_all(blocks, axis, 0, 0, tiled=True)


def three_parts(g):
    high = lax.reduce_precision(g, 8, 7)
    rest = g - high
    mid = lax.reduce_precision(rest, 8, 7)
    return high, mid, rest - mid


def dot(a, b, dims=(((1,), (0,)), ((), ()))):
    return lax.dot_general(a, b, dims, preferred_element_type=F32)


def shape(dims, kind=BF16):
    return jax.ShapeDtypeStruct(dims, kind)


def fixed(*dims):
    return pl.BlockSpec(dims, lambda *i: (0,) * len(dims))


def pack_kernel(w, wo, out):
    for s in range(2):
        for m in range(3):
            out[s, m * 128 : (m + 1) * 128, :] = w[m, s * 256 : (s + 1) * 256, :].T
        out[s, 384:512, :] = wo[:, s * 256 : (s + 1) * 256]


def pack_weights(w, wo):
    return pl.pallas_call(
        pack_kernel,
        name="pack_weights",
        out_shape=shape((2, 512, 256)),
        compiler_params=PARAMS,
    )(w, wo)


def normalize_kernel(idx, *refs):
    xs, gains = refs[:16], refs[16:32]
    mod, normed, inv_out = refs[32:]
    rows = mod.shape[0]
    squares = jnp.zeros((rows, 256), F32)
    for a in xs:
        xb = a[...].astype(F32)
        squares = squares + xb * xb
    inv = lax.rsqrt(jnp.sum(squares, axis=1, keepdims=True) / 4096 + epsilon)
    inv_out[...] = inv
    second = mod[...] == 1
    for n in range(16):
        g = gains[n][...].astype(F32)
        g0 = (g[0:1] + g[2:3]) + g[4:5]
        g1 = (g[1:2] + g[3:4]) + g[5:6]
        scaled = xs[n][...].astype(F32) * inv
        normed[idx[n]] = (scaled * jnp.where(second, g1, g0)).astype(BF16)


def normalize(idx, xs, modality):
    tile = 128
    rows = lambda cols: pl.BlockSpec((tile, cols), lambda i: (i, 0))
    return pl.pallas_call(
        normalize_kernel,
        name="normalize",
        grid=(512 // tile,),
        in_specs=[SMEM] + [rows(256)] * 16 + [pl.BlockSpec((16, 256), lambda i: (32, 0))] * 16 + [rows(1)],
        out_specs=[pl.BlockSpec((16, tile, 256), lambda i: (0, i, 0)), rows(1)],
        out_shape=[shape((16, 512, 256)), shape((512, 1), F32)],
        compiler_params=PARAMS,
    )(idx, *xs, *xs, modality[:, None])


def project_kernel(idx, normed, *refs):
    ws, (q, kv) = refs[:8], refs[8:]
    total = jnp.zeros((q.shape[0], 384), F32)
    for n in range(8):
        for s in range(2):
            total = total + dot(normed[idx[n] * 2 + s], ws[n][s], NT)
    both = total.astype(BF16)
    q[...] = both[:, 0:128]
    kv[...] = both[:, 128:384]


def project(idx, normed, ws):
    tile = 256
    rows = lambda cols: pl.BlockSpec((tile, cols), lambda i: (i, 0))
    return pl.pallas_call(
        project_kernel,
        name="project",
        grid=(512 // tile,),
        in_specs=[SMEM, pl.BlockSpec((16, tile, 256), lambda i: (0, i, 0))] + [fixed(2, 384, 256)] * 8,
        out_specs=[rows(128), rows(256)],
        out_shape=[shape((512, 128)), shape((512, 256))],
        compiler_params=PARAMS,
    )(idx, normed, *ws)


def order_kernel(idx, core, *refs):
    ws, (kept, sent, wo) = refs[:8], refs[8:]
    for n in range(8):
        k = idx[n]
        kept[k] = ws[n][core[0], 0:384, :]
        sent[k] = ws[n][1 - core[0], 0:384, :]
        for s in range(2):
            wo[k * 2 + s] = ws[n][s, 384:512, :]


def order_weights(idx, core, ws):
    vmem = pl.BlockSpec(memory_space=pltpu.VMEM)
    return pl.pallas_call(
        order_kernel,
        name="order_weights",
        in_specs=[SMEM, SMEM] + [vmem] * 8,
        out_shape=[shape((8, 384, 256)), shape((8, 384, 256)), shape((16, 128, 256))],
        compiler_params=PARAMS,
    )(idx, core, *ws)


def upstream_kernel(idx, *refs):
    gs, (w, out, ordered) = refs[:16], refs[16:]
    acc = jnp.zeros(out.shape, F32)
    for n in range(16):
        g = gs[n][...]
        ordered[idx[n]] = g
        acc = acc + dot(g, w[idx[n]], NT)
    out[...] = acc.astype(BF16)


def upstream(idx, gs, wo):
    tile = 128
    return pl.pallas_call(
        upstream_kernel,
        name="upstream",
        grid=(512 // tile,),
        in_specs=[SMEM]
        + [pl.BlockSpec((tile, 256), lambda i: (i, 0))] * 16
        + [fixed(16, 128, 256)],
        out_specs=[
            pl.BlockSpec((tile, 128), lambda i: (i, 0)),
            pl.BlockSpec((16, tile, 256), lambda i: (0, i, 0)),
        ],
        out_shape=[shape((512, 128)), shape((16, 512, 256))],
        compiler_params=PARAMS,
    )(idx, *gs, wo)


KEY_BLOCK = 512
SCALE = 1.0 / math.sqrt(128)
TO_BASE2 = SCALE * math.log2(math.e)


def masked_scores(b, kv, q, edge):
    s = dot(kv[pl.ds(b * KEY_BLOCK, KEY_BLOCK), 0:128], q[...], NT) * TO_BASE2
    pos = lax.broadcasted_iota(jnp.int32, s.shape, 0) + b * KEY_BLOCK
    return jnp.where(pos < edge, s, masked_low)


def forward_kernel(idx, limit, q, *refs):
    parts, (att, att_t, lse, kv, s_all) = refs[:8], refs[8:]
    for n in range(8):
        kv[pl.ds(idx[n] * 512, 512), :] = parts[n][...]
    count = kv.shape[0] // KEY_BLOCK
    cols = q.shape[0]
    edge = limit[...]

    def scores(b, top):
        s = masked_scores(b, kv, q, edge)
        s_all[pl.ds(b * KEY_BLOCK, KEY_BLOCK), :] = s
        return jnp.maximum(top, jnp.max(s, axis=0, keepdims=True))

    top = lax.fori_loop(0, count, scores, jnp.full((1, cols), masked_low, F32))

    def sums(b, total):
        at = pl.ds(b * KEY_BLOCK, KEY_BLOCK)
        e = jnp.exp2(s_all[at, :] - top)
        s_all[at, :] = e
        return total + jnp.sum(e, axis=0, keepdims=True)

    total = lax.fori_loop(0, count, sums, jnp.zeros((1, cols), F32))
    inv = 1.0 / total
    lse[...] = top + jnp.log2(total)

    def attend(b, acc):
        at = pl.ds(b * KEY_BLOCK, KEY_BLOCK)
        return acc + dot(kv[at, 128:256], (s_all[at, :] * inv).astype(BF16), TN)

    out_t = lax.fori_loop(0, count, attend, jnp.zeros((128, cols), F32)).astype(BF16)
    att_t[...] = out_t
    att[...] = out_t.T


def forward(idx, limit, q, parts):
    vmem = pl.BlockSpec(memory_space=pltpu.VMEM)
    return pl.pallas_call(
        forward_kernel,
        name="forward",
        in_specs=[SMEM] + [vmem] * 10,
        out_shape=[shape((512, 128)), shape((128, 512)), shape((1, 512), F32), shape((4096, 256))],
        scratch_shapes=[pltpu.VMEM((4096, 512), F32)],
        compiler_params=PARAMS,
    )(idx, limit, q, *parts)


def backward_kernel(limit, lse, q, kv, da, att_t, dq, dkv):
    count = kv.shape[0] // KEY_BLOCK
    edge = limit[...]
    da_t = da[...].T
    row_dots = jnp.sum(att_t[...].astype(F32) * da_t.astype(F32), axis=0, keepdims=True)

    def back(b, acc):
        at = pl.ds(b * KEY_BLOCK, KEY_BLOCK)
        p = jnp.exp2(masked_scores(b, kv, q, edge) - lse[...])
        d_probs = dot(kv[at, 128:256], da[...], NT)
        ds = (p * (d_probs - row_dots) * SCALE).astype(BF16)
        dkv[at, 0:128] = dot(ds, q[...]).astype(BF16)
        dkv[at, 128:256] = dot(p.astype(BF16), da[...]).astype(BF16)
        return acc + dot(kv[at, 0:128], ds, TN)

    dq_t = lax.fori_loop(0, count, back, jnp.zeros((128, q.shape[0]), F32))
    dq[...] = dq_t.astype(BF16).T


def backward(limit, lse, q, kv, da, att_t):
    return pl.pallas_call(
        backward_kernel,
        name="backward",
        out_shape=[shape((512, 128)), shape((4096, 256))],
        compiler_params=PARAMS,
    )(limit, lse, q, kv, da, att_t)


def split_rows(dots):
    rows = []
    for p in (dots[:, 0:256], dots[:, 256:512]):
        high = p.astype(BF16).astype(F32)
        mid = (p - high).astype(BF16).astype(F32)
        rows.append((high, mid, p - high - mid))
    kind = lax.broadcasted_iota(jnp.int32, (16, 256), 0)
    both = jnp.zeros((16, 256), F32)
    for r in range(6):
        both = jnp.where(kind == r, rows[r % 2][r // 2], both)
    return both.astype(BF16)


def joined_rows(block):
    t = block.astype(F32)
    return (t[0:2] + t[2:4]) + t[4:6]


def gradients_kernel(dkv, dq, q, kv, normed, dwo, g_out, dots, out, g_t):
    step = pl.program_id(0)

    @pl.when(step == 0)
    def _():
        total = dkv[0].astype(F32)
        for k in range(1, 8):
            total = total + dkv[k].astype(F32)
        g = jnp.concatenate([dq[...], total.astype(BF16)], axis=1)
        g_out[...] = g
        g_t[...] = g.T
        gf = g.astype(F32)
        prod = gf[:, 0:128] * q[...].astype(F32)
        prod = prod + gf[:, 128:256] * kv[:, 0:128].astype(F32)
        prod = prod + gf[:, 256:384] * kv[:, 128:256].astype(F32)
        ones = jnp.ones((8, 128), F32)
        dots[...] = lax.dot_general(
            ones, prod, NT, precision=lax.Precision.HIGHEST, preferred_element_type=F32
        )

    @pl.when(step > 0)
    def _():
        for k in range(8):
            out[k, 0:384, :] = dot(g_t[...], normed[k]).astype(BF16)
            out[k, 384:512, :] = dwo[k]


def gradients(dkv, dq, q, kv, normed, dwo):
    later = lambda i: (jnp.maximum(i - 1, 0), 0, 0)
    return pl.pallas_call(
        gradients_kernel,
        name="gradients",
        grid=(3,),
        in_specs=[
            fixed(8, 512, 256),
            fixed(512, 128),
            fixed(512, 128),
            fixed(512, 256),
            pl.BlockSpec((8, 512, 256), later),
            pl.BlockSpec((8, 128, 256), later),
        ],
        out_specs=[fixed(512, 384), fixed(8, 512), pl.BlockSpec((8, 512, 256), later)],
        out_shape=[shape((512, 384)), shape((8, 512), F32), shape((16, 512, 256))],
        scratch_shapes=[pltpu.VMEM((384, 512), BF16)],
        compiler_params=PARAMS,
    )(dkv, dq, q, kv, normed, dwo)


def input_grad_kernel(idx, g, g2, w, w2, dots, dots2, *outs):
    rows = split_rows(dots[0:1] + dots2[0:1])
    for n in range(8):
        out, at = outs[n // 2], idx[n]
        both = dot(g[...], w[at]) + dot(g2[...], w2[at])
        out[n % 2, 0:512, :] = both.astype(BF16)
        out[n % 2, 512:528, :] = rows


def input_grad(idx, g, g2, w, w2, dots, dots2):
    vmem = pl.BlockSpec(memory_space=pltpu.VMEM)
    return pl.pallas_call(
        input_grad_kernel,
        name="input_grad",
        in_specs=[SMEM] + [vmem] * 6,
        out_shape=[shape((2, 528, 256))] * 4,
        compiler_params=PARAMS,
    )(idx, g, g2, w, w2, dots, dots2)


def weight_grad_kernel(left, right, out):
    for k in range(right.shape[0]):
        out[k] = dot(left[...], right[k]).astype(BF16)


def weight_grad(left, right):
    rows = left.shape[0]
    return pl.pallas_call(
        weight_grad_kernel,
        name="weight_grad",
        grid=(2,),
        in_specs=[fixed(rows, 512), pl.BlockSpec((8, 512, 256), lambda j: (j, 0, 0))],
        out_specs=pl.BlockSpec((8, rows, 256), lambda j: (j, 0, 0)),
        out_shape=shape((16, rows, 256)),
        compiler_params=PARAMS,
    )(left, right)


def line_kernel(side, *refs):
    terms, (x, x_next, inv, mod, own, own_dots, sent, gains) = refs[:4], refs[4:]
    second = mod[...] == 1
    for slot, block in ((0, x), (1, x_next)):
        total = terms[0][slot, 0:512].astype(F32)
        dots = joined_rows(terms[0][slot, 512:528])
        for t in terms[1:]:
            total = total + t[slot, 0:512].astype(F32)
            dots = dots + joined_rows(t[slot, 512:528])
        if slot == 0:
            own[...] = total
            own_dots[0:2] = dots
        else:
            sent[0:512] = total.astype(BF16)
            sent[512:528] = split_rows(jnp.concatenate([dots[0:1], dots[1:2]], axis=1))
        each = total * (block[...].astype(F32) * inv[...])
        first = jnp.sum(jnp.where(second, 0.0, each), axis=0, keepdims=True)
        other = jnp.sum(jnp.where(second, each, 0.0), axis=0, keepdims=True)
        at = side[0] if slot == 0 else 1 - side[0]
        for k in range(8):
            gains[k, at, 0:1] = first
            gains[k, at, 1:2] = other


def line_sum(side, terms, x, x_next, inv, modality):
    return pl.pallas_call(
        line_kernel,
        name="line_sum",
        grid=(1,),
        in_specs=[SMEM]
        + [fixed(2, 528, 256)] * 4
        + [fixed(512, 256), fixed(512, 256), fixed(512, 1), fixed(512, 1)],
        out_specs=[fixed(512, 256), fixed(8, 256), fixed(528, 256), fixed(8, 2, 2, 256)],
        out_shape=[
            shape((512, 256), F32),
            shape((8, 256), F32),
            shape((528, 256)),
            shape((8, 2, 2, 256), F32),
        ],
        compiler_params=PARAMS,
    )(side, *terms, x, x_next, inv, modality[:, None])


def finish_kernel(own, own_dots, last, x, inv, mod, gain, grad_in):
    gn = own[...] + last[0:512].astype(F32)
    dots = own_dots[0:2] + joined_rows(last[512:528])
    columns = [jnp.broadcast_to(dots[r : r + 1], (128, 256)).T[:, 0:1] for r in range(2)]
    mean = jnp.concatenate(columns, axis=0) / 4096
    scaled = x[...].astype(F32) * inv[...]
    up = gn * jnp.where(mod[...] == 1, gain[1:2], gain[0:1])
    grad_in[...] = (inv[...] * (up - scaled * mean)).astype(BF16)


def finish(own, own_dots, last, x, inv, modality, gain):
    return pl.pallas_call(
        finish_kernel,
        name="finish",
        out_shape=shape((512, 256)),
        compiler_params=PARAMS,
    )(own, own_dots, last, x, inv, modality[:, None], gain)


def output_kernel(idx, *refs):
    atts, (rows, out) = refs[:16], refs[16:]
    total = jnp.zeros(out.shape, F32)
    for n in range(16):
        total = total + dot(atts[n][...], rows[idx[n]]).astype(BF16).astype(F32)
    out[...] = total.astype(BF16)


def output(idx, atts, rows):
    tile = 128
    return pl.pallas_call(
        output_kernel,
        name="output",
        grid=(512 // tile,),
        in_specs=[SMEM]
        + [pl.BlockSpec((tile, 128), lambda i: (i, 0))] * 16
        + [fixed(16, 128, 256)],
        out_specs=pl.BlockSpec((tile, 256), lambda i: (i, 0)),
        out_shape=shape((512, 256)),
        compiler_params=PARAMS,
    )(idx, *atts, rows)


def sum_weights_kernel(parts, qkv, wout):
    total = parts[0, 0].astype(F32)
    for k in range(1, 8):
        total = total + parts[k, 0].astype(F32)
    for m in range(3):
        qkv[m] = total[m * 128 : (m + 1) * 128].T
    wout[...] = total[384:512]


def sum_weights(parts):
    return pl.pallas_call(
        sum_weights_kernel,
        name="sum_weights",
        grid=(2,),
        in_specs=[pl.BlockSpec((8, 1, 512, 256), lambda s: (0, s, 0, 0))],
        out_specs=[
            pl.BlockSpec((3, 256, 128), lambda s: (0, s, 0)),
            pl.BlockSpec((128, 256), lambda s: (0, s)),
        ],
        out_shape=[shape((3, 512, 128), F32), shape((128, 512), F32)],
        compiler_params=PARAMS,
    )(parts)


def sublayer(layer_input, modality, image_spans, norm_gain, w_qkv, w_out, grad_out):
    x, h, c = (lax.axis_index(a) for a in GROUP)
    z, u = (lax.axis_index(a) for a in TOKENS_AXES)
    blocks = [((x - d) % 4, h ^ s, c ^ k) for k in range(2) for s in range(2) for d in TURNS]
    idx = jnp.stack([a * 4 + b * 2 + e for a, b, e in blocks]).astype(jnp.int32)
    tok_idx = jnp.stack([((z - d) % 4) * 2 + (u ^ s) for s in range(2) for d in TURNS]).astype(jnp.int32)
    places = jnp.stack([((x + d) % 4) * 2 + (h ^ s) for d in range(4) for s in range(2)]).astype(jnp.int32)
    core = c.astype(jnp.int32)[None]
    side = h.astype(jnp.int32)[None]

    gain_rows = jnp.concatenate(three_parts(norm_gain), axis=0).astype(BF16)
    gain_rows = jnp.concatenate([gain_rows, jnp.zeros((10, 256), BF16)], axis=0)
    xs = spread(jnp.concatenate([layer_input, gain_rows], axis=0))
    ws = gather_tokens_axes(pack_weights(w_qkv, w_out))
    gs = spread(grad_out)

    normed, inv = normalize(idx, xs, modality)
    q, kv = project(tok_idx, normed, ws)
    kvs = gather_tokens_axes(kv)
    w_kept, w_sent, wo = order_weights(tok_idx, core, ws)
    w_other = swap(w_sent, "c")
    da, g_all = upstream(idx, gs, wo)

    pos = (z * 2 + u) * 512 + jnp.arange(512, dtype=jnp.int32)
    inside = (pos[:, None] >= image_spans[0][None]) & (pos[:, None] < image_spans[1][None])
    ends = jnp.max(jnp.where(inside, image_spans[1][None], 0), axis=1)
    limit = jnp.maximum(pos + 1, ends)[None, :]

    out_rows = exchange(wo, GROUP)
    att, att_t, lse, all_kv = forward(tok_idx, limit, q, kvs)
    dq, dkv = backward(limit, lse, q, all_kv, da, att_t)
    dkv_parts = exchange(dkv.reshape(8, 512, 256), TOKENS_AXES)

    dwo = weight_grad(att_t, g_all)
    atts = spread(att)
    attn_out = output(idx, atts, out_rows)

    g, dots, w_parts = gradients(dkv_parts, dq, q, kv, normed, dwo)
    w_parts = exchange(w_parts.reshape(8, 2, 512, 256), TOKENS_AXES)
    g2, dots2 = swap(g, "c"), swap(dots, "c")
    terms = input_grad(places, g, g2, w_kept, w_other, dots, dots2)
    terms = [turn(t, d) if d else t for d, t in enumerate(terms)]
    own, own_dots, sent, gains = line_sum(side, terms, layer_input, xs[4], inv, modality)
    last = swap(sent, "h")
    gains = exchange(gains.reshape(16, 2, 256), ("z", "u", "h"))
    grad_in = finish(own, own_dots, last, layer_input, inv, modality, norm_gain)
    grad_qkv, grad_wout = sum_weights(w_parts)
    grad_gain = jnp.sum(gains, axis=0)
    return (attn_out, grad_in, grad_qkv, grad_wout, grad_gain)


def solution(mesh):
    fine = Mesh(mesh.devices.reshape(4, 2, 2, 4, 2), ("x", "h", "c", "z", "u"))
    tok, feat = TOKENS_AXES, GROUP
    in_specs = (P(tok, feat), P(tok), P(), P(None, feat), P(None, tok, feat), P(feat, tok), P(tok, feat))
    out_specs = (P(tok, feat), P(tok, feat), P(None, tok, feat), P(feat, tok), P(None, feat))
    return jax.shard_map(sublayer, mesh=fine, in_specs=in_specs, out_specs=out_specs, check_vma=False)
```

time: 387 us -> 340 us (0.88)
  waiting for transfers between devices: 219 us -> 147 us
  starting transfers between devices: 73.4 us -> 91.9 us
  blocking collectives: 0 us -> 11 us
  local copies, waits for them, and re-layouts: 16.6 us -> 9.64 us
    ppermute x19 -> x33, waiting for transfers between devices: 112 us -> 50.2 us  [swap(): return lax.ppermute(a, axis, [(0, 1), (1, 0)])]
    ppermute x12 -> x33, starting transfers between devices: 18.8 us -> 57.9 us  [turn(): return lax.ppermute(a, axis, [(i, (i + d) % 4) for i in range(4)])]
    all_to_all x8 -> x3, starting transfers between devices: 51 us -> 17.2 us  [exchange(): return lax.all_to_all(blocks, axis, 0, 0, tiled=True)]
    ppermute x19 -> x33, starting transfers between devices: 3.68 us -> 16.8 us  [swap(): return lax.ppermute(a, axis, [(0, 1), (1, 0)])]
    all_to_all x8 -> x3, waiting for transfers between devices: 39.4 us -> 26.8 us  [exchange(): return lax.all_to_all(blocks, axis, 0, 0, tiled=True)]
    all_to_all x0 -> x1, blocking collectives: none -> 11 us  [exchange(): return lax.all_to_all(blocks, axis, 0, 0, tiled=True)]
    pallas_call x8, Pallas kernels: 30.2 us -> 37.5 us  [the longest x1 8.89 us: forward(): pl.pallas_call(forward_kernel, name='forward', in_specs=[SMEM] + [vmem] *...]
    pallas_call x2 -> x1, Pallas kernels: 8.33 us -> 3.54 us  [weight_grad(): pl.pallas_call(weight_grad_kernel, name='weight_grad', grid=(2,), in_spec...]
  transfers between devices with their start and end apart: 39 -> 69, of which waited for: 20 -> 25; matrix products, arithmetic and copies ran while one was open for 3% -> 2% of each run, Pallas kernels for 12% -> 15%
where the time goes in v1:
time: 340 us; the launch traced here: 337 us
  waiting for transfers between devices  147 us (43%)
  starting transfers between devices  91.9 us (27%)
  Pallas kernels  74 us (22%)
  blocking collectives  11 us (3%)
  local copies, waits for them, and re-layouts  9.64 us (3%)
    ppermute x33, waiting for transfers between devices, turn(): return lax.ppermute(a, axis, [(i, (i + d) % 4) for i in range(4)])  70.5 us
    ppermute x33, starting transfers between devices, turn(): return lax.ppermute(a, axis, [(i, (i + d) % 4) for i in range(4)])  57.9 us
    ppermute x33, waiting for transfers between devices, swap(): return lax.ppermute(a, axis, [(0, 1), (1, 0)])  50.2 us
    all_to_all x3, waiting for transfers between devices, exchange(): return lax.all_to_all(blocks, axis, 0, 0, tiled=True)  26.8 us
    all_to_all x3, starting transfers between devices, exchange(): return lax.all_to_all(blocks, axis, 0, 0, tiled=True)  17.2 us
    ppermute x33, starting transfers between devices, swap(): return lax.ppermute(a, axis, [(0, 1), (1, 0)])  16.8 us
    all_to_all x1, blocking collectives, exchange(): return lax.all_to_all(blocks, axis, 0, 0, tiled=True)  11 us
    pallas_call x1, Pallas kernels, backward(): pl.pallas_call(backward_kernel, name='backward', out_shape=[shape((512, 1...  10.1 us
  transfers between devices with their start and end apart: 69, of which 25 were waited for; matrix products, arithmetic and copies ran while one was open for 2% of the time, Pallas kernels for 15%

profile of v1, /device:TPU:0, one launch (start us, length us, event | category | flops | bytes accessed | tf_op | source)
XLA Modules:
  0.0 337.2 jit_solution(15827579047995339410)
XLA Ops:
  11.7 7.1 %collective-permute-start.1 = (bf16[528,256]{1,0:T(8,128)(2,1)S(1)}, bf16[528,256]{1,0:T(8,128)(2,1)S(1)}, u32[]{:S(2)}, u32[]{:S(2)}) collective-permute-start(bf16[528,256]{1,0:T(8,128)(2,1)S(1)} %concatenate.6.refs_0_.refs_16_), channel_id=1, source_target_pairs={{0,96},{32,0},{64,32},{96,64},{1,97},{33,1},{65,33},{97,65},{2,98}... | collective-permute-start | bytes 811016 | tf_op jit(solution)/shard_map/ppermute | solution.py:30
  28.6 3.4 collective-permute-start.17
  32.0 3.3 collective-permute-start.18
  39.8 10.0 %collective-permute-done.16.refs_2_ = bf16[2,512,256]{2,1,0:T(8,128)(2,1)S(1)} collective-permute-done((bf16[2,512,256]{2,1,0:T(8,128)(2,1)}, bf16[2,512,256]{2,1,0:T(8,128)(2,1)S(1)}, u32[]{:S(2)}, u32[]{:S(2)}) %collective-permute-start.16) | collective-permute-done | bytes 524320 | tf_op jit(solution)/shard_map/ppermute | solution.py:30
  54.1 4.9 %collective-permute-done.49.refs_6_ = bf16[512,256]{1,0:T(8,128)(2,1)S(1)} collective-permute-done((bf16[512,256]{1,0:T(8,128)(2,1)S(1)}, bf16[512,256]{1,0:T(8,128)(2,1)S(1)}, u32[]{:S(2)}, u32[]{:S(2)}) %collective-permute-start.49) | collective-permute-done | bytes 262176 | tf_op jit(solution)/shard_map/ppermute | solution.py:30
  59.6 4.2 %collective-permute-done.5.refs_6_.refs_22_ = bf16[528,256]{1,0:T(8,128)(2,1)S(1)} collective-permute-done((bf16[528,256]{1,0:T(8,128)(2,1)S(1)}, bf16[528,256]{1,0:T(8,128)(2,1)S(1)}, u32[]{:S(2)}, u32[]{:S(2)}) %collective-permute-start.5) | collective-permute-done | bytes 270368 | tf_op jit(solution)/shard_map/ppermute | solution.py:30
  72.9 17.7 %collective-permute-done.19.refs_5_ = bf16[2,512,256]{2,1,0:T(8,128)(2,1)S(1)} collective-permute-done((bf16[2,512,256]{2,1,0:T(8,128)(2,1)S(1)}, bf16[2,512,256]{2,1,0:T(8,128)(2,1)S(1)}, u32[]{:S(2)}, u32[]{:S(2)}) %collective-permute-start.19) | collective-permute-done | bytes 524320 | tf_op jit(solution)/shard_map/ppermute | solution.py:30
  95.1 6.2 %normalize.1 = (bf16[16,512,256]{2,1,0:T(8,128)(2,1)}, f32[512,1]{1,0:T(8,128)}) custom-call(s32[16]{0:T(128)} %stack.121.idx, bf16[528,256]{1,0:T(8,128)(2,1)} %copy-done.2, bf16[528,256]{1,0:T(8,128)(2,1)} %copy-done.11, bf16[528,256]{1,0:T(8,128)(2,1)} %copy-done.12, bf16[528,256]{1,0:T(8,128)(2,1)} %collective-permute-done.2.refs_3_.refs_19_, ...), custom_call_target="tpu_custom_call" | custom-call | tf_op jit(solution)/shard_map/normalize/pallas_call | solution.py:107
  101.4 5.8 %project.1 = (bf16[512,128]{1,0:T(8,128)(2,1)}, bf16[512,256]{1,0:T(8,128)(2,1)}) custom-call(s32[8]{0:T(128)} %stack.130.idx, bf16[16,512,256]{2,1,0:T(8,128)(2,1)} %get-tuple-element.33.normed, bf16[2,512,256]{2,1,0:T(8,128)(2,1)} %pack_weights.1.refs_0_, bf16[2,512,256]{2,1,0:T(8,128)(2,1)} %copy-done.4, bf16[2,512,256]{2,1,0:T(8,128)(2,1)} %copy-done.5, ...), custom_call_target="tpu_custom_call" | custom-call | tf_op jit(solution)/shard_map/project/pallas_call | solution.py:132
  110.7 3.2 collective-permute-start.23
  114.9 3.5 %collective-permute-done.25.refs_4_ = bf16[512,256]{1,0:T(8,128)(2,1)S(1)} collective-permute-done((bf16[512,256]{1,0:T(8,128)(2,1)}, bf16[512,256]{1,0:T(8,128)(2,1)S(1)}, u32[]{:S(2)}, u32[]{:S(2)}) %collective-permute-start.25) | collective-permute-done | bytes 262176 | tf_op jit(solution)/shard_map/ppermute | solution.py:26
  118.5 3.2 collective-permute-start.27
  121.7 2.8 collective-permute-start.28
  125.2 4.5 %order_weights.1 = (bf16[8,384,256]{2,1,0:T(8,128)(2,1)}, bf16[8,384,256]{2,1,0:T(8,128)(2,1)}, bf16[16,128,256]{2,1,0:T(8,128)(2,1)}) custom-call(s32[8]{0:T(128)} %stack.130.idx, s32[1]{0:T(128)} %bitcast.28.core, bf16[2,512,256]{2,1,0:T(8,128)(2,1)} %pack_weights.1.refs_0_, bf16[2,512,256]{2,1,0:T(8,128)(2,1)} %copy-done.4, ...), custom_call_target="tpu_custom_call" | custom-call | tf_op jit(solution)/shard_map/order_weights/pallas_call | solution.py:155
  129.7 6.3 %upstream.1 = (bf16[512,128]{1,0:T(8,128)(2,1)}, bf16[16,512,256]{2,1,0:T(8,128)(2,1)}) custom-call(s32[16]{0:T(128)} %stack.121.idx, bf16[512,256]{1,0:T(8,128)(2,1)} %refs_0_.1, bf16[512,256]{1,0:T(8,128)(2,1)} %copy-done.33, bf16[512,256]{1,0:T(8,128)(2,1)} %copy-done.34, bf16[512,256]{1,0:T(8,128)(2,1)} %copy-done.35, bf16[512,256]{1,0:T(8,128)(2,1)} %copy-done.36, ...), custom_call_target="tpu_custom_call" | custom-call | tf_op jit(solution)/shard_map/upstream/pallas_call | solution.py:176
  137.1 8.9 %forward.1 = (bf16[512,128]{1,0:T(8,128)(2,1)}, bf16[128,512]{1,0:T(8,128)(2,1)}, f32[1,512]{1,0:T(1,128)}, bf16[4096,256]{1,0:T(8,128)(2,1)}) custom-call(s32[8]{0:T(128)} %stack.130.idx, s32[1,512]{1,0:T(1,128)} %add_maximum_fusion.limit, bf16[512,128]{1,0:T(8,128)(2,1)} %get-tuple-element.34.q, bf16[512,256]{1,0:T(8,128)(2,1)} %get-tuple-element.35.refs_0_.kv, ...), custom_call_target="tpu_custom_call" | custom-call | tf_op jit(solution)/shard_map/forward/pallas_call | solution.py:239
  146.0 10.1 %backward.1 = (bf16[512,128]{1,0:T(8,128)(2,1)}, bf16[4096,256]{1,0:T(8,128)(2,1)}) custom-call(s32[1,512]{1,0:T(1,128)} %add_maximum_fusion.limit, f32[1,512]{1,0:T(1,128)} %get-tuple-element.38.lse, bf16[512,128]{1,0:T(8,128)(2,1)} %get-tuple-element.34.q, bf16[4096,256]{1,0:T(8,128)(2,1)} %get-tuple-element.39.kv, bf16[512,128]{1,0:T(8,128)(2,1)} %get-tuple-element.40.da, ...), custom_call_target="tpu_custom_call" | custom-call | tf_op jit(solution)/shard_map/backward/pallas_call | solution.py:269
  156.1 5.7 %all-to-all-start.1 = ((bf16[8,512,256]{2,1,0:T(8,128)(2,1)}), bf16[8,512,256]{2,1,0:T(8,128)(2,1)S(1)}, u32[]{:S(2)}, u32[]{:S(2)}) async-start(bf16[8,512,256]{2,1,0:T(8,128)(2,1)} %bitcast.44), calls=%async_computation.1 | async-start | bytes 4194304 | tf_op jit(solution)/shard_map/all_to_all | solution.py:47
  161.8 26.8 %all-to-all-done.1.dkv = bf16[8,512,256]{2,1,0:T(8,128)(2,1)S(1)} async-done(((bf16[8,512,256]{2,1,0:T(8,128)(2,1)}), bf16[8,512,256]{2,1,0:T(8,128)(2,1)S(1)}, u32[]{:S(2)}, u32[]{:S(2)}) %all-to-all-start.1) | async-done | bytes 2097184 | tf_op jit(solution)/shard_map/all_to_all | solution.py:47
  188.6 6.9 %all-to-all-start = ((bf16[16,128,256]{2,1,0:T(8,128)(2,1)}), bf16[16,128,256]{2,1,0:T(8,128)(2,1)S(1)}, u32[]{:S(2)}, u32[]{:S(2)}) async-start(bf16[16,128,256]{2,1,0:T(8,128)(2,1)} %get-tuple-element.37.refs_16_), calls=%async_computation | async-start | bytes 2097152 | tf_op jit(solution)/shard_map/all_to_all | solution.py:47
  195.4 3.5 %weight_grad.1.dwo = bf16[16,128,256]{2,1,0:T(8,128)(2,1)} custom-call(bf16[128,512]{1,0:T(8,128)(2,1)} %get-tuple-element.41.att_t.left, bf16[16,512,256]{2,1,0:T(8,128)(2,1)} %get-tuple-element.44.right), custom_call_target="tpu_custom_call" | custom-call | tf_op jit(solution)/shard_map/weight_grad/pallas_call | solution.py:370
  199.0 7.3 %gradients.1 = (bf16[512,384]{1,0:T(8,128)(2,1)}, f32[8,512]{1,0:T(8,128)}, bf16[16,512,256]{2,1,0:T(8,128)(2,1)}) custom-call(bf16[8,512,256]{2,1,0:T(8,128)(2,1)} %copy-done, bf16[512,128]{1,0:T(8,128)(2,1)} %get-tuple-element.43.dq, bf16[512,128]{1,0:T(8,128)(2,1)} %get-tuple-element.34.q, bf16[512,256]{1,0:T(8,128)(2,1)} %get-tuple-element.35.refs_0_.kv, ...), custom_call_target="tpu_custom_call" | custom-call | tf_op jit(solution)/shard_map/gradients/pallas_call | solution.py:324
  209.0 5.8 %input_grad.1 = (bf16[2,528,256]{2,1,0:T(8,128)(2,1)}, bf16[2,528,256]{2,1,0:T(8,128)(2,1)}, bf16[2,528,256]{2,1,0:T(8,128)(2,1)}, bf16[2,528,256]{2,1,0:T(8,128)(2,1)}) custom-call(s32[8]{0:T(128)} %stack.139.idx, bf16[512,384]{1,0:T(8,128)(2,1)} %get-tuple-element.45.g, bf16[512,384]{1,0:T(8,128)(2,1)} %copy-done.24, ...), custom_call_target="tpu_custom_call" | custom-call | tf_op jit(solution)/shard_map/input_grad/pallas_call | solution.py:354
  220.8 9.9 %collective-permute-done.62.refs_1_ = bf16[2,528,256]{2,1,0:T(8,128)(2,1)S(1)} collective-permute-done((bf16[2,528,256]{2,1,0:T(8,128)(2,1)}, bf16[2,528,256]{2,1,0:T(8,128)(2,1)S(1)}, u32[]{:S(2)}, u32[]{:S(2)}) %collective-permute-start.62) | collective-permute-done | bytes 540704 | tf_op jit(solution)/shard_map/ppermute | solution.py:30
  230.8 12.7 %collective-permute-done.63.refs_2_ = bf16[2,528,256]{2,1,0:T(8,128)(2,1)S(1)} collective-permute-done((bf16[2,528,256]{2,1,0:T(8,128)(2,1)}, bf16[2,528,256]{2,1,0:T(8,128)(2,1)S(1)}, u32[]{:S(2)}, u32[]{:S(2)}) %collective-permute-start.63) | collective-permute-done | bytes 540704 | tf_op jit(solution)/shard_map/ppermute | solution.py:30
  244.5 3.1 line_sum.1
  247.6 11.0 %all_to_all.20 = f32[16,2,256]{2,1,0:T(2,128)S(1)} all-to-all(f32[16,2,256]{2,1,0:T(2,128)} %bitcast.45), channel_id=1, replica_groups=mesh['x'=4,'h'=2,'c'=2,'z'=4,'u'=2] {'z','u','h'}, dimensions={0} | all-to-all | bytes 65536 | tf_op jit(solution)/shard_map/all_to_all | solution.py:47
  258.6 4.7 %all-to-all-start.2 = ((bf16[8,2,512,256]{3,2,1,0:T(8,128)(2,1)}), bf16[8,2,512,256]{3,2,1,0:T(8,128)(2,1)}, u32[]{:S(2)}, u32[]{:S(2)}) async-start(bf16[8,2,512,256]{3,2,1,0:T(8,128)(2,1)} %bitcast.43), calls=%async_computation.2 | async-start | bytes 8388608 | tf_op jit(solution)/shard_map/all_to_all | solution.py:47
  268.5 42.4 %collective-permute-done.32.refs_4_ = bf16[512,128]{1,0:T(8,128)(2,1)S(1)} collective-permute-done((bf16[512,128]{1,0:T(8,128)(2,1)S(1)}, bf16[512,128]{1,0:T(8,128)(2,1)S(1)}, u32[]{:S(2)}, u32[]{:S(2)}) %collective-permute-start.32) | collective-permute-done | bytes 131104 | tf_op jit(solution)/shard_map/ppermute | solution.py:26
  318.1 4.1 %collective-permute-done.35.refs_7_ = bf16[512,128]{1,0:T(8,128)(2,1)S(1)} collective-permute-done((bf16[512,128]{1,0:T(8,128)(2,1)S(1)}, bf16[512,128]{1,0:T(8,128)(2,1)S(1)}, u32[]{:S(2)}, u32[]{:S(2)}) %collective-permute-start.35) | collective-permute-done | bytes 131104 | tf_op jit(solution)/shard_map/ppermute | solution.py:30
  325.4 4.7 %output.1 = bf16[512,256]{1,0:T(8,128)(2,1)} custom-call(s32[16]{0:T(128)} %stack.121.idx, bf16[512,128]{1,0:T(8,128)(2,1)} %get-tuple-element.36.refs_0_, bf16[512,128]{1,0:T(8,128)(2,1)} %copy-done.47, bf16[512,128]{1,0:T(8,128)(2,1)} %copy-done.48, bf16[512,128]{1,0:T(8,128)(2,1)} %copy-done.49, bf16[512,128]{1,0:T(8,128)(2,1)} %copy-done.46, ...), custom_call_target="tpu_custom_call" | custom-call | tf_op jit(solution)/shard_map/output/pallas_call | solution.py:453
  333.9 3.4 sum_weights.1
  (261 shorter events, 78.9 us)
Async XLA Ops:
  11.7 16.9 %collective-permute-start.1 = (bf16[528,256]{1,0:T(8,128)(2,1)S(1)}, bf16[528,256]{1,0:T(8,128)(2,1)S(1)}, u32[]{:S(2)}, u32[]{:S(2)}) collective-permute-start(bf16[528,256]{1,0:T(8,128)(2,1)S(1)} %concatenate.6.refs_0_.refs_16_), channel_id=1, source_target_pairs={{0,96},{32,0},{64,32},{96,64},{1,97},{33,1},{65,33},{97,65},{2,98}... | collective-permute-start | bytes 811016 | tf_op jit(solution)/shard_map/ppermute | solution.py:30
  18.9 16.4 %collective-permute-start.3 = (bf16[528,256]{1,0:T(8,128)(2,1)S(1)}, bf16[528,256]{1,0:T(8,128)(2,1)S(1)}, u32[]{:S(2)}, u32[]{:S(2)}) collective-permute-start(bf16[528,256]{1,0:T(8,128)(2,1)S(1)} %concatenate.6.refs_0_.refs_16_), channel_id=1, source_target_pairs={{0,16},{16,0},{1,17},{17,1},{2,18},{18,2},{3,19},{19,3},{4,20},{20... | collective-permute-start | bytes 811016 | tf_op jit(solution)/shard_map/ppermute | solution.py:26
  22.7 16.2 %collective-permute-start.15 = (bf16[2,512,256]{2,1,0:T(8,128)(2,1)}, bf16[2,512,256]{2,1,0:T(8,128)(2,1)S(1)}, u32[]{:S(2)}, u32[]{:S(2)}) collective-permute-start(bf16[2,512,256]{2,1,0:T(8,128)(2,1)} %pack_weights.1.refs_0_), channel_id=1, source_target_pairs={{0,2},{2,4},{4,6},{6,0},{1,3},{3,5},{5,7},{7,1},{8,10},{10,12},{12... | collective-permute-start | bytes 1572872 | tf_op jit(solution)/shard_map/ppermute | solution.py:30
  24.7 25.1 %collective-permute-start.16 = (bf16[2,512,256]{2,1,0:T(8,128)(2,1)}, bf16[2,512,256]{2,1,0:T(8,128)(2,1)S(1)}, u32[]{:S(2)}, u32[]{:S(2)}) collective-permute-start(bf16[2,512,256]{2,1,0:T(8,128)(2,1)} %pack_weights.1.refs_0_), channel_id=1, source_target_pairs={{0,6},{2,0},{4,2},{6,4},{1,7},{3,1},{5,3},{7,5},{8,14},{10,8},{12,... | collective-permute-start | bytes 1572872 | tf_op jit(solution)/shard_map/ppermute | solution.py:30
  28.6 22.4 %collective-permute-start.17 = (bf16[2,512,256]{2,1,0:T(8,128)(2,1)}, bf16[2,512,256]{2,1,0:T(8,128)(2,1)S(1)}, u32[]{:S(2)}, u32[]{:S(2)}) collective-permute-start(bf16[2,512,256]{2,1,0:T(8,128)(2,1)} %pack_weights.1.refs_0_), channel_id=1, source_target_pairs={{0,4},{2,6},{4,0},{6,2},{1,5},{3,7},{5,1},{7,3},{8,12},{10,14},{12... | collective-permute-start | bytes 1572872 | tf_op jit(solution)/shard_map/ppermute | solution.py:30
  32.0 19.6 %collective-permute-start.18 = (bf16[2,512,256]{2,1,0:T(8,128)(2,1)}, bf16[2,512,256]{2,1,0:T(8,128)(2,1)S(1)}, u32[]{:S(2)}, u32[]{:S(2)}) collective-permute-start(bf16[2,512,256]{2,1,0:T(8,128)(2,1)} %pack_weights.1.refs_0_), channel_id=1, source_target_pairs={{0,1},{1,0},{2,3},{3,2},{4,5},{5,4},{6,7},{7,6},{8,9},{9,8},{10,11... | collective-permute-start | bytes 1572872 | tf_op jit(solution)/shard_map/ppermute | solution.py:26
  36.8 22.2 %collective-permute-start.4 = (bf16[528,256]{1,0:T(8,128)(2,1)S(1)}, bf16[528,256]{1,0:T(8,128)(2,1)S(1)}, u32[]{:S(2)}, u32[]{:S(2)}) collective-permute-start(bf16[528,256]{1,0:T(8,128)(2,1)S(1)} %collective-permute-done.3.refs_4_.refs_20_.refs_5_), channel_id=1, source_target_pairs={{0,32},{32,64},{64,96},{96,0},{1,33},{33,65},{65,97},{97,1},{2,34}... | collective-permute-start | bytes 811016 | tf_op jit(solution)/shard_map/ppermute | solution.py:30
  64.3 26.4 %collective-permute-start.19 = (bf16[2,512,256]{2,1,0:T(8,128)(2,1)S(1)}, bf16[2,512,256]{2,1,0:T(8,128)(2,1)S(1)}, u32[]{:S(2)}, u32[]{:S(2)}) collective-permute-start(bf16[2,512,256]{2,1,0:T(8,128)(2,1)S(1)} %collective-permute-done.18.refs_4_), channel_id=1, source_target_pairs={{0,2},{2,4},{4,6},{6,0},{1,3},{3,5},{5,7},{7,1},{8,10},{10,12},{12... | collective-permute-start | bytes 1572872 | tf_op jit(solution)/shard_map/ppermute | solution.py:30
  65.3 25.4 %collective-permute-start.20 = (bf16[2,512,256]{2,1,0:T(8,128)(2,1)S(1)}, bf16[2,512,256]{2,1,0:T(8,128)(2,1)S(1)}, u32[]{:S(2)}, u32[]{:S(2)}) collective-permute-start(bf16[2,512,256]{2,1,0:T(8,128)(2,1)S(1)} %collective-permute-done.18.refs_4_), channel_id=1, source_target_pairs={{0,6},{2,0},{4,2},{6,4},{1,7},{3,1},{5,3},{7,5},{8,14},{10,8},{12,... | collective-permute-start | bytes 1572872 | tf_op jit(solution)/shard_map/ppermute | solution.py:30
  67.6 23.6 %collective-permute-start.21 = (bf16[2,512,256]{2,1,0:T(8,128)(2,1)S(1)}, bf16[2,512,256]{2,1,0:T(8,128)(2,1)S(1)}, u32[]{:S(2)}, u32[]{:S(2)}) collective-permute-start(bf16[2,512,256]{2,1,0:T(8,128)(2,1)S(1)} %collective-permute-done.18.refs_4_), channel_id=1, source_target_pairs={{0,4},{2,6},{4,0},{6,2},{1,5},{3,7},{5,1},{7,3},{8,12},{10,14},{12... | collective-permute-start | bytes 1572872 | tf_op jit(solution)/shard_map/ppermute | solution.py:30
  70.3 37.0 %collective-permute-start.50 = (bf16[512,256]{1,0:T(8,128)(2,1)}, bf16[512,256]{1,0:T(8,128)(2,1)}, u32[]{:S(2)}, u32[]{:S(2)}) collective-permute-start(bf16[512,256]{1,0:T(8,128)(2,1)} %copy-done.36), channel_id=1, source_target_pairs={{0,64},{32,96},{64,0},{96,32},{1,65},{33,97},{65,1},{97,33},{2,66}... | collective-permute-start | bytes 786440 | tf_op jit(solution)/shard_map/ppermute | solution.py:30
  72.9 34.8 %collective-permute-start.52 = (bf16[512,256]{1,0:T(8,128)(2,1)}, bf16[512,256]{1,0:T(8,128)(2,1)}, u32[]{:S(2)}, u32[]{:S(2)}) collective-permute-start(bf16[512,256]{1,0:T(8,128)(2,1)} %copy-done.33), channel_id=1, source_target_pairs={{0,8},{8,0},{1,9},{9,1},{2,10},{10,2},{3,11},{11,3},{4,12},{12,4},... | collective-permute-start | bytes 786440 | tf_op jit(solution)/shard_map/ppermute | solution.py:26
  90.7 17.2 %collective-permute-start.53 = (bf16[512,256]{1,0:T(8,128)(2,1)}, bf16[512,256]{1,0:T(8,128)(2,1)}, u32[]{:S(2)}, u32[]{:S(2)}) collective-permute-start(bf16[512,256]{1,0:T(8,128)(2,1)} %copy-done.34), channel_id=1, source_target_pairs={{0,8},{8,0},{1,9},{9,1},{2,10},{10,2},{3,11},{11,3},{4,12},{12,4},... | collective-permute-start | bytes 786440 | tf_op jit(solution)/shard_map/ppermute | solution.py:26
  90.7 17.6 %collective-permute-start.54 = (bf16[512,256]{1,0:T(8,128)(2,1)}, bf16[512,256]{1,0:T(8,128)(2,1)}, u32[]{:S(2)}, u32[]{:S(2)}) collective-permute-start(bf16[512,256]{1,0:T(8,128)(2,1)} %copy-done.35), channel_id=1, source_target_pairs={{0,8},{8,0},{1,9},{9,1},{2,10},{10,2},{3,11},{11,3},{4,12},{12,4},... | collective-permute-start | bytes 786440 | tf_op jit(solution)/shard_map/ppermute | solution.py:26
  91.5 16.8 %collective-permute-start.55 = (bf16[512,256]{1,0:T(8,128)(2,1)}, bf16[512,256]{1,0:T(8,128)(2,1)}, u32[]{:S(2)}, u32[]{:S(2)}) collective-permute-start(bf16[512,256]{1,0:T(8,128)(2,1)} %copy-done.36), channel_id=1, source_target_pairs={{0,8},{8,0},{1,9},{9,1},{2,10},{10,2},{3,11},{11,3},{4,12},{12,4},... | collective-permute-start | bytes 786440 | tf_op jit(solution)/shard_map/ppermute | solution.py:26
  110.7 25.3 %collective-permute-start.23 = (bf16[512,256]{1,0:T(8,128)(2,1)}, bf16[512,256]{1,0:T(8,128)(2,1)S(1)}, u32[]{:S(2)}, u32[]{:S(2)}) collective-permute-start(bf16[512,256]{1,0:T(8,128)(2,1)} %get-tuple-element.35.refs_0_.kv), channel_id=1, source_target_pairs={{0,6},{2,0},{4,2},{6,4},{1,7},{3,1},{5,3},{7,5},{8,14},{10,8},{12,... | collective-permute-start | bytes 786440 | tf_op jit(solution)/shard_map/ppermute | solution.py:30
  114.0 22.1 %collective-permute-start.24 = (bf16[512,256]{1,0:T(8,128)(2,1)}, bf16[512,256]{1,0:T(8,128)(2,1)S(1)}, u32[]{:S(2)}, u32[]{:S(2)}) collective-permute-start(bf16[512,256]{1,0:T(8,128)(2,1)} %get-tuple-element.35.refs_0_.kv), channel_id=1, source_target_pairs={{0,4},{2,6},{4,0},{6,2},{1,5},{3,7},{5,1},{7,3},{8,12},{10,14},{12... | collective-permute-start | bytes 786440 | tf_op jit(solution)/shard_map/ppermute | solution.py:30
  118.4 17.6 %collective-permute-start.26 = (bf16[512,256]{1,0:T(8,128)(2,1)S(1)}, bf16[512,256]{1,0:T(8,128)(2,1)S(1)}, u32[]{:S(2)}, u32[]{:S(2)}) collective-permute-start(bf16[512,256]{1,0:T(8,128)(2,1)S(1)} %collective-permute-done.25.refs_4_), channel_id=1, source_target_pairs={{0,2},{2,4},{4,6},{6,0},{1,3},{3,5},{5,7},{7,1},{8,10},{10,12},{12... | collective-permute-start | bytes 786440 | tf_op jit(solution)/shard_map/ppermute | solution.py:30
  118.5 17.9 %collective-permute-start.27 = (bf16[512,256]{1,0:T(8,128)(2,1)S(1)}, bf16[512,256]{1,0:T(8,128)(2,1)S(1)}, u32[]{:S(2)}, u32[]{:S(2)}) collective-permute-start(bf16[512,256]{1,0:T(8,128)(2,1)S(1)} %collective-permute-done.25.refs_4_), channel_id=1, source_target_pairs={{0,6},{2,0},{4,2},{6,4},{1,7},{3,1},{5,3},{7,5},{8,14},{10,8},{12,... | collective-permute-start | bytes 786440 | tf_op jit(solution)/shard_map/ppermute | solution.py:30
  156.1 32.5 %all-to-all-start.1 = ((bf16[8,512,256]{2,1,0:T(8,128)(2,1)}), bf16[8,512,256]{2,1,0:T(8,128)(2,1)S(1)}, u32[]{:S(2)}, u32[]{:S(2)}) async-start(bf16[8,512,256]{2,1,0:T(8,128)(2,1)} %bitcast.44), calls=%async_computation.1 | async-start | bytes 4194304 | tf_op jit(solution)/shard_map/all_to_all | solution.py:47
  161.8 45.9 %collective-permute-start.60 = (bf16[8,384,256]{2,1,0:T(8,128)(2,1)}, bf16[8,384,256]{2,1,0:T(8,128)(2,1)}, u32[]{:S(2)}, u32[]{:S(2)}) collective-permute-start(bf16[8,384,256]{2,1,0:T(8,128)(2,1)} %get-tuple-element.47), channel_id=1, source_target_pairs={{0,8},{8,0},{1,9},{9,1},{2,10},{10,2},{3,11},{11,3},{4,12},{12,4},... | collective-permute-start | bytes 4718600 | tf_op jit(solution)/shard_map/ppermute | solution.py:26
  188.6 59.0 %all-to-all-start = ((bf16[16,128,256]{2,1,0:T(8,128)(2,1)}), bf16[16,128,256]{2,1,0:T(8,128)(2,1)S(1)}, u32[]{:S(2)}, u32[]{:S(2)}) async-start(bf16[16,128,256]{2,1,0:T(8,128)(2,1)} %get-tuple-element.37.refs_16_), calls=%async_computation | async-start | bytes 2097152 | tf_op jit(solution)/shard_map/all_to_all | solution.py:47
  214.8 16.0 %collective-permute-start.62 = (bf16[2,528,256]{2,1,0:T(8,128)(2,1)}, bf16[2,528,256]{2,1,0:T(8,128)(2,1)S(1)}, u32[]{:S(2)}, u32[]{:S(2)}) collective-permute-start(bf16[2,528,256]{2,1,0:T(8,128)(2,1)} %get-tuple-element.50), channel_id=1, source_target_pairs={{0,32},{32,64},{64,96},{96,0},{1,33},{33,65},{65,97},{97,1},{2,34}... | collective-permute-start | bytes 1622024 | tf_op jit(solution)/shard_map/ppermute | solution.py:30
  216.7 26.8 %collective-permute-start.63 = (bf16[2,528,256]{2,1,0:T(8,128)(2,1)}, bf16[2,528,256]{2,1,0:T(8,128)(2,1)S(1)}, u32[]{:S(2)}, u32[]{:S(2)}) collective-permute-start(bf16[2,528,256]{2,1,0:T(8,128)(2,1)} %get-tuple-element.51), channel_id=1, source_target_pairs={{0,64},{32,96},{64,0},{96,32},{1,65},{33,97},{65,1},{97,33},{2,66}... | collective-permute-start | bytes 1622024 | tf_op jit(solution)/shard_map/ppermute | solution.py:30
  219.4 24.1 %collective-permute-start.64 = (bf16[2,528,256]{2,1,0:T(8,128)(2,1)}, bf16[2,528,256]{2,1,0:T(8,128)(2,1)S(1)}, u32[]{:S(2)}, u32[]{:S(2)}) collective-permute-start(bf16[2,528,256]{2,1,0:T(8,128)(2,1)} %get-tuple-element.52), channel_id=1, source_target_pairs={{0,96},{32,0},{64,32},{96,64},{1,97},{33,1},{65,33},{97,65},{2,98}... | collective-permute-start | bytes 1622024 | tf_op jit(solution)/shard_map/ppermute | solution.py:30
  258.6 75.2 %all-to-all-start.2 = ((bf16[8,2,512,256]{3,2,1,0:T(8,128)(2,1)}), bf16[8,2,512,256]{3,2,1,0:T(8,128)(2,1)}, u32[]{:S(2)}, u32[]{:S(2)}) async-start(bf16[8,2,512,256]{3,2,1,0:T(8,128)(2,1)} %bitcast.43), calls=%async_computation.2 | async-start | bytes 8388608 | tf_op jit(solution)/shard_map/all_to_all | solution.py:47
  263.3 47.6 %collective-permute-start.32 = (bf16[512,128]{1,0:T(8,128)(2,1)S(1)}, bf16[512,128]{1,0:T(8,128)(2,1)S(1)}, u32[]{:S(2)}, u32[]{:S(2)}) collective-permute-start(bf16[512,128]{1,0:T(8,128)(2,1)S(1)} %copy-done.45), channel_id=1, source_target_pairs={{0,16},{16,0},{1,17},{17,1},{2,18},{18,2},{3,19},{19,3},{4,20},{20... | collective-permute-start | bytes 393224 | tf_op jit(solution)/shard_map/ppermute | solution.py:26
  264.0 47.9 %collective-permute-start.29 = (bf16[512,128]{1,0:T(8,128)(2,1)S(1)}, bf16[512,128]{1,0:T(8,128)(2,1)S(1)}, u32[]{:S(2)}, u32[]{:S(2)}) collective-permute-start(bf16[512,128]{1,0:T(8,128)(2,1)S(1)} %copy-done.45), channel_id=1, source_target_pairs={{0,32},{32,64},{64,96},{96,0},{1,33},{33,65},{65,97},{97,1},{2,34}... | collective-permute-start | bytes 393224 | tf_op jit(solution)/shard_map/ppermute | solution.py:30
  265.0 49.2 %collective-permute-start.30 = (bf16[512,128]{1,0:T(8,128)(2,1)S(1)}, bf16[512,128]{1,0:T(8,128)(2,1)S(1)}, u32[]{:S(2)}, u32[]{:S(2)}) collective-permute-start(bf16[512,128]{1,0:T(8,128)(2,1)S(1)} %copy-done.45), channel_id=1, source_target_pairs={{0,96},{32,0},{64,32},{96,64},{1,97},{33,1},{65,33},{97,65},{2,98}... | collective-permute-start | bytes 393224 | tf_op jit(solution)/shard_map/ppermute | solution.py:30
  267.2 48.5 %collective-permute-start.31 = (bf16[512,128]{1,0:T(8,128)(2,1)S(1)}, bf16[512,128]{1,0:T(8,128)(2,1)S(1)}, u32[]{:S(2)}, u32[]{:S(2)}) collective-permute-start(bf16[512,128]{1,0:T(8,128)(2,1)S(1)} %copy-done.45), channel_id=1, source_target_pairs={{0,64},{32,96},{64,0},{96,32},{1,65},{33,97},{65,1},{97,33},{2,66}... | collective-permute-start | bytes 393224 | tf_op jit(solution)/shard_map/ppermute | solution.py:30
  268.5 48.3 %collective-permute-start.36 = (bf16[512,128]{1,0:T(8,128)(2,1)S(1)}, bf16[512,128]{1,0:T(8,128)(2,1)S(1)}, u32[]{:S(2)}, u32[]{:S(2)}) collective-permute-start(bf16[512,128]{1,0:T(8,128)(2,1)S(1)} %copy-done.45), channel_id=1, source_target_pairs={{0,8},{8,0},{1,9},{9,1},{2,10},{10,2},{3,11},{11,3},{4,12},{12,4},... | collective-permute-start | bytes 393224 | tf_op jit(solution)/shard_map/ppermute | solution.py:26
  314.2 16.5 %collective-permute-start.65 = (bf16[528,256]{1,0:T(8,128)(2,1)S(1)}, bf16[528,256]{1,0:T(8,128)(2,1)S(1)}, u32[]{:S(2)}, u32[]{:S(2)}) collective-permute-start(bf16[528,256]{1,0:T(8,128)(2,1)S(1)} %copy-done.63), channel_id=1, source_target_pairs={{0,16},{16,0},{1,17},{17,1},{2,18},{18,2},{3,19},{19,3},{4,20},{20... | collective-permute-start | bytes 811016 | tf_op jit(solution)/shard_map/ppermute | solution.py:26
  (101 other events, 1347.0 us)

commit v2 on v1

--- a/solution.py
+++ b/solution.py
@@ -40,7 +40,11 @@
 
 
 def gather_tokens_axes(block):
-    return turns(block, "z") + turns(swap(block, "u"), "z")
+    own = [block] + [turn(block, d, "z") for d in (1, 3)]
+    own.append(turn(block, 2, "z"))
+    near = swap(block, "u")
+    near = [near] + [turn(near, d, "z") for d in (1, 3)]
+    return own + near + [swap(own[3], "u")]
 
 
 def exchange(blocks, axis):
@@ -112,7 +116,7 @@
         out_specs=[pl.BlockSpec((16, tile, 256), lambda i: (0, i, 0)), rows(1)],
         out_shape=[shape((16, 512, 256)), shape((512, 1), F32)],
         compiler_params=PARAMS,
-    )(idx, *xs, *xs, modality[:, None])
+    )(idx, *xs, *xs, modality)
 
 
 def project_kernel(idx, normed, *refs):
@@ -141,52 +145,59 @@
 
 
 def order_kernel(idx, core, *refs):
-    ws, (kept, sent, wo) = refs[:8], refs[8:]
+    ws, (kept, sent) = refs[:8], refs[8:]
     for n in range(8):
         k = idx[n]
-        kept[k] = ws[n][core[0], 0:384, :]
-        sent[k] = ws[n][1 - core[0], 0:384, :]
-        for s in range(2):
-            wo[k * 2 + s] = ws[n][s, 384:512, :]
+        kept[k] = ws[n][core[0]]
+        sent[k] = ws[n][1 - core[0]]
 
 
 def order_weights(idx, core, ws):
-    vmem = pl.BlockSpec(memory_space=pltpu.VMEM)
     return pl.pallas_call(
         order_kernel,
         name="order_weights",
-        in_specs=[SMEM, SMEM] + [vmem] * 8,
-        out_shape=[shape((8, 384, 256)), shape((8, 384, 256)), shape((16, 128, 256))],
+        grid=(1,),
+        in_specs=[SMEM, SMEM] + [fixed(2, 384, 256)] * 8,
+        out_specs=[fixed(8, 384, 256)] * 2,
+        out_shape=[shape((8, 384, 256))] * 2,
         compiler_params=PARAMS,
     )(idx, core, *ws)
 
 
-def upstream_kernel(idx, *refs):
-    gs, (w, out, ordered) = refs[:16], refs[16:]
+def upstream_kernel(idx, tok_idx, *refs):
+    gs, ws, (out, ordered, wo) = refs[:16], refs[16:24], refs[24:]
+
+    @pl.when(pl.program_id(0) == 0)
+    def _():
+        for n in range(8):
+            for s in range(2):
+                wo[tok_idx[n] * 2 + s] = ws[n][s]
+
     acc = jnp.zeros(out.shape, F32)
     for n in range(16):
         g = gs[n][...]
         ordered[idx[n]] = g
-        acc = acc + dot(g, w[idx[n]], NT)
+        acc = acc + dot(g, wo[idx[n]], NT)
     out[...] = acc.astype(BF16)
 
 
-def upstream(idx, gs, wo):
+def upstream(idx, tok_idx, gs, ws):
     tile = 128
     return pl.pallas_call(
         upstream_kernel,
         name="upstream",
         grid=(512 // tile,),
-        in_specs=[SMEM]
+        in_specs=[SMEM, SMEM]
         + [pl.BlockSpec((tile, 256), lambda i: (i, 0))] * 16
-        + [fixed(16, 128, 256)],
+        + [pl.BlockSpec((2, 128, 256), lambda i: (0, 3, 0))] * 8,
         out_specs=[
             pl.BlockSpec((tile, 128), lambda i: (i, 0)),
             pl.BlockSpec((16, tile, 256), lambda i: (0, i, 0)),
+            fixed(16, 128, 256),
         ],
-        out_shape=[shape((512, 128)), shape((16, 512, 256))],
-        compiler_params=PARAMS,
-    )(idx, *gs, wo)
+        out_shape=[shape((512, 128)), shape((16, 512, 256)), shape((16, 128, 256))],
+        compiler_params=PARAMS,
+    )(idx, tok_idx, *gs, *ws)
 
 
 KEY_BLOCK = 512
@@ -292,7 +303,7 @@
     return (t[0:2] + t[2:4]) + t[4:6]
 
 
-def gradients_kernel(dkv, dq, q, kv, normed, dwo, g_out, dots, out, g_t):
+def gradients_kernel(idx, dkv, dq, q, kv, n0, n1, w0, w1, g_out, dots, up, down, far, far_next, here, g_t):
     step = pl.program_id(0)
 
     @pl.when(step == 0)
@@ -312,32 +323,77 @@
             ones, prod, NT, precision=lax.Precision.HIGHEST, preferred_element_type=F32
         )
 
-    @pl.when(step > 0)
-    def _():
-        for k in range(8):
-            out[k, 0:384, :] = dot(g_t[...], normed[k]).astype(BF16)
-            out[k, 384:512, :] = dwo[k]
-
-
-def gradients(dkv, dq, q, kv, normed, dwo):
-    later = lambda i: (jnp.maximum(i - 1, 0), 0, 0)
-    return pl.pallas_call(
-        gradients_kernel,
-        name="gradients",
-        grid=(3,),
+    outs = ((up.at[0], up.at[1]), (down.at[0], down.at[1]), (far, far_next), (here.at[0], here.at[1]))
+    for n, pair in enumerate(outs):
+
+        @pl.when(step == n + 1)
+        def _(pair=pair):
+            for out, block, wo in ((pair[0], n0, w0), (pair[1], n1, w1)):
+                for k in range(2):
+                    out[k, 0:384, :] = dot(g_t[...], block[k]).astype(BF16)
+                    out[k, 384:512, :] = wo[k]
+
+
+def gradients(idx, dkv, dq, q, kv, normed, dwo):
+    at = lambda slot: lambda i, idx: (idx[2 * jnp.maximum(i - 1, 0) + slot], 0, 0)
+    spec = pltpu.PrefetchScalarGridSpec(
+        num_scalar_prefetch=1,
+        grid=(5,),
         in_specs=[
             fixed(8, 512, 256),
             fixed(512, 128),
             fixed(512, 128),
             fixed(512, 256),
-            pl.BlockSpec((8, 512, 256), later),
-            pl.BlockSpec((8, 128, 256), later),
+            pl.BlockSpec((2, 512, 256), at(0)),
+            pl.BlockSpec((2, 512, 256), at(1)),
+            pl.BlockSpec((2, 128, 256), at(0)),
+            pl.BlockSpec((2, 128, 256), at(1)),
         ],
-        out_specs=[fixed(512, 384), fixed(8, 512), pl.BlockSpec((8, 512, 256), later)],
-        out_shape=[shape((512, 384)), shape((8, 512), F32), shape((16, 512, 256))],
+        out_specs=[
+            fixed(512, 384),
+            fixed(8, 512),
+            fixed(2, 2, 512, 256),
+            fixed(2, 2, 512, 256),
+            fixed(2, 512, 256),
+            fixed(2, 512, 256),
+            fixed(2, 2, 512, 256),
+        ],
         scratch_shapes=[pltpu.VMEM((384, 512), BF16)],
-        compiler_params=PARAMS,
-    )(dkv, dq, q, kv, normed, dwo)
+    )
+    return pl.pallas_call(
+        gradients_kernel,
+        name="gradients",
+        grid_spec=spec,
+        out_shape=[
+            shape((512, 384)),
+            shape((8, 512), F32),
+            shape((2, 2, 512, 256)),
+            shape((2, 2, 512, 256)),
+            shape((2, 512, 256)),
+            shape((2, 512, 256)),
+            shape((2, 2, 512, 256)),
+        ],
+        compiler_params=PARAMS,
+    )(idx, dkv, dq, q, kv, normed, normed, dwo, dwo)
+
+
+def add_kernel(*refs):
+    total = refs[0][...].astype(F32)
+    for t in refs[1:-1]:
+        total = total + t[...].astype(F32)
+    refs[-1][...] = total.astype(BF16)
+
+
+def add_blocks(terms, specs):
+    return pl.pallas_call(
+        add_kernel,
+        name="add_blocks",
+        grid=(2,),
+        in_specs=specs,
+        out_specs=pl.BlockSpec((None, 512, 256), lambda i: (i, 0, 0)),
+        out_shape=shape((2, 512, 256)),
+        compiler_params=PARAMS,
+    )(*terms)
 
 
 def input_grad_kernel(idx, g, g2, w, w2, dots, dots2, *outs):
@@ -418,7 +474,7 @@
             shape((8, 2, 2, 256), F32),
         ],
         compiler_params=PARAMS,
-    )(side, *terms, x, x_next, inv, modality[:, None])
+    )(side, *terms, x, x_next, inv, modality)
 
 
 def finish_kernel(own, own_dots, last, x, inv, mod, gain, grad_in):
@@ -437,7 +493,7 @@
         name="finish",
         out_shape=shape((512, 256)),
         compiler_params=PARAMS,
-    )(own, own_dots, last, x, inv, modality[:, None], gain)
+    )(own, own_dots, last, x, inv, modality, gain)
 
 
 def output_kernel(idx, *refs):
@@ -463,28 +519,34 @@
     )(idx, *atts, rows)
 
 
-def sum_weights_kernel(parts, qkv, wout):
-    total = parts[0, 0].astype(F32)
-    for k in range(1, 8):
-        total = total + parts[k, 0].astype(F32)
+def sum_weights_kernel(*refs):
+    parts, (qkv, wout) = refs[:5], refs[5:]
+    total = parts[0][...].astype(F32)
+    for t in parts[1:]:
+        total = total + t[...].astype(F32)
     for m in range(3):
         qkv[m] = total[m * 128 : (m + 1) * 128].T
     wout[...] = total[384:512]
 
 
+ONE = pl.BlockSpec((None, 512, 256), lambda i: (i, 0, 0))
+FIRST = pl.BlockSpec((None, None, 512, 256), lambda i: (0, i, 0, 0))
+SECOND = pl.BlockSpec((None, None, 512, 256), lambda i: (1, i, 0, 0))
+
+
 def sum_weights(parts):
     return pl.pallas_call(
         sum_weights_kernel,
         name="sum_weights",
         grid=(2,),
-        in_specs=[pl.BlockSpec((8, 1, 512, 256), lambda s: (0, s, 0, 0))],
+        in_specs=[FIRST, FIRST, FIRST, ONE, ONE],
         out_specs=[
             pl.BlockSpec((3, 256, 128), lambda s: (0, s, 0)),
             pl.BlockSpec((128, 256), lambda s: (0, s)),
         ],
         out_shape=[shape((3, 512, 128), F32), shape((128, 512), F32)],
         compiler_params=PARAMS,
-    )(parts)
+    )(*parts)
 
 
 def sublayer(layer_input, modality, image_spans, norm_gain, w_qkv, w_out, grad_out):
@@ -494,8 +556,11 @@
     idx = jnp.stack([a * 4 + b * 2 + e for a, b, e in blocks]).astype(jnp.int32)
     tok_idx = jnp.stack([((z - d) % 4) * 2 + (u ^ s) for s in range(2) for d in TURNS]).astype(jnp.int32)
     places = jnp.stack([((x + d) % 4) * 2 + (h ^ s) for d in range(4) for s in range(2)]).astype(jnp.int32)
+    outward = [((z + d) % 4) * 2 + (u ^ s) for d in (1, 3, 2, 0) for s in range(2)]
+    out_idx = jnp.stack(outward).astype(jnp.int32)
     core = c.astype(jnp.int32)[None]
     side = h.astype(jnp.int32)[None]
+    column = modality[:, None]
 
     gain_rows = jnp.concatenate(three_parts(norm_gain), axis=0).astype(BF16)
     gain_rows = jnp.concatenate([gain_rows, jnp.zeros((10, 256), BF16)], axis=0)
@@ -503,12 +568,12 @@
     ws = gather_tokens_axes(pack_weights(w_qkv, w_out))
     gs = spread(grad_out)
 
-    normed, inv = normalize(idx, xs, modality)
+    normed, inv = normalize(idx, xs, column)
     q, kv = project(tok_idx, normed, ws)
     kvs = gather_tokens_axes(kv)
-    w_kept, w_sent, wo = order_weights(tok_idx, core, ws)
+    w_kept, w_sent = order_weights(tok_idx, core, ws)
     w_other = swap(w_sent, "c")
-    da, g_all = upstream(idx, gs, wo)
+    da, g_all, wo = upstream(idx, tok_idx, gs, ws)
 
     pos = (z * 2 + u) * 512 + jnp.arange(512, dtype=jnp.int32)
     inside = (pos[:, None] >= image_spans[0][None]) & (pos[:, None] < image_spans[1][None])
@@ -524,16 +589,19 @@
     atts = spread(att)
     attn_out = output(idx, atts, out_rows)
 
-    g, dots, w_parts = gradients(dkv_parts, dq, q, kv, normed, dwo)
-    w_parts = exchange(w_parts.reshape(8, 2, 512, 256), TOKENS_AXES)
+    g, dots, up, down, far, far_next, here = gradients(out_idx, dkv_parts, dq, q, kv, normed, dwo)
+    far_next = swap(far_next, "u")
+    up, down = turn(up, 1, "z"), turn(down, 3, "z")
+    far = turn(add_blocks([far, far_next], [ONE, ONE]), 2, "z")
+    across = swap(add_blocks([here, up, down], [SECOND] * 3), "u")
     g2, dots2 = swap(g, "c"), swap(dots, "c")
     terms = input_grad(places, g, g2, w_kept, w_other, dots, dots2)
     terms = [turn(t, d) if d else t for d, t in enumerate(terms)]
-    own, own_dots, sent, gains = line_sum(side, terms, layer_input, xs[4], inv, modality)
+    own, own_dots, sent, gains = line_sum(side, terms, layer_input, xs[4], inv, column)
     last = swap(sent, "h")
     gains = exchange(gains.reshape(16, 2, 256), ("z", "u", "h"))
-    grad_in = finish(own, own_dots, last, layer_input, inv, modality, norm_gain)
-    grad_qkv, grad_wout = sum_weights(w_parts)
+    grad_in = finish(own, own_dots, last, layer_input, inv, column, norm_gain)
+    grad_qkv, grad_wout = sum_weights([here, up, down, far, across])
     grad_gain = jnp.sum(gains, axis=0)
     return (attn_out, grad_in, grad_qkv, grad_wout, grad_gain)
 

time: 340 us -> 280 us (0.82)
  waiting for transfers between devices: 147 us -> 85 us
  blocking collectives: 11 us -> 0 us
  starting transfers between devices: 91.9 us -> 98.2 us
  Pallas kernels: 74 us -> 79.8 us
    ppermute x33 -> x37, waiting for transfers between devices: 50.2 us -> 11.8 us  [swap(): return lax.ppermute(a, axis, [(0, 1), (1, 0)])]
    ppermute x33 -> x34, waiting for transfers between devices: 70.5 us -> 53.8 us  [turn(): return lax.ppermute(a, axis, [(i, (i + d) % 4) for i in range(4)])]
    all_to_all x1 -> x0, blocking collectives: 11 us -> none  [exchange(): return lax.all_to_all(blocks, axis, 0, 0, tiled=True)]
    ppermute x33 -> x34, starting transfers between devices: 57.9 us -> 66.5 us  [turn(): return lax.ppermute(a, axis, [(i, (i + d) % 4) for i in range(4)])]
    all_to_all x3, waiting for transfers between devices: 26.8 us -> 19.4 us  [exchange(): return lax.all_to_all(blocks, axis, 0, 0, tiled=True)]
    pallas_call x2 -> x4, Pallas kernels: 11.8 us -> 17.9 us  [the longest x1 9.36 us: gradients(): pl.pallas_call(gradients_kernel, name='gradients', grid_spec=spec, out_sh...]
    all_to_all x3, starting transfers between devices: 17.2 us -> 13.8 us  [exchange(): return lax.all_to_all(blocks, axis, 0, 0, tiled=True)]
    unnamed x128 -> x124, local copies, waits for them, and re-layouts: 5.1 us -> 6.82 us
  transfers between devices with their start and end apart: 69 -> 74, of which waited for: 25 -> 23; matrix products, arithmetic and copies ran while one was open for 2% -> 3% of each run, Pallas kernels for 15% -> 21%
where the time goes in v2:
time: 280 us; the launch traced here: 278 us
  starting transfers between devices  98.2 us (35%)
  waiting for transfers between devices  85 us (30%)
  Pallas kernels  79.8 us (28%)
  local copies, waits for them, and re-layouts  12.1 us (4%)
    ppermute x34, starting transfers between devices, turn(): return lax.ppermute(a, axis, [(i, (i + d) % 4) for i in range(4)])  66.5 us
    ppermute x34, waiting for transfers between devices, turn(): return lax.ppermute(a, axis, [(i, (i + d) % 4) for i in range(4)])  53.8 us
    all_to_all x3, waiting for transfers between devices, exchange(): return lax.all_to_all(blocks, axis, 0, 0, tiled=True)  19.4 us
    ppermute x37, starting transfers between devices, swap(): return lax.ppermute(a, axis, [(0, 1), (1, 0)])  17.9 us
    all_to_all x3, starting transfers between devices, exchange(): return lax.all_to_all(blocks, axis, 0, 0, tiled=True)  13.8 us
    ppermute x37, waiting for transfers between devices, swap(): return lax.ppermute(a, axis, [(0, 1), (1, 0)])  11.8 us
    pallas_call x1, Pallas kernels, backward(): pl.pallas_call(backward_kernel, name='backward', out_shape=[shape((512, 1...  10.1 us
    pallas_call x1, Pallas kernels, gradients(): pl.pallas_call(gradients_kernel, name='gradients', grid_spec=spec, out_sh...  9.36 us
  transfers between devices with their start and end apart: 74, of which 23 were waited for; matrix products, arithmetic and copies ran while one was open for 3% of the time, Pallas kernels for 21%

profile of v2, /device:TPU:0, one launch (start us, length us, event | category | flops | bytes accessed | tf_op | source)
XLA Modules:
  0.0 278.4 jit_solution(110657338524911490)
XLA Ops:
  14.8 5.9 %collective-permute-done.45.refs_2_ = bf16[512,256]{1,0:T(8,128)(2,1)S(1)} collective-permute-done((bf16[512,256]{1,0:T(8,128)(2,1)}, bf16[512,256]{1,0:T(8,128)(2,1)S(1)}, u32[]{:S(2)}, u32[]{:S(2)}) %collective-permute-start.45) | collective-permute-done | bytes 262176 | tf_op jit(solution)/shard_map/ppermute | solution.py:30
  20.8 4.2 %collective-permute-start.1 = (bf16[528,256]{1,0:T(8,128)(2,1)S(1)}, bf16[528,256]{1,0:T(8,128)(2,1)}, u32[]{:S(2)}, u32[]{:S(2)}) collective-permute-start(bf16[528,256]{1,0:T(8,128)(2,1)S(1)} %concatenate.6.refs_0_.refs_16_), channel_id=1, source_target_pairs={{0,96},{32,0},{64,32},{96,64},{1,97},{33,1},{65,33},{97,65},{2,98}... | collective-permute-start | bytes 811016 | tf_op jit(solution)/shard_map/ppermute | solution.py:30
  29.9 4.0 %collective-permute-start.17 = (bf16[2,512,256]{2,1,0:T(8,128)(2,1)}, bf16[2,512,256]{2,1,0:T(8,128)(2,1)S(1)}, u32[]{:S(2)}, u32[]{:S(2)}) collective-permute-start(bf16[2,512,256]{2,1,0:T(8,128)(2,1)} %pack_weights.1.refs_0_.refs_16_), channel_id=1, source_target_pairs={{0,4},{2,6},{4,0},{6,2},{1,5},{3,7},{5,1},{7,3},{8,12},{10,14},{12... | collective-permute-start | bytes 1572872 | tf_op jit(solution)/shard_map/ppermute | solution.py:30
  40.1 4.6 %collective-permute-done.17.refs_3_.refs_19_ = bf16[2,512,256]{2,1,0:T(8,128)(2,1)S(1)} collective-permute-done((bf16[2,512,256]{2,1,0:T(8,128)(2,1)}, bf16[2,512,256]{2,1,0:T(8,128)(2,1)S(1)}, u32[]{:S(2)}, u32[]{:S(2)}) %collective-permute-start.17) | collective-permute-done | bytes 524320 | tf_op jit(solution)/shard_map/ppermute | solution.py:30
  45.2 5.1 %collective-permute-done.15.refs_1_.refs_17_ = bf16[2,512,256]{2,1,0:T(8,128)(2,1)S(1)} collective-permute-done((bf16[2,512,256]{2,1,0:T(8,128)(2,1)}, bf16[2,512,256]{2,1,0:T(8,128)(2,1)S(1)}, u32[]{:S(2)}, u32[]{:S(2)}) %collective-permute-start.15) | collective-permute-done | bytes 524320 | tf_op jit(solution)/shard_map/ppermute | solution.py:30
  55.4 4.2 %collective-permute-done.5.refs_6_.refs_22_ = bf16[528,256]{1,0:T(8,128)(2,1)S(1)} collective-permute-done((bf16[528,256]{1,0:T(8,128)(2,1)S(1)}, bf16[528,256]{1,0:T(8,128)(2,1)S(1)}, u32[]{:S(2)}, u32[]{:S(2)}) %collective-permute-start.5) | collective-permute-done | bytes 270368 | tf_op jit(solution)/shard_map/ppermute | solution.py:30
  65.9 4.1 %collective-permute-start.50 = (bf16[512,256]{1,0:T(8,128)(2,1)}, bf16[512,256]{1,0:T(8,128)(2,1)}, u32[]{:S(2)}, u32[]{:S(2)}) collective-permute-start(bf16[512,256]{1,0:T(8,128)(2,1)} %copy-done.30), channel_id=1, source_target_pairs={{0,64},{32,96},{64,0},{96,32},{1,65},{33,97},{65,1},{97,33},{2,66}... | collective-permute-start | bytes 786440 | tf_op jit(solution)/shard_map/ppermute | solution.py:30
  70.0 5.7 %collective-permute-done.19.refs_5_.refs_21_ = bf16[2,512,256]{2,1,0:T(8,128)(2,1)S(1)} collective-permute-done((bf16[2,512,256]{2,1,0:T(8,128)(2,1)S(1)}, bf16[2,512,256]{2,1,0:T(8,128)(2,1)S(1)}, u32[]{:S(2)}, u32[]{:S(2)}) %collective-permute-start.19) | collective-permute-done | bytes 524320 | tf_op jit(solution)/shard_map/ppermute | solution.py:30
  82.7 6.1 %normalize.1 = (bf16[16,512,256]{2,1,0:T(8,128)(2,1)}, f32[512,1]{1,0:T(8,128)}) custom-call(s32[16]{0:T(128)} %stack.144.idx, bf16[528,256]{1,0:T(8,128)(2,1)} %copy-done.11, bf16[528,256]{1,0:T(8,128)(2,1)} %collective-permute-done.refs_1_.refs_17_, bf16[528,256]{1,0:T(8,128)(2,1)} %collective-permute-done.1.refs_2_.refs_18_, bf16[528,256]{1,0:T(8,128)(2,1)} %copy-done.13, ...), custom_call_target="tpu_custom_call" | custom-call | tf_op jit(solution)/shard_map/normalize/pallas_call | solution.py:111
  88.9 5.8 %project.1 = (bf16[512,128]{1,0:T(8,128)(2,1)}, bf16[512,256]{1,0:T(8,128)(2,1)}) custom-call(s32[8]{0:T(128)} %stack.153.idx.tok_idx, bf16[16,512,256]{2,1,0:T(8,128)(2,1)} %get-tuple-element.37.normed.n0.n1, bf16[2,512,256]{2,1,0:T(8,128)(2,1)} %pack_weights.1.refs_0_.refs_16_, bf16[2,512,256]{2,1,0:T(8,128)(2,1)} %copy-done.3, ...), custom_call_target="tpu_custom_call" | custom-call | tf_op jit(solution)/shard_map/project/pallas_call | solution.py:136
  101.7 4.1 %collective-permute-done.25.refs_4_ = bf16[512,256]{1,0:T(8,128)(2,1)S(1)} collective-permute-done((bf16[512,256]{1,0:T(8,128)(2,1)}, bf16[512,256]{1,0:T(8,128)(2,1)S(1)}, u32[]{:S(2)}, u32[]{:S(2)}) %collective-permute-start.25) | collective-permute-done | bytes 262176 | tf_op jit(solution)/shard_map/ppermute | solution.py:26
  105.9 3.2 %collective-permute-start.27 = (bf16[512,256]{1,0:T(8,128)(2,1)S(1)}, bf16[512,256]{1,0:T(8,128)(2,1)S(1)}, u32[]{:S(2)}, u32[]{:S(2)}) collective-permute-start(bf16[512,256]{1,0:T(8,128)(2,1)S(1)} %collective-permute-done.25.refs_4_), channel_id=1, source_target_pairs={{0,6},{2,0},{4,2},{6,4},{1,7},{3,1},{5,3},{7,5},{8,14},{10,8},{12,... | collective-permute-start | bytes 786440 | tf_op jit(solution)/shard_map/ppermute | solution.py:30
  111.0 6.7 %upstream.1 = (bf16[512,128]{1,0:T(8,128)(2,1)}, bf16[16,512,256]{2,1,0:T(8,128)(2,1)}, bf16[16,128,256]{2,1,0:T(8,128)(2,1)}) custom-call(s32[16]{0:T(128)} %stack.144.idx, s32[8]{0:T(128)} %stack.153.idx.tok_idx, bf16[512,256]{1,0:T(8,128)(2,1)} %refs_0_.1, bf16[512,256]{1,0:T(8,128)(2,1)} %copy-done.31, bf16[512,256]{1,0:T(8,128)(2,1)} %copy-done.32, ...), custom_call_target="tpu_custom_call" | custom-call | tf_op jit(solution)/shard_map/upstream/pallas_call | solution.py:186
  118.7 8.9 %forward.1 = (bf16[512,128]{1,0:T(8,128)(2,1)}, bf16[128,512]{1,0:T(8,128)(2,1)}, f32[1,512]{1,0:T(1,128)}, bf16[4096,256]{1,0:T(8,128)(2,1)}) custom-call(s32[8]{0:T(128)} %stack.153.idx.tok_idx, s32[1,512]{1,0:T(1,128)} %add_maximum_fusion.limit, bf16[512,128]{1,0:T(8,128)(2,1)} %get-tuple-element.38.q, bf16[512,256]{1,0:T(8,128)(2,1)} %get-tuple-element.39.refs_0_.kv, ...), custom_call_target="tpu_custom_call" | custom-call | tf_op jit(solution)/shard_map/forward/pallas_call | solution.py:250
  127.6 10.1 %backward.1 = (bf16[512,128]{1,0:T(8,128)(2,1)}, bf16[4096,256]{1,0:T(8,128)(2,1)}) custom-call(s32[1,512]{1,0:T(1,128)} %add_maximum_fusion.limit, f32[1,512]{1,0:T(1,128)} %get-tuple-element.42.lse, bf16[512,128]{1,0:T(8,128)(2,1)} %get-tuple-element.38.q, bf16[4096,256]{1,0:T(8,128)(2,1)} %get-tuple-element.43.kv, bf16[512,128]{1,0:T(8,128)(2,1)} %get-tuple-element.44.da, ...), custom_call_target="tpu_custom_call" | custom-call | tf_op jit(solution)/shard_map/backward/pallas_call | solution.py:280
  137.7 4.6 %all-to-all-start.1 = ((bf16[8,512,256]{2,1,0:T(8,128)(2,1)}), bf16[8,512,256]{2,1,0:T(8,128)(2,1)S(1)}, u32[]{:S(2)}, u32[]{:S(2)}) async-start(bf16[8,512,256]{2,1,0:T(8,128)(2,1)} %bitcast.48), calls=%async_computation.1 | async-start | bytes 4194304 | tf_op jit(solution)/shard_map/all_to_all | solution.py:51
  142.2 3.7 %order_weights.1 = (bf16[8,384,256]{2,1,0:T(8,128)(2,1)}, bf16[8,384,256]{2,1,0:T(8,128)(2,1)}) custom-call(s32[8]{0:T(128)} %stack.153.idx.tok_idx, s32[1]{0:T(128)} %bitcast.44.core, bf16[2,512,256]{2,1,0:T(8,128)(2,1)} %pack_weights.1.refs_0_.refs_16_, bf16[2,512,256]{2,1,0:T(8,128)(2,1)} %copy-done.3, bf16[2,512,256]{2,1,0:T(8,128)(2,1)} %copy-done.4, ...), custom_call_target="tpu_custom_call" | custom-call | tf_op jit(solution)/shard_map/order_weights/pallas_call | solution.py:156
  146.1 4.5 %collective-permute-start.29 = (bf16[512,128]{1,0:T(8,128)(2,1)}, bf16[512,128]{1,0:T(8,128)(2,1)S(1)}, u32[]{:S(2)}, u32[]{:S(2)}) collective-permute-start(bf16[512,128]{1,0:T(8,128)(2,1)} %get-tuple-element.40.refs_0_), channel_id=1, source_target_pairs={{0,32},{32,64},{64,96},{96,0},{1,33},{33,65},{65,97},{97,1},{2,34}... | collective-permute-start | bytes 393224 | tf_op jit(solution)/shard_map/ppermute | solution.py:30
  151.2 3.5 %weight_grad.1.w0.w1 = bf16[16,128,256]{2,1,0:T(8,128)(2,1)} custom-call(bf16[128,512]{1,0:T(8,128)(2,1)} %get-tuple-element.45.att_t.left, bf16[16,512,256]{2,1,0:T(8,128)(2,1)} %get-tuple-element.48.right), custom_call_target="tpu_custom_call" | custom-call | tf_op jit(solution)/shard_map/weight_grad/pallas_call | solution.py:426
  154.7 17.4 %all-to-all-done.1.dkv = bf16[8,512,256]{2,1,0:T(8,128)(2,1)S(1)} async-done(((bf16[8,512,256]{2,1,0:T(8,128)(2,1)}), bf16[8,512,256]{2,1,0:T(8,128)(2,1)S(1)}, u32[]{:S(2)}, u32[]{:S(2)}) %all-to-all-start.1) | async-done | bytes 2097184 | tf_op jit(solution)/shard_map/all_to_all | solution.py:51
  173.4 9.4 %gradients.1 = (bf16[512,384]{1,0:T(8,128)(2,1)}, f32[8,512]{1,0:T(8,128)}, bf16[2,2,512,256]{3,2,1,0:T(8,128)(2,1)}, bf16[2,2,512,256]{3,2,1,0:T(8,128)(2,1)}, ...) custom-call(s32[8]{0:T(128)} %stack.169.idx, ...), custom_call_target="tpu_custom_call" | custom-call | tf_op jit(solution)/shard_map/gradients/pallas_call | solution.py:363
  183.0 3.0 %collective-permute-start.67 = (bf16[2,2,512,256]{3,2,1,0:T(8,128)(2,1)}, bf16[2,2,512,256]{3,2,1,0:T(8,128)(2,1)S(1)}, u32[]{:S(2)}, u32[]{:S(2)}) collective-permute-start(bf16[2,2,512,256]{3,2,1,0:T(8,128)(2,1)} %get-tuple-element.63), channel_id=1, source_target_pairs={{0,6},{2,0},{4,2},{6,4},{1,7},{3,1},{5,3},{7,5},{8,14},{10,8},{12,... | collective-permute-start | bytes 3145736 | tf_op jit(solution)/shard_map/ppermute | solution.py:30
  186.0 5.9 %collective-permute-start.30 = (bf16[512,128]{1,0:T(8,128)(2,1)}, bf16[512,128]{1,0:T(8,128)(2,1)S(1)}, u32[]{:S(2)}, u32[]{:S(2)}) collective-permute-start(bf16[512,128]{1,0:T(8,128)(2,1)} %get-tuple-element.40.refs_0_), channel_id=1, source_target_pairs={{0,96},{32,0},{64,32},{96,64},{1,97},{33,1},{65,33},{97,65},{2,98}... | collective-permute-start | bytes 393224 | tf_op jit(solution)/shard_map/ppermute | solution.py:30
  192.2 4.0 %collective-permute-done.30.refs_2_ = bf16[512,128]{1,0:T(8,128)(2,1)S(1)} collective-permute-done((bf16[512,128]{1,0:T(8,128)(2,1)}, bf16[512,128]{1,0:T(8,128)(2,1)S(1)}, u32[]{:S(2)}, u32[]{:S(2)}) %collective-permute-start.30) | collective-permute-done | bytes 131104 | tf_op jit(solution)/shard_map/ppermute | solution.py:30
  200.4 4.6 %all-to-all-start = ((bf16[16,128,256]{2,1,0:T(8,128)(2,1)}), bf16[16,128,256]{2,1,0:T(8,128)(2,1)S(1)}, u32[]{:S(2)}, u32[]{:S(2)}) async-start(bf16[16,128,256]{2,1,0:T(8,128)(2,1)} %get-tuple-element.41), calls=%async_computation | async-start | bytes 2097152 | tf_op jit(solution)/shard_map/all_to_all | solution.py:51
  205.7 5.8 %input_grad.1 = (bf16[2,528,256]{2,1,0:T(8,128)(2,1)}, bf16[2,528,256]{2,1,0:T(8,128)(2,1)}, bf16[2,528,256]{2,1,0:T(8,128)(2,1)}, bf16[2,528,256]{2,1,0:T(8,128)(2,1)}) custom-call(s32[8]{0:T(128)} %stack.162.idx, bf16[512,384]{1,0:T(8,128)(2,1)} %get-tuple-element.49.g, bf16[512,384]{1,0:T(8,128)(2,1)} %copy-done.28, ...), custom_call_target="tpu_custom_call" | custom-call | tf_op jit(solution)/shard_map/input_grad/pallas_call | solution.py:410
  216.0 9.0 %collective-permute-start.64 = (bf16[2,528,256]{2,1,0:T(8,128)(2,1)}, bf16[2,528,256]{2,1,0:T(8,128)(2,1)}, u32[]{:S(2)}, u32[]{:S(2)}) collective-permute-start(bf16[2,528,256]{2,1,0:T(8,128)(2,1)} %get-tuple-element.56), channel_id=1, source_target_pairs={{0,96},{32,0},{64,32},{96,64},{1,97},{33,1},{65,33},{97,65},{2,98}... | collective-permute-start | bytes 1622024 | tf_op jit(solution)/shard_map/ppermute | solution.py:30
  230.0 16.1 %collective-permute-done.34.refs_6_ = bf16[512,128]{1,0:T(8,128)(2,1)} collective-permute-done((bf16[512,128]{1,0:T(8,128)(2,1)}, bf16[512,128]{1,0:T(8,128)(2,1)}, u32[]{:S(2)}, u32[]{:S(2)}) %collective-permute-start.34) | collective-permute-done | bytes 131104 | tf_op jit(solution)/shard_map/ppermute | solution.py:30
  247.0 3.6 %collective-permute-start.70 = (bf16[2,512,256]{2,1,0:T(8,128)(2,1)}, bf16[2,512,256]{2,1,0:T(8,128)(2,1)S(1)}, u32[]{:S(2)}, u32[]{:S(2)}) collective-permute-start(bf16[2,512,256]{2,1,0:T(8,128)(2,1)} %add_blocks.3), channel_id=1, source_target_pairs={{0,1},{1,0},{2,3},{3,2},{4,5},{5,4},{6,7},{7,6},{8,9},{9,8},{10,11... | collective-permute-start | bytes 1572872 | tf_op jit(solution)/shard_map/ppermute | solution.py:26
  251.4 3.1 %line_sum.1 = (f32[512,256]{1,0:T(8,128)}, f32[8,256]{1,0:T(8,128)}, bf16[528,256]{1,0:T(8,128)(2,1)}, f32[8,2,2,256]{3,2,1,0:T(2,128)}) custom-call(s32[1]{0:T(128)} %bitcast.28.side, bf16[2,528,256]{2,1,0:T(8,128)(2,1)} %get-tuple-element.53.refs_0_, bf16[2,528,256]{2,1,0:T(8,128)(2,1)} %copy-done.25, ...), custom_call_target="tpu_custom_call" | custom-call | tf_op jit(solution)/shard_map/line_sum/pallas_call | solution.py:462
  257.6 4.6 %all-to-all-start.2 = ((f32[16,2,256]{2,1,0:T(2,128)}), f32[16,2,256]{2,1,0:T(2,128)S(1)}, u32[]{:S(2)}, u32[]{:S(2)}) async-start(f32[16,2,256]{2,1,0:T(2,128)} %bitcast.49), calls=%async_computation.2 | async-start | bytes 65536 | tf_op jit(solution)/shard_map/all_to_all | solution.py:51
  263.6 4.7 %output.1 = bf16[512,256]{1,0:T(8,128)(2,1)} custom-call(s32[16]{0:T(128)} %stack.144.idx, bf16[512,128]{1,0:T(8,128)(2,1)} %get-tuple-element.40.refs_0_, bf16[512,128]{1,0:T(8,128)(2,1)} %copy-done.47, bf16[512,128]{1,0:T(8,128)(2,1)} %copy-done.49, bf16[512,128]{1,0:T(8,128)(2,1)} %copy-done.51, bf16[512,128]{1,0:T(8,128)(2,1)} %copy-done.45, ...), custom_call_target="tpu_custom_call" | custom-call | tf_op jit(solution)/shard_map/output/pallas_call | solution.py:509
  (269 shorter events, 86.9 us)
Async XLA Ops:
  3.9 16.9 %collective-permute-start.45 = (bf16[512,256]{1,0:T(8,128)(2,1)}, bf16[512,256]{1,0:T(8,128)(2,1)S(1)}, u32[]{:S(2)}, u32[]{:S(2)}) collective-permute-start(bf16[512,256]{1,0:T(8,128)(2,1)} %refs_0_.1), channel_id=1, source_target_pairs={{0,96},{32,0},{64,32},{96,64},{1,97},{33,1},{65,33},{97,65},{2,98}... | collective-permute-start | bytes 786440 | tf_op jit(solution)/shard_map/ppermute | solution.py:30
  9.3 20.6 %collective-permute-start.3 = (bf16[528,256]{1,0:T(8,128)(2,1)S(1)}, bf16[528,256]{1,0:T(8,128)(2,1)S(1)}, u32[]{:S(2)}, u32[]{:S(2)}) collective-permute-start(bf16[528,256]{1,0:T(8,128)(2,1)S(1)} %concatenate.6.refs_0_.refs_16_), channel_id=1, source_target_pairs={{0,16},{16,0},{1,17},{17,1},{2,18},{18,2},{3,19},{19,3},{4,20},{20... | collective-permute-start | bytes 811016 | tf_op jit(solution)/shard_map/ppermute | solution.py:26
  9.8 17.1 %collective-permute-start.51 = (bf16[512,256]{1,0:T(8,128)(2,1)}, bf16[512,256]{1,0:T(8,128)(2,1)S(1)}, u32[]{:S(2)}, u32[]{:S(2)}) collective-permute-start(bf16[512,256]{1,0:T(8,128)(2,1)} %refs_0_.1), channel_id=1, source_target_pairs={{0,8},{8,0},{1,9},{9,1},{2,10},{10,2},{3,11},{11,3},{4,12},{12,4},... | collective-permute-start | bytes 786440 | tf_op jit(solution)/shard_map/ppermute | solution.py:26
  12.0 21.9 %collective-permute-start.2 = (bf16[528,256]{1,0:T(8,128)(2,1)S(1)}, bf16[528,256]{1,0:T(8,128)(2,1)S(1)}, u32[]{:S(2)}, u32[]{:S(2)}) collective-permute-start(bf16[528,256]{1,0:T(8,128)(2,1)S(1)} %concatenate.6.refs_0_.refs_16_), channel_id=1, source_target_pairs={{0,64},{32,96},{64,0},{96,32},{1,65},{33,97},{65,1},{97,33},{2,66}... | collective-permute-start | bytes 811016 | tf_op jit(solution)/shard_map/ppermute | solution.py:30
  20.8 16.4 %collective-permute-start.1 = (bf16[528,256]{1,0:T(8,128)(2,1)S(1)}, bf16[528,256]{1,0:T(8,128)(2,1)}, u32[]{:S(2)}, u32[]{:S(2)}) collective-permute-start(bf16[528,256]{1,0:T(8,128)(2,1)S(1)} %concatenate.6.refs_0_.refs_16_), channel_id=1, source_target_pairs={{0,96},{32,0},{64,32},{96,64},{1,97},{33,1},{65,33},{97,65},{2,98}... | collective-permute-start | bytes 811016 | tf_op jit(solution)/shard_map/ppermute | solution.py:30
  33.9 16.4 %collective-permute-start.15 = (bf16[2,512,256]{2,1,0:T(8,128)(2,1)}, bf16[2,512,256]{2,1,0:T(8,128)(2,1)S(1)}, u32[]{:S(2)}, u32[]{:S(2)}) collective-permute-start(bf16[2,512,256]{2,1,0:T(8,128)(2,1)} %pack_weights.1.refs_0_.refs_16_), channel_id=1, source_target_pairs={{0,2},{2,4},{4,6},{6,0},{1,3},{3,5},{5,7},{7,1},{8,10},{10,12},{12... | collective-permute-start | bytes 1572872 | tf_op jit(solution)/shard_map/ppermute | solution.py:30
  34.9 16.1 %collective-permute-start.16 = (bf16[2,512,256]{2,1,0:T(8,128)(2,1)}, bf16[2,512,256]{2,1,0:T(8,128)(2,1)S(1)}, u32[]{:S(2)}, u32[]{:S(2)}) collective-permute-start(bf16[2,512,256]{2,1,0:T(8,128)(2,1)} %pack_weights.1.refs_0_.refs_16_), channel_id=1, source_target_pairs={{0,6},{2,0},{4,2},{6,4},{1,7},{3,1},{5,3},{7,5},{8,14},{10,8},{12,... | collective-permute-start | bytes 1572872 | tf_op jit(solution)/shard_map/ppermute | solution.py:30
  38.7 16.6 %collective-permute-start.4 = (bf16[528,256]{1,0:T(8,128)(2,1)S(1)}, bf16[528,256]{1,0:T(8,128)(2,1)S(1)}, u32[]{:S(2)}, u32[]{:S(2)}) collective-permute-start(bf16[528,256]{1,0:T(8,128)(2,1)S(1)} %collective-permute-done.3.refs_4_.refs_20_.refs_5_), channel_id=1, source_target_pairs={{0,32},{32,64},{64,96},{96,0},{1,33},{33,65},{65,97},{97,1},{2,34}... | collective-permute-start | bytes 811016 | tf_op jit(solution)/shard_map/ppermute | solution.py:30
  38.7 16.1 %collective-permute-start.48 = (bf16[512,256]{1,0:T(8,128)(2,1)S(1)}, bf16[512,256]{1,0:T(8,128)(2,1)}, u32[]{:S(2)}, u32[]{:S(2)}) collective-permute-start(bf16[512,256]{1,0:T(8,128)(2,1)S(1)} %collective-permute-done.47.refs_4_), channel_id=1, source_target_pairs={{0,32},{32,64},{64,96},{96,0},{1,33},{33,65},{65,97},{97,1},{2,34}... | collective-permute-start | bytes 786440 | tf_op jit(solution)/shard_map/ppermute | solution.py:30
  65.9 28.8 %collective-permute-start.50 = (bf16[512,256]{1,0:T(8,128)(2,1)}, bf16[512,256]{1,0:T(8,128)(2,1)}, u32[]{:S(2)}, u32[]{:S(2)}) collective-permute-start(bf16[512,256]{1,0:T(8,128)(2,1)} %copy-done.30), channel_id=1, source_target_pairs={{0,64},{32,96},{64,0},{96,32},{1,65},{33,97},{65,1},{97,33},{2,66}... | collective-permute-start | bytes 786440 | tf_op jit(solution)/shard_map/ppermute | solution.py:30
  70.0 25.3 %collective-permute-start.55 = (bf16[512,256]{1,0:T(8,128)(2,1)}, bf16[512,256]{1,0:T(8,128)(2,1)}, u32[]{:S(2)}, u32[]{:S(2)}) collective-permute-start(bf16[512,256]{1,0:T(8,128)(2,1)} %copy-done.30), channel_id=1, source_target_pairs={{0,8},{8,0},{1,9},{9,1},{2,10},{10,2},{3,11},{11,3},{4,12},{12,4},... | collective-permute-start | bytes 786440 | tf_op jit(solution)/shard_map/ppermute | solution.py:26
  75.6 19.8 %collective-permute-start.52 = (bf16[512,256]{1,0:T(8,128)(2,1)}, bf16[512,256]{1,0:T(8,128)(2,1)}, u32[]{:S(2)}, u32[]{:S(2)}) collective-permute-start(bf16[512,256]{1,0:T(8,128)(2,1)} %copy-done.31), channel_id=1, source_target_pairs={{0,8},{8,0},{1,9},{9,1},{2,10},{10,2},{3,11},{11,3},{4,12},{12,4},... | collective-permute-start | bytes 786440 | tf_op jit(solution)/shard_map/ppermute | solution.py:26
  75.7 20.1 %collective-permute-start.53 = (bf16[512,256]{1,0:T(8,128)(2,1)}, bf16[512,256]{1,0:T(8,128)(2,1)}, u32[]{:S(2)}, u32[]{:S(2)}) collective-permute-start(bf16[512,256]{1,0:T(8,128)(2,1)} %copy-done.32), channel_id=1, source_target_pairs={{0,8},{8,0},{1,9},{9,1},{2,10},{10,2},{3,11},{11,3},{4,12},{12,4},... | collective-permute-start | bytes 786440 | tf_op jit(solution)/shard_map/ppermute | solution.py:26
  79.5 17.4 %collective-permute-start.54 = (bf16[512,256]{1,0:T(8,128)(2,1)}, bf16[512,256]{1,0:T(8,128)(2,1)}, u32[]{:S(2)}, u32[]{:S(2)}) collective-permute-start(bf16[512,256]{1,0:T(8,128)(2,1)} %copy-done.33), channel_id=1, source_target_pairs={{0,8},{8,0},{1,9},{9,1},{2,10},{10,2},{3,11},{11,3},{4,12},{12,4},... | collective-permute-start | bytes 786440 | tf_op jit(solution)/shard_map/ppermute | solution.py:26
  98.4 19.3 %collective-permute-start.22 = (bf16[512,256]{1,0:T(8,128)(2,1)}, bf16[512,256]{1,0:T(8,128)(2,1)S(1)}, u32[]{:S(2)}, u32[]{:S(2)}) collective-permute-start(bf16[512,256]{1,0:T(8,128)(2,1)} %get-tuple-element.39.refs_0_.kv), channel_id=1, source_target_pairs={{0,2},{2,4},{4,6},{6,0},{1,3},{3,5},{5,7},{7,1},{8,10},{10,12},{12... | collective-permute-start | bytes 786440 | tf_op jit(solution)/shard_map/ppermute | solution.py:30
  99.5 18.2 %collective-permute-start.23 = (bf16[512,256]{1,0:T(8,128)(2,1)}, bf16[512,256]{1,0:T(8,128)(2,1)S(1)}, u32[]{:S(2)}, u32[]{:S(2)}) collective-permute-start(bf16[512,256]{1,0:T(8,128)(2,1)} %get-tuple-element.39.refs_0_.kv), channel_id=1, source_target_pairs={{0,6},{2,0},{4,2},{6,4},{1,7},{3,1},{5,3},{7,5},{8,14},{10,8},{12,... | collective-permute-start | bytes 786440 | tf_op jit(solution)/shard_map/ppermute | solution.py:30
  137.7 34.4 %all-to-all-start.1 = ((bf16[8,512,256]{2,1,0:T(8,128)(2,1)}), bf16[8,512,256]{2,1,0:T(8,128)(2,1)S(1)}, u32[]{:S(2)}, u32[]{:S(2)}) async-start(bf16[8,512,256]{2,1,0:T(8,128)(2,1)} %bitcast.48), calls=%async_computation.1 | async-start | bytes 4194304 | tf_op jit(solution)/shard_map/all_to_all | solution.py:51
  145.9 52.7 %collective-permute-start.60 = (bf16[8,384,256]{2,1,0:T(8,128)(2,1)}, bf16[8,384,256]{2,1,0:T(8,128)(2,1)}, u32[]{:S(2)}, u32[]{:S(2)}) collective-permute-start(bf16[8,384,256]{2,1,0:T(8,128)(2,1)} %get-tuple-element.51), channel_id=1, source_target_pairs={{0,8},{8,0},{1,9},{9,1},{2,10},{10,2},{3,11},{11,3},{4,12},{12,4},... | collective-permute-start | bytes 4718600 | tf_op jit(solution)/shard_map/ppermute | solution.py:26
  145.9 40.1 %collective-permute-start.32 = (bf16[512,128]{1,0:T(8,128)(2,1)}, bf16[512,128]{1,0:T(8,128)(2,1)S(1)}, u32[]{:S(2)}, u32[]{:S(2)}) collective-permute-start(bf16[512,128]{1,0:T(8,128)(2,1)} %get-tuple-element.40.refs_0_), channel_id=1, source_target_pairs={{0,16},{16,0},{1,17},{17,1},{2,18},{18,2},{3,19},{19,3},{4,20},{20... | collective-permute-start | bytes 393224 | tf_op jit(solution)/shard_map/ppermute | solution.py:26
  146.1 45.9 %collective-permute-start.29 = (bf16[512,128]{1,0:T(8,128)(2,1)}, bf16[512,128]{1,0:T(8,128)(2,1)S(1)}, u32[]{:S(2)}, u32[]{:S(2)}) collective-permute-start(bf16[512,128]{1,0:T(8,128)(2,1)} %get-tuple-element.40.refs_0_), channel_id=1, source_target_pairs={{0,32},{32,64},{64,96},{96,0},{1,33},{33,65},{65,97},{97,1},{2,34}... | collective-permute-start | bytes 393224 | tf_op jit(solution)/shard_map/ppermute | solution.py:30
  182.8 42.2 %collective-permute-start.66 = (bf16[2,2,512,256]{3,2,1,0:T(8,128)(2,1)}, bf16[2,2,512,256]{3,2,1,0:T(8,128)(2,1)S(1)}, u32[]{:S(2)}, u32[]{:S(2)}) collective-permute-start(bf16[2,2,512,256]{3,2,1,0:T(8,128)(2,1)} %get-tuple-element.62), channel_id=1, source_target_pairs={{0,2},{2,4},{4,6},{6,0},{1,3},{3,5},{5,7},{7,1},{8,10},{10,12},{12... | collective-permute-start | bytes 3145736 | tf_op jit(solution)/shard_map/ppermute | solution.py:30
  183.0 42.0 %collective-permute-start.67 = (bf16[2,2,512,256]{3,2,1,0:T(8,128)(2,1)}, bf16[2,2,512,256]{3,2,1,0:T(8,128)(2,1)S(1)}, u32[]{:S(2)}, u32[]{:S(2)}) collective-permute-start(bf16[2,2,512,256]{3,2,1,0:T(8,128)(2,1)} %get-tuple-element.63), channel_id=1, source_target_pairs={{0,6},{2,0},{4,2},{6,4},{1,7},{3,1},{5,3},{7,5},{8,14},{10,8},{12,... | collective-permute-start | bytes 3145736 | tf_op jit(solution)/shard_map/ppermute | solution.py:30
  198.6 17.4 %collective-permute-start.68 = (bf16[2,512,256]{2,1,0:T(8,128)(2,1)}, bf16[2,512,256]{2,1,0:T(8,128)(2,1)}, u32[]{:S(2)}, u32[]{:S(2)}) collective-permute-start(bf16[2,512,256]{2,1,0:T(8,128)(2,1)} %get-tuple-element.65), channel_id=1, source_target_pairs={{0,1},{1,0},{2,3},{3,2},{4,5},{5,4},{6,7},{7,6},{8,9},{9,8},{10,11... | collective-permute-start | bytes 1572872 | tf_op jit(solution)/shard_map/ppermute | solution.py:26
  200.4 57.3 %all-to-all-start = ((bf16[16,128,256]{2,1,0:T(8,128)(2,1)}), bf16[16,128,256]{2,1,0:T(8,128)(2,1)S(1)}, u32[]{:S(2)}, u32[]{:S(2)}) async-start(bf16[16,128,256]{2,1,0:T(8,128)(2,1)} %get-tuple-element.41), calls=%async_computation | async-start | bytes 2097152 | tf_op jit(solution)/shard_map/all_to_all | solution.py:51
  211.4 39.2 %collective-permute-start.62 = (bf16[2,528,256]{2,1,0:T(8,128)(2,1)}, bf16[2,528,256]{2,1,0:T(8,128)(2,1)S(1)}, u32[]{:S(2)}, u32[]{:S(2)}) collective-permute-start(bf16[2,528,256]{2,1,0:T(8,128)(2,1)} %get-tuple-element.54), channel_id=1, source_target_pairs={{0,32},{32,64},{64,96},{96,0},{1,33},{33,65},{65,97},{97,1},{2,34}... | collective-permute-start | bytes 1622024 | tf_op jit(solution)/shard_map/ppermute | solution.py:30
  213.3 37.4 %collective-permute-start.63 = (bf16[2,528,256]{2,1,0:T(8,128)(2,1)}, bf16[2,528,256]{2,1,0:T(8,128)(2,1)}, u32[]{:S(2)}, u32[]{:S(2)}) collective-permute-start(bf16[2,528,256]{2,1,0:T(8,128)(2,1)} %get-tuple-element.55), channel_id=1, source_target_pairs={{0,64},{32,96},{64,0},{96,32},{1,65},{33,97},{65,1},{97,33},{2,66}... | collective-permute-start | bytes 1622024 | tf_op jit(solution)/shard_map/ppermute | solution.py:30
  216.0 35.2 %collective-permute-start.64 = (bf16[2,528,256]{2,1,0:T(8,128)(2,1)}, bf16[2,528,256]{2,1,0:T(8,128)(2,1)}, u32[]{:S(2)}, u32[]{:S(2)}) collective-permute-start(bf16[2,528,256]{2,1,0:T(8,128)(2,1)} %get-tuple-element.56), channel_id=1, source_target_pairs={{0,96},{32,0},{64,32},{96,64},{1,97},{33,1},{65,33},{97,65},{2,98}... | collective-permute-start | bytes 1622024 | tf_op jit(solution)/shard_map/ppermute | solution.py:30
  225.0 21.1 %collective-permute-start.34 = (bf16[512,128]{1,0:T(8,128)(2,1)}, bf16[512,128]{1,0:T(8,128)(2,1)}, u32[]{:S(2)}, u32[]{:S(2)}) collective-permute-start(bf16[512,128]{1,0:T(8,128)(2,1)} %copy-done.45), channel_id=1, source_target_pairs={{0,96},{32,0},{64,32},{96,64},{1,97},{33,1},{65,33},{97,65},{2,98}... | collective-permute-start | bytes 393224 | tf_op jit(solution)/shard_map/ppermute | solution.py:30
  225.0 21.9 %collective-permute-start.35 = (bf16[512,128]{1,0:T(8,128)(2,1)}, bf16[512,128]{1,0:T(8,128)(2,1)}, u32[]{:S(2)}, u32[]{:S(2)}) collective-permute-start(bf16[512,128]{1,0:T(8,128)(2,1)} %copy-done.45), channel_id=1, source_target_pairs={{0,64},{32,96},{64,0},{96,32},{1,65},{33,97},{65,1},{97,33},{2,66}... | collective-permute-start | bytes 393224 | tf_op jit(solution)/shard_map/ppermute | solution.py:30
  246.1 28.0 %collective-permute-start.69 = (bf16[2,512,256]{2,1,0:T(8,128)(2,1)}, bf16[2,512,256]{2,1,0:T(8,128)(2,1)S(1)}, u32[]{:S(2)}, u32[]{:S(2)}) collective-permute-start(bf16[2,512,256]{2,1,0:T(8,128)(2,1)} %add_blocks.2), channel_id=1, source_target_pairs={{0,4},{2,6},{4,0},{6,2},{1,5},{3,7},{5,1},{7,3},{8,12},{10,14},{12... | collective-permute-start | bytes 1572872 | tf_op jit(solution)/shard_map/ppermute | solution.py:30
  247.0 27.1 %collective-permute-start.70 = (bf16[2,512,256]{2,1,0:T(8,128)(2,1)}, bf16[2,512,256]{2,1,0:T(8,128)(2,1)S(1)}, u32[]{:S(2)}, u32[]{:S(2)}) collective-permute-start(bf16[2,512,256]{2,1,0:T(8,128)(2,1)} %add_blocks.3), channel_id=1, source_target_pairs={{0,1},{1,0},{2,3},{3,2},{4,5},{5,4},{6,7},{7,6},{8,9},{9,8},{10,11... | collective-permute-start | bytes 1572872 | tf_op jit(solution)/shard_map/ppermute | solution.py:26
  254.5 16.4 %collective-permute-start.65 = (bf16[528,256]{1,0:T(8,128)(2,1)}, bf16[528,256]{1,0:T(8,128)(2,1)S(1)}, u32[]{:S(2)}, u32[]{:S(2)}) collective-permute-start(bf16[528,256]{1,0:T(8,128)(2,1)} %get-tuple-element.60), channel_id=1, source_target_pairs={{0,16},{16,0},{1,17},{17,1},{2,18},{18,2},{3,19},{19,3},{4,20},{20... | collective-permute-start | bytes 811016 | tf_op jit(solution)/shard_map/ppermute | solution.py:26
  (104 other events, 1227.3 us)

commit v3 on v2

--- a/solution.py
+++ b/solution.py
@@ -35,7 +35,9 @@
 
 
 def spread(block):
-    row = turns(block) + turns(swap(block, "h"))
+    other = swap(block, "h")
+    pair = jnp.stack([block, other])
+    row = turns(pair)
     return row + [swap(a, "c") for a in row]
 
 
@@ -87,21 +89,22 @@
 
 
 def normalize_kernel(idx, *refs):
-    xs, gains = refs[:16], refs[16:32]
-    mod, normed, inv_out = refs[32:]
+    xs, gains = refs[:8], refs[8:16]
+    mod, normed, inv_out = refs[16:]
     rows = mod.shape[0]
     squares = jnp.zeros((rows, 256), F32)
     for a in xs:
-        xb = a[...].astype(F32)
-        squares = squares + xb * xb
+        for s in range(2):
+            xb = a[s].astype(F32)
+            squares = squares + xb * xb
     inv = lax.rsqrt(jnp.sum(squares, axis=1, keepdims=True) / 4096 + epsilon)
     inv_out[...] = inv
     second = mod[...] == 1
     for n in range(16):
-        g = gains[n][...].astype(F32)
+        g = gains[n // 2][n % 2].astype(F32)
         g0 = (g[0:1] + g[2:3]) + g[4:5]
         g1 = (g[1:2] + g[3:4]) + g[5:6]
-        scaled = xs[n][...].astype(F32) * inv
+        scaled = xs[n // 2][n % 2].astype(F32) * inv
         normed[idx[n]] = (scaled * jnp.where(second, g1, g0)).astype(BF16)
 
 
@@ -112,7 +115,10 @@
         normalize_kernel,
         name="normalize",
         grid=(512 // tile,),
-        in_specs=[SMEM] + [rows(256)] * 16 + [pl.BlockSpec((16, 256), lambda i: (32, 0))] * 16 + [rows(1)],
+        in_specs=[SMEM]
+        + [pl.BlockSpec((2, tile, 256), lambda i: (0, i, 0))] * 8
+        + [pl.BlockSpec((2, 16, 256), lambda i: (0, 32, 0))] * 8
+        + [rows(1)],
         out_specs=[pl.BlockSpec((16, tile, 256), lambda i: (0, i, 0)), rows(1)],
         out_shape=[shape((16, 512, 256)), shape((512, 1), F32)],
         compiler_params=PARAMS,
@@ -165,7 +171,7 @@
 
 
 def upstream_kernel(idx, tok_idx, *refs):
-    gs, ws, (out, ordered, wo) = refs[:16], refs[16:24], refs[24:]
+    gs, ws, (out, ordered, wo) = refs[:8], refs[8:16], refs[16:]
 
     @pl.when(pl.program_id(0) == 0)
     def _():
@@ -175,7 +181,7 @@
 
     acc = jnp.zeros(out.shape, F32)
     for n in range(16):
-        g = gs[n][...]
+        g = gs[n // 2][n % 2]
         ordered[idx[n]] = g
         acc = acc + dot(g, wo[idx[n]], NT)
     out[...] = acc.astype(BF16)
@@ -188,7 +194,7 @@
         name="upstream",
         grid=(512 // tile,),
         in_specs=[SMEM, SMEM]
-        + [pl.BlockSpec((tile, 256), lambda i: (i, 0))] * 16
+        + [pl.BlockSpec((2, tile, 256), lambda i: (0, i, 0))] * 8
         + [pl.BlockSpec((2, 128, 256), lambda i: (0, 3, 0))] * 8,
         out_specs=[
             pl.BlockSpec((tile, 128), lambda i: (i, 0)),
@@ -458,6 +464,9 @@
             gains[k, at, 1:2] = other
 
 
+NEXT = pl.BlockSpec((None, 512, 256), lambda i: (1, 0, 0))
+
+
 def line_sum(side, terms, x, x_next, inv, modality):
     return pl.pallas_call(
         line_kernel,
@@ -465,7 +474,7 @@
         grid=(1,),
         in_specs=[SMEM]
         + [fixed(2, 528, 256)] * 4
-        + [fixed(512, 256), fixed(512, 256), fixed(512, 1), fixed(512, 1)],
+        + [fixed(512, 256), NEXT, fixed(512, 1), fixed(512, 1)],
         out_specs=[fixed(512, 256), fixed(8, 256), fixed(528, 256), fixed(8, 2, 2, 256)],
         out_shape=[
             shape((512, 256), F32),
@@ -497,10 +506,10 @@
 
 
 def output_kernel(idx, *refs):
-    atts, (rows, out) = refs[:16], refs[16:]
+    atts, (rows, out) = refs[:8], refs[8:]
     total = jnp.zeros(out.shape, F32)
     for n in range(16):
-        total = total + dot(atts[n][...], rows[idx[n]]).astype(BF16).astype(F32)
+        total = total + dot(atts[n // 2][n % 2], rows[idx[n]]).astype(BF16).astype(F32)
     out[...] = total.astype(BF16)
 
 
@@ -511,7 +520,7 @@
         name="output",
         grid=(512 // tile,),
         in_specs=[SMEM]
-        + [pl.BlockSpec((tile, 128), lambda i: (i, 0))] * 16
+        + [pl.BlockSpec((2, tile, 128), lambda i: (0, i, 0))] * 8
         + [fixed(16, 128, 256)],
         out_specs=pl.BlockSpec((tile, 256), lambda i: (i, 0)),
         out_shape=shape((512, 256)),
@@ -552,7 +561,7 @@
 def sublayer(layer_input, modality, image_spans, norm_gain, w_qkv, w_out, grad_out):
     x, h, c = (lax.axis_index(a) for a in GROUP)
     z, u = (lax.axis_index(a) for a in TOKENS_AXES)
-    blocks = [((x - d) % 4, h ^ s, c ^ k) for k in range(2) for s in range(2) for d in TURNS]
+    blocks = [((x - d) % 4, h ^ s, c ^ k) for k in range(2) for d in TURNS for s in range(2)]
     idx = jnp.stack([a * 4 + b * 2 + e for a, b, e in blocks]).astype(jnp.int32)
     tok_idx = jnp.stack([((z - d) % 4) * 2 + (u ^ s) for s in range(2) for d in TURNS]).astype(jnp.int32)
     places = jnp.stack([((x + d) % 4) * 2 + (h ^ s) for d in range(4) for s in range(2)]).astype(jnp.int32)
@@ -597,7 +606,7 @@
     g2, dots2 = swap(g, "c"), swap(dots, "c")
     terms = input_grad(places, g, g2, w_kept, w_other, dots, dots2)
     terms = [turn(t, d) if d else t for d, t in enumerate(terms)]
-    own, own_dots, sent, gains = line_sum(side, terms, layer_input, xs[4], inv, column)
+    own, own_dots, sent, gains = line_sum(side, terms, layer_input, xs[0], inv, column)
     last = swap(sent, "h")
     gains = exchange(gains.reshape(16, 2, 256), ("z", "u", "h"))
     grad_in = finish(own, own_dots, last, layer_input, inv, column, norm_gain)

time: 280 us -> 276 us (0.986)
  starting transfers between devices: 98.2 us -> 76.1 us
  waiting for transfers between devices: 85 us -> 100 us
    ppermute x34 -> x25, starting transfers between devices: 66.5 us -> 44.2 us  [turn(): return lax.ppermute(a, axis, [(i, (i + d) % 4) for i in range(4)])]
    ppermute x34 -> x25, waiting for transfers between devices: 53.8 us -> 62.5 us  [turn(): return lax.ppermute(a, axis, [(i, (i + d) % 4) for i in range(4)])]
    ppermute x37 -> x25, waiting for transfers between devices: 11.8 us -> 15.9 us  [swap(): return lax.ppermute(a, axis, [(0, 1), (1, 0)])]
    unnamed x124 -> x82, local copies, waits for them, and re-layouts: 6.82 us -> 8.74 us
    ppermute x37 -> x25, starting transfers between devices: 17.9 us -> 18.8 us  [swap(): return lax.ppermute(a, axis, [(0, 1), (1, 0)])]
  transfers between devices with their start and end apart: 74 -> 53, of which waited for: 23 -> 18; matrix products, arithmetic and copies ran while one was open for 3% -> 3% of each run, Pallas kernels for 21% -> 20%
where the time goes in v3:
time: 276 us; the launch traced here: 274 us
  waiting for transfers between devices  100 us (36%)
  Pallas kernels  79 us (29%)
  starting transfers between devices  76.1 us (28%)
  local copies, waits for them, and re-layouts  13.4 us (5%)
  other arithmetic  3.85 us (1%)
    ppermute x25, waiting for transfers between devices, turn(): return lax.ppermute(a, axis, [(i, (i + d) % 4) for i in range(4)])  62.5 us
    ppermute x25, starting transfers between devices, turn(): return lax.ppermute(a, axis, [(i, (i + d) % 4) for i in range(4)])  44.2 us
    all_to_all x3, waiting for transfers between devices, exchange(): return lax.all_to_all(blocks, axis, 0, 0, tiled=True)  21.9 us
    ppermute x25, starting transfers between devices, swap(): return lax.ppermute(a, axis, [(0, 1), (1, 0)])  18.8 us
    ppermute x25, waiting for transfers between devices, swap(): return lax.ppermute(a, axis, [(0, 1), (1, 0)])  15.9 us
    all_to_all x3, starting transfers between devices, exchange(): return lax.all_to_all(blocks, axis, 0, 0, tiled=True)  13.2 us
    pallas_call x1, Pallas kernels, backward(): pl.pallas_call(backward_kernel, name='backward', out_shape=[shape((512, 1...  10.1 us
    pallas_call x1, Pallas kernels, gradients(): pl.pallas_call(gradients_kernel, name='gradients', grid_spec=spec, out_sh...  9.5 us
  transfers between devices with their start and end apart: 53, of which 18 were waited for; matrix products, arithmetic and copies ran while one was open for 3% of the time, Pallas kernels for 20%

profile of v3, /device:TPU:0, one launch (start us, length us, event | category | flops | bytes accessed | tf_op | source)
XLA Modules:
  0.0 273.7 jit_solution(13310950536463854592)
XLA Ops:
  2.6 3.3 %collective-permute-start.11 = (bf16[2,512,256]{2,1,0:T(8,128)(2,1)}, bf16[2,512,256]{2,1,0:T(8,128)(2,1)S(1)}, u32[]{:S(2)}, u32[]{:S(2)}) collective-permute-start(bf16[2,512,256]{2,1,0:T(8,128)(2,1)} %pack_weights.1.refs_0_.refs_8_), channel_id=1, source_target_pairs={{0,1},{1,0},{2,3},{3,2},{4,5},{5,4},{6,7},{7,6},{8,9},{9,8},{10,11... | collective-permute-start | bytes 1572872 | tf_op jit(solution)/shard_map/ppermute | solution.py:26
  5.9 3.9 %collective-permute-start.10 = (bf16[2,512,256]{2,1,0:T(8,128)(2,1)}, bf16[2,512,256]{2,1,0:T(8,128)(2,1)S(1)}, u32[]{:S(2)}, u32[]{:S(2)}) collective-permute-start(bf16[2,512,256]{2,1,0:T(8,128)(2,1)} %pack_weights.1.refs_0_.refs_8_), channel_id=1, source_target_pairs={{0,4},{2,6},{4,0},{6,2},{1,5},{3,7},{5,1},{7,3},{8,12},{10,14},{12... | collective-permute-start | bytes 1572872 | tf_op jit(solution)/shard_map/ppermute | solution.py:30
  14.7 10.4 %collective-permute-done.30 = bf16[512,256]{1,0:T(8,128)(2,1)S(1)} collective-permute-done((bf16[512,256]{1,0:T(8,128)(2,1)}, bf16[512,256]{1,0:T(8,128)(2,1)S(1)}, u32[]{:S(2)}, u32[]{:S(2)}) %collective-permute-start.30) | collective-permute-done | bytes 262176 | tf_op jit(solution)/shard_map/ppermute | solution.py:26
  25.2 4.0 %collective-permute-start.9 = (bf16[2,512,256]{2,1,0:T(8,128)(2,1)}, bf16[2,512,256]{2,1,0:T(8,128)(2,1)S(1)}, u32[]{:S(2)}, u32[]{:S(2)}) collective-permute-start(bf16[2,512,256]{2,1,0:T(8,128)(2,1)} %pack_weights.1.refs_0_.refs_8_), channel_id=1, source_target_pairs={{0,6},{2,0},{4,2},{6,4},{1,7},{3,1},{5,3},{7,5},{8,14},{10,8},{12,... | collective-permute-start | bytes 1572872 | tf_op jit(solution)/shard_map/ppermute | solution.py:30
  34.7 2.7 collective-permute-start.33
  38.7 2.8 %collective-permute-start.2 = (bf16[2,528,256]{2,1,0:T(8,128)(2,1)S(1)}, bf16[2,528,256]{2,1,0:T(8,128)(2,1)S(1)}, u32[]{:S(2)}, u32[]{:S(2)}) collective-permute-start(bf16[2,528,256]{2,1,0:T(8,128)(2,1)S(1)} %pad_maximum_fusion.refs_0_.refs_8_.refs_5_), channel_id=1, source_target_pairs={{0,96},{32,0},{64,32},{96,64},{1,97},{33,1},{65,33},{97,65},{2,98}... | collective-permute-start | bytes 1622024 | tf_op jit(solution)/shard_map/ppermute | solution.py:30
  41.5 5.7 %collective-permute-done.31.refs_1_ = bf16[2,512,256]{2,1,0:T(8,128)(2,1)S(1)} collective-permute-done((bf16[2,512,256]{2,1,0:T(8,128)(2,1)}, bf16[2,512,256]{2,1,0:T(8,128)(2,1)S(1)}, u32[]{:S(2)}, u32[]{:S(2)}) %collective-permute-start.31) | collective-permute-done | bytes 524320 | tf_op jit(solution)/shard_map/ppermute | solution.py:30
  49.1 8.8 %collective-permute-done.32.refs_2_ = bf16[2,512,256]{2,1,0:T(8,128)(2,1)} collective-permute-done((bf16[2,512,256]{2,1,0:T(8,128)(2,1)}, bf16[2,512,256]{2,1,0:T(8,128)(2,1)}, u32[]{:S(2)}, u32[]{:S(2)}) %collective-permute-start.32) | collective-permute-done | bytes 524320 | tf_op jit(solution)/shard_map/ppermute | solution.py:30
  57.9 13.3 %collective-permute-done.33.refs_3_ = bf16[2,512,256]{2,1,0:T(8,128)(2,1)} collective-permute-done((bf16[2,512,256]{2,1,0:T(8,128)(2,1)}, bf16[2,512,256]{2,1,0:T(8,128)(2,1)}, u32[]{:S(2)}, u32[]{:S(2)}) %collective-permute-start.33) | collective-permute-done | bytes 524320 | tf_op jit(solution)/shard_map/ppermute | solution.py:30
  74.4 5.1 %collective-permute-done.3.refs_3_.refs_11_ = bf16[2,528,256]{2,1,0:T(8,128)(2,1)S(1)} collective-permute-done((bf16[2,528,256]{2,1,0:T(8,128)(2,1)S(1)}, bf16[2,528,256]{2,1,0:T(8,128)(2,1)S(1)}, u32[]{:S(2)}, u32[]{:S(2)}) %collective-permute-start.3) | collective-permute-done | bytes 540704 | tf_op jit(solution)/shard_map/ppermute | solution.py:30
  88.5 6.1 %normalize.1 = (bf16[16,512,256]{2,1,0:T(8,128)(2,1)}, f32[512,1]{1,0:T(8,128)}) custom-call(s32[16]{0:T(128)} %stack.171.idx, bf16[2,528,256]{2,1,0:T(8,128)(2,1)} %copy-done, bf16[2,528,256]{2,1,0:T(8,128)(2,1)} %copy-done.11, bf16[2,528,256]{2,1,0:T(8,128)(2,1)} %copy-done.12, bf16[2,528,256]{2,1,0:T(8,128)(2,1)} %copy-done.13, ...), custom_call_target="tpu_custom_call" | custom-call | tf_op jit(solution)/shard_map/normalize/pallas_call | solution.py:114
  95.5 5.8 %project.1 = (bf16[512,128]{1,0:T(8,128)(2,1)}, bf16[512,256]{1,0:T(8,128)(2,1)}) custom-call(s32[8]{0:T(128)} %stack.180.idx.tok_idx, bf16[16,512,256]{2,1,0:T(8,128)(2,1)} %get-tuple-element.37.normed.n0.n1, bf16[2,512,256]{2,1,0:T(8,128)(2,1)} %pack_weights.1.refs_0_.refs_8_, bf16[2,512,256]{2,1,0:T(8,128)(2,1)} %copy-done.4, ...), custom_call_target="tpu_custom_call" | custom-call | tf_op jit(solution)/shard_map/project/pallas_call | solution.py:142
  103.2 3.9 %collective-permute-start.17 = (bf16[512,256]{1,0:T(8,128)(2,1)}, bf16[512,256]{1,0:T(8,128)(2,1)S(1)}, u32[]{:S(2)}, u32[]{:S(2)}) collective-permute-start(bf16[512,256]{1,0:T(8,128)(2,1)} %get-tuple-element.39.refs_0_.kv), channel_id=1, source_target_pairs={{0,4},{2,6},{4,0},{6,2},{1,5},{3,7},{5,1},{7,3},{8,12},{10,14},{12... | collective-permute-start | bytes 786440 | tf_op jit(solution)/shard_map/ppermute | solution.py:30
  117.2 6.7 %upstream.1 = (bf16[512,128]{1,0:T(8,128)(2,1)}, bf16[16,512,256]{2,1,0:T(8,128)(2,1)}, bf16[16,128,256]{2,1,0:T(8,128)(2,1)}) custom-call(s32[16]{0:T(128)} %stack.171.idx, s32[8]{0:T(128)} %stack.180.idx.tok_idx, bf16[2,512,256]{2,1,0:T(8,128)(2,1)} %pad_maximum_fusion.1.refs_0_, bf16[2,512,256]{2,1,0:T(8,128)(2,1)} %copy-done.19, ...), custom_call_target="tpu_custom_call" | custom-call | tf_op jit(solution)/shard_map/upstream/pallas_call | solution.py:192
  125.5 8.9 %forward.1 = (bf16[512,128]{1,0:T(8,128)(2,1)}, bf16[128,512]{1,0:T(8,128)(2,1)}, f32[1,512]{1,0:T(1,128)}, bf16[4096,256]{1,0:T(8,128)(2,1)}) custom-call(s32[8]{0:T(128)} %stack.180.idx.tok_idx, s32[1,512]{1,0:T(1,128)} %add_maximum_fusion.limit, bf16[512,128]{1,0:T(8,128)(2,1)} %get-tuple-element.38.q, bf16[512,256]{1,0:T(8,128)(2,1)} %get-tuple-element.39.refs_0_.kv, ...), custom_call_target="tpu_custom_call" | custom-call | tf_op jit(solution)/shard_map/forward/pallas_call | solution.py:256
  134.4 10.1 %backward.1 = (bf16[512,128]{1,0:T(8,128)(2,1)}, bf16[4096,256]{1,0:T(8,128)(2,1)}) custom-call(s32[1,512]{1,0:T(1,128)} %add_maximum_fusion.limit, f32[1,512]{1,0:T(1,128)} %get-tuple-element.42.lse, bf16[512,128]{1,0:T(8,128)(2,1)} %get-tuple-element.38.q, bf16[4096,256]{1,0:T(8,128)(2,1)} %get-tuple-element.43.kv, bf16[512,128]{1,0:T(8,128)(2,1)} %get-tuple-element.44.da, ...), custom_call_target="tpu_custom_call" | custom-call | tf_op jit(solution)/shard_map/backward/pallas_call | solution.py:286
  144.5 5.3 %all-to-all-start.1 = ((bf16[8,512,256]{2,1,0:T(8,128)(2,1)}), bf16[8,512,256]{2,1,0:T(8,128)(2,1)S(1)}, u32[]{:S(2)}, u32[]{:S(2)}) async-start(bf16[8,512,256]{2,1,0:T(8,128)(2,1)} %bitcast.54), calls=%async_computation.1 | async-start | bytes 4194304 | tf_op jit(solution)/shard_map/all_to_all | solution.py:53
  149.9 3.7 %order_weights.1 = (bf16[8,384,256]{2,1,0:T(8,128)(2,1)}, bf16[8,384,256]{2,1,0:T(8,128)(2,1)}) custom-call(s32[8]{0:T(128)} %stack.180.idx.tok_idx, s32[1]{0:T(128)} %bitcast.50.core, bf16[2,512,256]{2,1,0:T(8,128)(2,1)} %pack_weights.1.refs_0_.refs_8_, bf16[2,512,256]{2,1,0:T(8,128)(2,1)} %copy-done.4, bf16[2,512,256]{2,1,0:T(8,128)(2,1)} %copy-done.5, ...), custom_call_target="tpu_custom_call" | custom-call | tf_op jit(solution)/shard_map/order_weights/pallas_call | solution.py:162
  154.2 3.5 %weight_grad.1.w0.w1 = bf16[16,128,256]{2,1,0:T(8,128)(2,1)} custom-call(bf16[128,512]{1,0:T(8,128)(2,1)} %get-tuple-element.45.att_t.left, bf16[16,512,256]{2,1,0:T(8,128)(2,1)} %get-tuple-element.48.right), custom_call_target="tpu_custom_call" | custom-call | tf_op jit(solution)/shard_map/weight_grad/pallas_call | solution.py:432
  157.7 20.0 %all-to-all-done.1.dkv = bf16[8,512,256]{2,1,0:T(8,128)(2,1)S(1)} async-done(((bf16[8,512,256]{2,1,0:T(8,128)(2,1)}), bf16[8,512,256]{2,1,0:T(8,128)(2,1)S(1)}, u32[]{:S(2)}, u32[]{:S(2)}) %all-to-all-start.1) | async-done | bytes 2097184 | tf_op jit(solution)/shard_map/all_to_all | solution.py:53
  179.0 9.5 %gradients.1 = (bf16[512,384]{1,0:T(8,128)(2,1)}, f32[8,512]{1,0:T(8,128)}, bf16[2,2,512,256]{3,2,1,0:T(8,128)(2,1)}, bf16[2,2,512,256]{3,2,1,0:T(8,128)(2,1)}, ...) custom-call(s32[8]{0:T(128)} %stack.205.idx, ...), custom_call_target="tpu_custom_call" | custom-call | tf_op jit(solution)/shard_map/gradients/pallas_call | solution.py:369
  192.0 3.0 %collective-permute-done.22 = bf16[512,128]{1,0:T(8,128)(2,1)S(1)} collective-permute-done((bf16[512,128]{1,0:T(8,128)(2,1)S(1)}, bf16[512,128]{1,0:T(8,128)(2,1)S(1)}, u32[]{:S(2)}, u32[]{:S(2)}) %collective-permute-start.22) | collective-permute-done | bytes 131104 | tf_op jit(solution)/shard_map/ppermute | solution.py:26
  198.4 2.5 collective-permute-start.24
  201.6 5.7 %input_grad.1 = (bf16[2,528,256]{2,1,0:T(8,128)(2,1)}, bf16[2,528,256]{2,1,0:T(8,128)(2,1)}, bf16[2,528,256]{2,1,0:T(8,128)(2,1)}, bf16[2,528,256]{2,1,0:T(8,128)(2,1)}) custom-call(s32[8]{0:T(128)} %stack.198.idx, bf16[512,384]{1,0:T(8,128)(2,1)} %get-tuple-element.49.g, bf16[512,384]{1,0:T(8,128)(2,1)} %copy-done.23, ...), custom_call_target="tpu_custom_call" | custom-call | tf_op jit(solution)/shard_map/input_grad/pallas_call | solution.py:416
  207.5 3.3 %collective-permute-start.42 = (bf16[2,528,256]{2,1,0:T(8,128)(2,1)}, bf16[2,528,256]{2,1,0:T(8,128)(2,1)}, u32[]{:S(2)}, u32[]{:S(2)}) collective-permute-start(bf16[2,528,256]{2,1,0:T(8,128)(2,1)} %get-tuple-element.55), channel_id=1, source_target_pairs={{0,64},{32,96},{64,0},{96,32},{1,65},{33,97},{65,1},{97,33},{2,66}... | collective-permute-start | bytes 1622024 | tf_op jit(solution)/shard_map/ppermute | solution.py:30
  211.6 4.3 %all-to-all-start = ((bf16[16,128,256]{2,1,0:T(8,128)(2,1)}), bf16[16,128,256]{2,1,0:T(8,128)(2,1)S(1)}, u32[]{:S(2)}, u32[]{:S(2)}) async-start(bf16[16,128,256]{2,1,0:T(8,128)(2,1)} %get-tuple-element.41), calls=%async_computation | async-start | bytes 2097152 | tf_op jit(solution)/shard_map/all_to_all | solution.py:53
  216.0 19.6 %collective-permute-done.41.refs_1_ = bf16[2,528,256]{2,1,0:T(8,128)(2,1)} collective-permute-done((bf16[2,528,256]{2,1,0:T(8,128)(2,1)}, bf16[2,528,256]{2,1,0:T(8,128)(2,1)}, u32[]{:S(2)}, u32[]{:S(2)}) %collective-permute-start.41) | collective-permute-done | bytes 540704 | tf_op jit(solution)/shard_map/ppermute | solution.py:30
  242.8 3.1 %line_sum.1 = (f32[512,256]{1,0:T(8,128)}, f32[8,256]{1,0:T(8,128)}, bf16[528,256]{1,0:T(8,128)(2,1)}, f32[8,2,2,256]{3,2,1,0:T(2,128)}) custom-call(s32[1]{0:T(128)} %bitcast.34.side, bf16[2,528,256]{2,1,0:T(8,128)(2,1)} %get-tuple-element.53.refs_0_, bf16[2,528,256]{2,1,0:T(8,128)(2,1)} %collective-permute-done.41.refs_1_, ...), custom_call_target="tpu_custom_call" | custom-call | tf_op jit(solution)/shard_map/line_sum/pallas_call | solution.py:471
  245.9 5.5 %collective-permute-done.25.refs_3_ = bf16[2,512,128]{2,1,0:T(8,128)(2,1)} collective-permute-done((bf16[2,512,128]{2,1,0:T(8,128)(2,1)S(1)}, bf16[2,512,128]{2,1,0:T(8,128)(2,1)}, u32[]{:S(2)}, u32[]{:S(2)}) %collective-permute-start.25) | collective-permute-done | bytes 262176 | tf_op jit(solution)/shard_map/ppermute | solution.py:30
  254.2 3.5 %all-to-all-start.2 = ((f32[16,2,256]{2,1,0:T(2,128)}), f32[16,2,256]{2,1,0:T(2,128)S(1)}, u32[]{:S(2)}, u32[]{:S(2)}) async-start(f32[16,2,256]{2,1,0:T(2,128)} %bitcast.61), calls=%async_computation.2 | async-start | bytes 65536 | tf_op jit(solution)/shard_map/all_to_all | solution.py:53
  259.1 4.7 %output.1 = bf16[512,256]{1,0:T(8,128)(2,1)} custom-call(s32[16]{0:T(128)} %stack.171.idx, bf16[2,512,128]{2,1,0:T(8,128)(2,1)} %copy-done.18, bf16[2,512,128]{2,1,0:T(8,128)(2,1)} %copy-done.25, bf16[2,512,128]{2,1,0:T(8,128)(2,1)} %collective-permute-done.24.refs_2_, bf16[2,512,128]{2,1,0:T(8,128)(2,1)} %collective-permute-done.25.refs_3_, ...), custom_call_target="tpu_custom_call" | custom-call | tf_op jit(solution)/shard_map/output/pallas_call | solution.py:518
  271.1 2.7 sum_weights.1
  (188 shorter events, 71.1 us)
Async XLA Ops:
  2.6 29.9 %collective-permute-start.11 = (bf16[2,512,256]{2,1,0:T(8,128)(2,1)}, bf16[2,512,256]{2,1,0:T(8,128)(2,1)S(1)}, u32[]{:S(2)}, u32[]{:S(2)}) collective-permute-start(bf16[2,512,256]{2,1,0:T(8,128)(2,1)} %pack_weights.1.refs_0_.refs_8_), channel_id=1, source_target_pairs={{0,1},{1,0},{2,3},{3,2},{4,5},{5,4},{6,7},{7,6},{8,9},{9,8},{10,11... | collective-permute-start | bytes 1572872 | tf_op jit(solution)/shard_map/ppermute | solution.py:26
  5.9 28.4 %collective-permute-start.10 = (bf16[2,512,256]{2,1,0:T(8,128)(2,1)}, bf16[2,512,256]{2,1,0:T(8,128)(2,1)S(1)}, u32[]{:S(2)}, u32[]{:S(2)}) collective-permute-start(bf16[2,512,256]{2,1,0:T(8,128)(2,1)} %pack_weights.1.refs_0_.refs_8_), channel_id=1, source_target_pairs={{0,4},{2,6},{4,0},{6,2},{1,5},{3,7},{5,1},{7,3},{8,12},{10,14},{12... | collective-permute-start | bytes 1572872 | tf_op jit(solution)/shard_map/ppermute | solution.py:30
  9.8 24.9 %collective-permute-start.8 = (bf16[2,512,256]{2,1,0:T(8,128)(2,1)}, bf16[2,512,256]{2,1,0:T(8,128)(2,1)S(1)}, u32[]{:S(2)}, u32[]{:S(2)}) collective-permute-start(bf16[2,512,256]{2,1,0:T(8,128)(2,1)} %pack_weights.1.refs_0_.refs_8_), channel_id=1, source_target_pairs={{0,2},{2,4},{4,6},{6,0},{1,3},{3,5},{5,7},{7,1},{8,10},{10,12},{12... | collective-permute-start | bytes 1572872 | tf_op jit(solution)/shard_map/ppermute | solution.py:30
  13.3 17.7 %collective-permute-start = (bf16[528,256]{1,0:T(8,128)(2,1)S(1)}, bf16[528,256]{1,0:T(8,128)(2,1)S(1)}, u32[]{:S(2)}, u32[]{:S(2)}) collective-permute-start(bf16[528,256]{1,0:T(8,128)(2,1)S(1)} %concatenate.6), channel_id=1, source_target_pairs={{0,16},{16,0},{1,17},{17,1},{2,18},{18,2},{3,19},{19,3},{4,20},{20... | collective-permute-start | bytes 811016 | tf_op jit(solution)/shard_map/ppermute | solution.py:26
  31.0 16.2 %collective-permute-start.31 = (bf16[2,512,256]{2,1,0:T(8,128)(2,1)}, bf16[2,512,256]{2,1,0:T(8,128)(2,1)S(1)}, u32[]{:S(2)}, u32[]{:S(2)}) collective-permute-start(bf16[2,512,256]{2,1,0:T(8,128)(2,1)} %pad_maximum_fusion.1.refs_0_), channel_id=1, source_target_pairs={{0,32},{32,64},{64,96},{96,0},{1,33},{33,65},{65,97},{97,1},{2,34}... | collective-permute-start | bytes 1572872 | tf_op jit(solution)/shard_map/ppermute | solution.py:30
  32.5 25.3 %collective-permute-start.32 = (bf16[2,512,256]{2,1,0:T(8,128)(2,1)}, bf16[2,512,256]{2,1,0:T(8,128)(2,1)}, u32[]{:S(2)}, u32[]{:S(2)}) collective-permute-start(bf16[2,512,256]{2,1,0:T(8,128)(2,1)} %pad_maximum_fusion.1.refs_0_), channel_id=1, source_target_pairs={{0,96},{32,0},{64,32},{96,64},{1,97},{33,1},{65,33},{97,65},{2,98}... | collective-permute-start | bytes 1572872 | tf_op jit(solution)/shard_map/ppermute | solution.py:30
  34.4 37.5 %collective-permute-start.1 = (bf16[2,528,256]{2,1,0:T(8,128)(2,1)S(1)}, bf16[2,528,256]{2,1,0:T(8,128)(2,1)S(1)}, u32[]{:S(2)}, u32[]{:S(2)}) collective-permute-start(bf16[2,528,256]{2,1,0:T(8,128)(2,1)S(1)} %pad_maximum_fusion.refs_0_.refs_8_.refs_5_), channel_id=1, source_target_pairs={{0,32},{32,64},{64,96},{96,0},{1,33},{33,65},{65,97},{97,1},{2,34}... | collective-permute-start | bytes 1622024 | tf_op jit(solution)/shard_map/ppermute | solution.py:30
  34.7 36.4 %collective-permute-start.33 = (bf16[2,512,256]{2,1,0:T(8,128)(2,1)}, bf16[2,512,256]{2,1,0:T(8,128)(2,1)}, u32[]{:S(2)}, u32[]{:S(2)}) collective-permute-start(bf16[2,512,256]{2,1,0:T(8,128)(2,1)} %pad_maximum_fusion.1.refs_0_), channel_id=1, source_target_pairs={{0,64},{32,96},{64,0},{96,32},{1,65},{33,97},{65,1},{97,33},{2,66}... | collective-permute-start | bytes 1572872 | tf_op jit(solution)/shard_map/ppermute | solution.py:30
  38.7 35.7 %collective-permute-start.2 = (bf16[2,528,256]{2,1,0:T(8,128)(2,1)S(1)}, bf16[2,528,256]{2,1,0:T(8,128)(2,1)S(1)}, u32[]{:S(2)}, u32[]{:S(2)}) collective-permute-start(bf16[2,528,256]{2,1,0:T(8,128)(2,1)S(1)} %pad_maximum_fusion.refs_0_.refs_8_.refs_5_), channel_id=1, source_target_pairs={{0,96},{32,0},{64,32},{96,64},{1,97},{33,1},{65,33},{97,65},{2,98}... | collective-permute-start | bytes 1622024 | tf_op jit(solution)/shard_map/ppermute | solution.py:30
  47.2 32.2 %collective-permute-start.3 = (bf16[2,528,256]{2,1,0:T(8,128)(2,1)S(1)}, bf16[2,528,256]{2,1,0:T(8,128)(2,1)S(1)}, u32[]{:S(2)}, u32[]{:S(2)}) collective-permute-start(bf16[2,528,256]{2,1,0:T(8,128)(2,1)S(1)} %pad_maximum_fusion.refs_0_.refs_8_.refs_5_), channel_id=1, source_target_pairs={{0,64},{32,96},{64,0},{96,32},{1,65},{33,97},{65,1},{97,33},{2,66}... | collective-permute-start | bytes 1622024 | tf_op jit(solution)/shard_map/ppermute | solution.py:30
  57.9 21.6 %collective-permute-start.4 = (bf16[2,528,256]{2,1,0:T(8,128)(2,1)S(1)}, bf16[2,528,256]{2,1,0:T(8,128)(2,1)S(1)}, u32[]{:S(2)}, u32[]{:S(2)}) collective-permute-start(bf16[2,528,256]{2,1,0:T(8,128)(2,1)S(1)} %pad_maximum_fusion.refs_0_.refs_8_.refs_5_), channel_id=1, source_target_pairs={{0,8},{8,0},{1,9},{9,1},{2,10},{10,2},{3,11},{11,3},{4,12},{12,4},... | collective-permute-start | bytes 1622024 | tf_op jit(solution)/shard_map/ppermute | solution.py:26
  84.1 19.2 %collective-permute-start.34 = (bf16[2,512,256]{2,1,0:T(8,128)(2,1)}, bf16[2,512,256]{2,1,0:T(8,128)(2,1)}, u32[]{:S(2)}, u32[]{:S(2)}) collective-permute-start(bf16[2,512,256]{2,1,0:T(8,128)(2,1)} %pad_maximum_fusion.1.refs_0_), channel_id=1, source_target_pairs={{0,8},{8,0},{1,9},{9,1},{2,10},{10,2},{3,11},{11,3},{4,12},{12,4},... | collective-permute-start | bytes 1572872 | tf_op jit(solution)/shard_map/ppermute | solution.py:26
  84.9 22.3 %collective-permute-start.35 = (bf16[2,512,256]{2,1,0:T(8,128)(2,1)S(1)}, bf16[2,512,256]{2,1,0:T(8,128)(2,1)}, u32[]{:S(2)}, u32[]{:S(2)}) collective-permute-start(bf16[2,512,256]{2,1,0:T(8,128)(2,1)S(1)} %collective-permute-done.31.refs_1_), channel_id=1, source_target_pairs={{0,8},{8,0},{1,9},{9,1},{2,10},{10,2},{3,11},{11,3},{4,12},{12,4},... | collective-permute-start | bytes 1572872 | tf_op jit(solution)/shard_map/ppermute | solution.py:26
  85.0 23.2 %collective-permute-start.36 = (bf16[2,512,256]{2,1,0:T(8,128)(2,1)}, bf16[2,512,256]{2,1,0:T(8,128)(2,1)}, u32[]{:S(2)}, u32[]{:S(2)}) collective-permute-start(bf16[2,512,256]{2,1,0:T(8,128)(2,1)} %collective-permute-done.32.refs_2_), channel_id=1, source_target_pairs={{0,8},{8,0},{1,9},{9,1},{2,10},{10,2},{3,11},{11,3},{4,12},{12,4},... | collective-permute-start | bytes 1572872 | tf_op jit(solution)/shard_map/ppermute | solution.py:26
  85.6 26.9 %collective-permute-start.37 = (bf16[2,512,256]{2,1,0:T(8,128)(2,1)}, bf16[2,512,256]{2,1,0:T(8,128)(2,1)}, u32[]{:S(2)}, u32[]{:S(2)}) collective-permute-start(bf16[2,512,256]{2,1,0:T(8,128)(2,1)} %collective-permute-done.33.refs_3_), channel_id=1, source_target_pairs={{0,8},{8,0},{1,9},{9,1},{2,10},{10,2},{3,11},{11,3},{4,12},{12,4},... | collective-permute-start | bytes 1572872 | tf_op jit(solution)/shard_map/ppermute | solution.py:26
  107.1 16.8 %collective-permute-start.15 = (bf16[512,256]{1,0:T(8,128)(2,1)}, bf16[512,256]{1,0:T(8,128)(2,1)S(1)}, u32[]{:S(2)}, u32[]{:S(2)}) collective-permute-start(bf16[512,256]{1,0:T(8,128)(2,1)} %get-tuple-element.39.refs_0_.kv), channel_id=1, source_target_pairs={{0,2},{2,4},{4,6},{6,0},{1,3},{3,5},{5,7},{7,1},{8,10},{10,12},{12... | collective-permute-start | bytes 786440 | tf_op jit(solution)/shard_map/ppermute | solution.py:30
  108.2 15.7 %collective-permute-start.16 = (bf16[512,256]{1,0:T(8,128)(2,1)}, bf16[512,256]{1,0:T(8,128)(2,1)S(1)}, u32[]{:S(2)}, u32[]{:S(2)}) collective-permute-start(bf16[512,256]{1,0:T(8,128)(2,1)} %get-tuple-element.39.refs_0_.kv), channel_id=1, source_target_pairs={{0,6},{2,0},{4,2},{6,4},{1,7},{3,1},{5,3},{7,5},{8,14},{10,8},{12,... | collective-permute-start | bytes 786440 | tf_op jit(solution)/shard_map/ppermute | solution.py:30
  144.5 33.2 %all-to-all-start.1 = ((bf16[8,512,256]{2,1,0:T(8,128)(2,1)}), bf16[8,512,256]{2,1,0:T(8,128)(2,1)S(1)}, u32[]{:S(2)}, u32[]{:S(2)}) async-start(bf16[8,512,256]{2,1,0:T(8,128)(2,1)} %bitcast.54), calls=%async_computation.1 | async-start | bytes 4194304 | tf_op jit(solution)/shard_map/all_to_all | solution.py:53
  153.5 42.3 %collective-permute-start.39 = (bf16[8,384,256]{2,1,0:T(8,128)(2,1)}, bf16[8,384,256]{2,1,0:T(8,128)(2,1)}, u32[]{:S(2)}, u32[]{:S(2)}) collective-permute-start(bf16[8,384,256]{2,1,0:T(8,128)(2,1)} %get-tuple-element.51), channel_id=1, source_target_pairs={{0,8},{8,0},{1,9},{9,1},{2,10},{10,2},{3,11},{11,3},{4,12},{12,4},... | collective-permute-start | bytes 4718600 | tf_op jit(solution)/shard_map/ppermute | solution.py:26
  190.0 20.9 %collective-permute-start.47 = (bf16[2,512,256]{2,1,0:T(8,128)(2,1)}, bf16[2,512,256]{2,1,0:T(8,128)(2,1)S(1)}, u32[]{:S(2)}, u32[]{:S(2)}) collective-permute-start(bf16[2,512,256]{2,1,0:T(8,128)(2,1)} %get-tuple-element.65), channel_id=1, source_target_pairs={{0,1},{1,0},{2,3},{3,2},{4,5},{5,4},{6,7},{7,6},{8,9},{9,8},{10,11... | collective-permute-start | bytes 1572872 | tf_op jit(solution)/shard_map/ppermute | solution.py:26
  191.4 44.3 %collective-permute-start.45 = (bf16[2,2,512,256]{3,2,1,0:T(8,128)(2,1)}, bf16[2,2,512,256]{3,2,1,0:T(8,128)(2,1)S(1)}, u32[]{:S(2)}, u32[]{:S(2)}) collective-permute-start(bf16[2,2,512,256]{3,2,1,0:T(8,128)(2,1)} %get-tuple-element.62), channel_id=1, source_target_pairs={{0,2},{2,4},{4,6},{6,0},{1,3},{3,5},{5,7},{7,1},{8,10},{10,12},{12... | collective-permute-start | bytes 3145736 | tf_op jit(solution)/shard_map/ppermute | solution.py:30
  195.0 41.1 %collective-permute-start.46 = (bf16[2,2,512,256]{3,2,1,0:T(8,128)(2,1)}, bf16[2,2,512,256]{3,2,1,0:T(8,128)(2,1)S(1)}, u32[]{:S(2)}, u32[]{:S(2)}) collective-permute-start(bf16[2,2,512,256]{3,2,1,0:T(8,128)(2,1)} %get-tuple-element.63), channel_id=1, source_target_pairs={{0,6},{2,0},{4,2},{6,4},{1,7},{3,1},{5,3},{7,5},{8,14},{10,8},{12,... | collective-permute-start | bytes 3145736 | tf_op jit(solution)/shard_map/ppermute | solution.py:30
  207.5 28.1 %collective-permute-start.41 = (bf16[2,528,256]{2,1,0:T(8,128)(2,1)}, bf16[2,528,256]{2,1,0:T(8,128)(2,1)}, u32[]{:S(2)}, u32[]{:S(2)}) collective-permute-start(bf16[2,528,256]{2,1,0:T(8,128)(2,1)} %get-tuple-element.54), channel_id=1, source_target_pairs={{0,32},{32,64},{64,96},{96,0},{1,33},{33,65},{65,97},{97,1},{2,34}... | collective-permute-start | bytes 1622024 | tf_op jit(solution)/shard_map/ppermute | solution.py:30
  207.5 33.2 %collective-permute-start.42 = (bf16[2,528,256]{2,1,0:T(8,128)(2,1)}, bf16[2,528,256]{2,1,0:T(8,128)(2,1)}, u32[]{:S(2)}, u32[]{:S(2)}) collective-permute-start(bf16[2,528,256]{2,1,0:T(8,128)(2,1)} %get-tuple-element.55), channel_id=1, source_target_pairs={{0,64},{32,96},{64,0},{96,32},{1,65},{33,97},{65,1},{97,33},{2,66}... | collective-permute-start | bytes 1622024 | tf_op jit(solution)/shard_map/ppermute | solution.py:30
  210.8 30.5 %collective-permute-start.43 = (bf16[2,528,256]{2,1,0:T(8,128)(2,1)}, bf16[2,528,256]{2,1,0:T(8,128)(2,1)}, u32[]{:S(2)}, u32[]{:S(2)}) collective-permute-start(bf16[2,528,256]{2,1,0:T(8,128)(2,1)} %get-tuple-element.56), channel_id=1, source_target_pairs={{0,96},{32,0},{64,32},{96,64},{1,97},{33,1},{65,33},{97,65},{2,98}... | collective-permute-start | bytes 1622024 | tf_op jit(solution)/shard_map/ppermute | solution.py:30
  211.6 42.6 %all-to-all-start = ((bf16[16,128,256]{2,1,0:T(8,128)(2,1)}), bf16[16,128,256]{2,1,0:T(8,128)(2,1)S(1)}, u32[]{:S(2)}, u32[]{:S(2)}) async-start(bf16[16,128,256]{2,1,0:T(8,128)(2,1)} %get-tuple-element.41), calls=%async_computation | async-start | bytes 2097152 | tf_op jit(solution)/shard_map/all_to_all | solution.py:53
  235.6 15.8 %collective-permute-start.25 = (bf16[2,512,128]{2,1,0:T(8,128)(2,1)S(1)}, bf16[2,512,128]{2,1,0:T(8,128)(2,1)}, u32[]{:S(2)}, u32[]{:S(2)}) collective-permute-start(bf16[2,512,128]{2,1,0:T(8,128)(2,1)S(1)} %pad_maximum_fusion.2.refs_0_), channel_id=1, source_target_pairs={{0,64},{32,96},{64,0},{96,32},{1,65},{33,97},{65,1},{97,33},{2,66}... | collective-permute-start | bytes 786440 | tf_op jit(solution)/shard_map/ppermute | solution.py:30
  235.8 17.0 %collective-permute-start.26 = (bf16[2,512,128]{2,1,0:T(8,128)(2,1)S(1)}, bf16[2,512,128]{2,1,0:T(8,128)(2,1)S(1)}, u32[]{:S(2)}, u32[]{:S(2)}) collective-permute-start(bf16[2,512,128]{2,1,0:T(8,128)(2,1)S(1)} %pad_maximum_fusion.2.refs_0_), channel_id=1, source_target_pairs={{0,8},{8,0},{1,9},{9,1},{2,10},{10,2},{3,11},{11,3},{4,12},{12,4},... | collective-permute-start | bytes 786440 | tf_op jit(solution)/shard_map/ppermute | solution.py:26
  236.1 16.7 %collective-permute-start.27 = (bf16[2,512,128]{2,1,0:T(8,128)(2,1)}, bf16[2,512,128]{2,1,0:T(8,128)(2,1)S(1)}, u32[]{:S(2)}, u32[]{:S(2)}) collective-permute-start(bf16[2,512,128]{2,1,0:T(8,128)(2,1)} %copy-done.25), channel_id=1, source_target_pairs={{0,8},{8,0},{1,9},{9,1},{2,10},{10,2},{3,11},{11,3},{4,12},{12,4},... | collective-permute-start | bytes 786440 | tf_op jit(solution)/shard_map/ppermute | solution.py:26
  240.7 28.8 %collective-permute-start.48 = (bf16[2,512,256]{2,1,0:T(8,128)(2,1)}, bf16[2,512,256]{2,1,0:T(8,128)(2,1)S(1)}, u32[]{:S(2)}, u32[]{:S(2)}) collective-permute-start(bf16[2,512,256]{2,1,0:T(8,128)(2,1)} %add_blocks.2), channel_id=1, source_target_pairs={{0,4},{2,6},{4,0},{6,2},{1,5},{3,7},{5,1},{7,3},{8,12},{10,14},{12... | collective-permute-start | bytes 1572872 | tf_op jit(solution)/shard_map/ppermute | solution.py:30
  241.4 28.1 %collective-permute-start.49 = (bf16[2,512,256]{2,1,0:T(8,128)(2,1)}, bf16[2,512,256]{2,1,0:T(8,128)(2,1)S(1)}, u32[]{:S(2)}, u32[]{:S(2)}) collective-permute-start(bf16[2,512,256]{2,1,0:T(8,128)(2,1)} %add_blocks.3), channel_id=1, source_target_pairs={{0,1},{1,0},{2,3},{3,2},{4,5},{5,4},{6,7},{7,6},{8,9},{9,8},{10,11... | collective-permute-start | bytes 1572872 | tf_op jit(solution)/shard_map/ppermute | solution.py:26
  251.4 14.9 %collective-permute-start.44 = (bf16[528,256]{1,0:T(8,128)(2,1)}, bf16[528,256]{1,0:T(8,128)(2,1)S(1)}, u32[]{:S(2)}, u32[]{:S(2)}) collective-permute-start(bf16[528,256]{1,0:T(8,128)(2,1)} %get-tuple-element.60), channel_id=1, source_target_pairs={{0,16},{16,0},{1,17},{17,1},{2,18},{18,2},{3,19},{19,3},{4,20},{20... | collective-permute-start | bytes 811016 | tf_op jit(solution)/shard_map/ppermute | solution.py:26
  (62 other events, 787.9 us)

commit v4 on v3

--- a/solution.py
+++ b/solution.py
@@ -109,7 +109,7 @@
 
 
 def normalize(idx, xs, modality):
-    tile = 128
+    tile = 256
     rows = lambda cols: pl.BlockSpec((tile, cols), lambda i: (i, 0))
     return pl.pallas_call(
         normalize_kernel,
@@ -188,7 +188,7 @@
 
 
 def upstream(idx, tok_idx, gs, ws):
-    tile = 128
+    tile = 256
     return pl.pallas_call(
         upstream_kernel,
         name="upstream",
@@ -206,7 +206,7 @@
     )(idx, tok_idx, *gs, *ws)
 
 
-KEY_BLOCK = 512
+KEY_BLOCK = 1024
 SCALE = 1.0 / math.sqrt(128)
 TO_BASE2 = SCALE * math.log2(math.e)
 
@@ -230,7 +230,7 @@
         s_all[pl.ds(b * KEY_BLOCK, KEY_BLOCK), :] = s
         return jnp.maximum(top, jnp.max(s, axis=0, keepdims=True))
 
-    top = lax.fori_loop(0, count, scores, jnp.full((1, cols), masked_low, F32))
+    top = lax.fori_loop(0, count, scores, jnp.full((1, cols), masked_low, F32), unroll=4)
 
     def sums(b, total):
         at = pl.ds(b * KEY_BLOCK, KEY_BLOCK)
@@ -238,7 +238,7 @@
         s_all[at, :] = e
         return total + jnp.sum(e, axis=0, keepdims=True)
 
-    total = lax.fori_loop(0, count, sums, jnp.zeros((1, cols), F32))
+    total = lax.fori_loop(0, count, sums, jnp.zeros((1, cols), F32), unroll=4)
     inv = 1.0 / total
     lse[...] = top + jnp.log2(total)
 
@@ -246,7 +246,7 @@
         at = pl.ds(b * KEY_BLOCK, KEY_BLOCK)
         return acc + dot(kv[at, 128:256], (s_all[at, :] * inv).astype(BF16), TN)
 
-    out_t = lax.fori_loop(0, count, attend, jnp.zeros((128, cols), F32)).astype(BF16)
+    out_t = lax.fori_loop(0, count, attend, jnp.zeros((128, cols), F32), unroll=4).astype(BF16)
     att_t[...] = out_t
     att[...] = out_t.T
 
@@ -278,7 +278,7 @@
         dkv[at, 128:256] = dot(p.astype(BF16), da[...]).astype(BF16)
         return acc + dot(kv[at, 0:128], ds, TN)
 
-    dq_t = lax.fori_loop(0, count, back, jnp.zeros((128, q.shape[0]), F32))
+    dq_t = lax.fori_loop(0, count, back, jnp.zeros((128, q.shape[0]), F32), unroll=2)
     dq[...] = dq_t.astype(BF16).T
 
 

time: 276 us -> 271 us (0.982)
  Pallas kernels: 79 us -> 72.8 us
    pallas_call x1, Pallas kernels: 8.92 us -> 5.98 us  [forward(): pl.pallas_call(forward_kernel, name='forward', in_specs=[SMEM] + [vmem] *...]
  transfers between devices with their start and end apart: 53 -> 53, of which waited for: 18 -> 17; matrix products, arithmetic and copies ran while one was open for 3% -> 3% of each run, Pallas kernels for 20% -> 20%
where the time goes in v4:
time: 271 us; the launch traced here: 269 us
  waiting for transfers between devices  102 us (38%)
  starting transfers between devices  75.9 us (28%)
  Pallas kernels  72.8 us (27%)
  local copies, waits for them, and re-layouts  13.4 us (5%)
  other arithmetic  3.85 us (1%)
    ppermute x25, waiting for transfers between devices, turn(): return lax.ppermute(a, axis, [(i, (i + d) % 4) for i in range(4)])  64 us
    ppermute x25, starting transfers between devices, turn(): return lax.ppermute(a, axis, [(i, (i + d) % 4) for i in range(4)])  44.4 us
    all_to_all x3, waiting for transfers between devices, exchange(): return lax.all_to_all(blocks, axis, 0, 0, tiled=True)  22 us
    ppermute x25, starting transfers between devices, swap(): return lax.ppermute(a, axis, [(0, 1), (1, 0)])  18.6 us
    ppermute x25, waiting for transfers between devices, swap(): return lax.ppermute(a, axis, [(0, 1), (1, 0)])  16.2 us
    all_to_all x3, starting transfers between devices, exchange(): return lax.all_to_all(blocks, axis, 0, 0, tiled=True)  12.9 us
    pallas_call x1, Pallas kernels, gradients(): pl.pallas_call(gradients_kernel, name='gradients', grid_spec=spec, out_sh...  9.5 us
    unnamed x82, local copies, waits for them, and re-layouts  8.75 us
  transfers between devices with their start and end apart: 53, of which 17 were waited for; matrix products, arithmetic and copies ran while one was open for 3% of the time, Pallas kernels for 20%

profile of v4, /device:TPU:0, one launch (start us, length us, event | category | flops | bytes accessed | tf_op | source)
XLA Modules:
  0.0 269.2 jit_solution(6902146192706367091)
XLA Ops:
  2.6 3.3 %collective-permute-start.11 = (bf16[2,512,256]{2,1,0:T(8,128)(2,1)}, bf16[2,512,256]{2,1,0:T(8,128)(2,1)S(1)}, u32[]{:S(2)}, u32[]{:S(2)}) collective-permute-start(bf16[2,512,256]{2,1,0:T(8,128)(2,1)} %pack_weights.1.refs_0_.refs_8_), channel_id=1, source_target_pairs={{0,1},{1,0},{2,3},{3,2},{4,5},{5,4},{6,7},{7,6},{8,9},{9,8},{10,11... | collective-permute-start | bytes 1572872 | tf_op jit(solution)/shard_map/ppermute | solution.py:26
  5.9 3.9 %collective-permute-start.10 = (bf16[2,512,256]{2,1,0:T(8,128)(2,1)}, bf16[2,512,256]{2,1,0:T(8,128)(2,1)S(1)}, u32[]{:S(2)}, u32[]{:S(2)}) collective-permute-start(bf16[2,512,256]{2,1,0:T(8,128)(2,1)} %pack_weights.1.refs_0_.refs_8_), channel_id=1, source_target_pairs={{0,4},{2,6},{4,0},{6,2},{1,5},{3,7},{5,1},{7,3},{8,12},{10,14},{12... | collective-permute-start | bytes 1572872 | tf_op jit(solution)/shard_map/ppermute | solution.py:30
  14.7 10.4 %collective-permute-done.30 = bf16[512,256]{1,0:T(8,128)(2,1)S(1)} collective-permute-done((bf16[512,256]{1,0:T(8,128)(2,1)}, bf16[512,256]{1,0:T(8,128)(2,1)S(1)}, u32[]{:S(2)}, u32[]{:S(2)}) %collective-permute-start.30) | collective-permute-done | bytes 262176 | tf_op jit(solution)/shard_map/ppermute | solution.py:26
  25.2 4.0 %collective-permute-start.9 = (bf16[2,512,256]{2,1,0:T(8,128)(2,1)}, bf16[2,512,256]{2,1,0:T(8,128)(2,1)S(1)}, u32[]{:S(2)}, u32[]{:S(2)}) collective-permute-start(bf16[2,512,256]{2,1,0:T(8,128)(2,1)} %pack_weights.1.refs_0_.refs_8_), channel_id=1, source_target_pairs={{0,6},{2,0},{4,2},{6,4},{1,7},{3,1},{5,3},{7,5},{8,14},{10,8},{12,... | collective-permute-start | bytes 1572872 | tf_op jit(solution)/shard_map/ppermute | solution.py:30
  34.7 2.7 %collective-permute-start.33 = (bf16[2,512,256]{2,1,0:T(8,128)(2,1)}, bf16[2,512,256]{2,1,0:T(8,128)(2,1)}, u32[]{:S(2)}, u32[]{:S(2)}) collective-permute-start(bf16[2,512,256]{2,1,0:T(8,128)(2,1)} %pad_maximum_fusion.1.refs_0_), channel_id=1, source_target_pairs={{0,64},{32,96},{64,0},{96,32},{1,65},{33,97},{65,1},{97,33},{2,66}... | collective-permute-start | bytes 1572872 | tf_op jit(solution)/shard_map/ppermute | solution.py:30
  38.7 2.8 %collective-permute-start.2 = (bf16[2,528,256]{2,1,0:T(8,128)(2,1)S(1)}, bf16[2,528,256]{2,1,0:T(8,128)(2,1)S(1)}, u32[]{:S(2)}, u32[]{:S(2)}) collective-permute-start(bf16[2,528,256]{2,1,0:T(8,128)(2,1)S(1)} %pad_maximum_fusion.refs_0_.refs_8_.refs_5_), channel_id=1, source_target_pairs={{0,96},{32,0},{64,32},{96,64},{1,97},{33,1},{65,33},{97,65},{2,98}... | collective-permute-start | bytes 1622024 | tf_op jit(solution)/shard_map/ppermute | solution.py:30
  41.5 5.7 %collective-permute-done.31.refs_1_ = bf16[2,512,256]{2,1,0:T(8,128)(2,1)S(1)} collective-permute-done((bf16[2,512,256]{2,1,0:T(8,128)(2,1)}, bf16[2,512,256]{2,1,0:T(8,128)(2,1)S(1)}, u32[]{:S(2)}, u32[]{:S(2)}) %collective-permute-start.31) | collective-permute-done | bytes 524320 | tf_op jit(solution)/shard_map/ppermute | solution.py:30
  49.1 8.8 %collective-permute-done.32.refs_2_ = bf16[2,512,256]{2,1,0:T(8,128)(2,1)} collective-permute-done((bf16[2,512,256]{2,1,0:T(8,128)(2,1)}, bf16[2,512,256]{2,1,0:T(8,128)(2,1)}, u32[]{:S(2)}, u32[]{:S(2)}) %collective-permute-start.32) | collective-permute-done | bytes 524320 | tf_op jit(solution)/shard_map/ppermute | solution.py:30
  57.9 13.3 %collective-permute-done.33.refs_3_ = bf16[2,512,256]{2,1,0:T(8,128)(2,1)} collective-permute-done((bf16[2,512,256]{2,1,0:T(8,128)(2,1)}, bf16[2,512,256]{2,1,0:T(8,128)(2,1)}, u32[]{:S(2)}, u32[]{:S(2)}) %collective-permute-start.33) | collective-permute-done | bytes 524320 | tf_op jit(solution)/shard_map/ppermute | solution.py:30
  71.9 2.5 collective-permute-start.13
  74.4 5.1 %collective-permute-done.3.refs_3_.refs_11_ = bf16[2,528,256]{2,1,0:T(8,128)(2,1)S(1)} collective-permute-done((bf16[2,528,256]{2,1,0:T(8,128)(2,1)S(1)}, bf16[2,528,256]{2,1,0:T(8,128)(2,1)S(1)}, u32[]{:S(2)}, u32[]{:S(2)}) %collective-permute-start.3) | collective-permute-done | bytes 540704 | tf_op jit(solution)/shard_map/ppermute | solution.py:30
  88.5 5.6 %normalize.1 = (bf16[16,512,256]{2,1,0:T(8,128)(2,1)}, f32[512,1]{1,0:T(8,128)}) custom-call(s32[16]{0:T(128)} %stack.171.idx, bf16[2,528,256]{2,1,0:T(8,128)(2,1)} %copy-done, bf16[2,528,256]{2,1,0:T(8,128)(2,1)} %copy-done.11, bf16[2,528,256]{2,1,0:T(8,128)(2,1)} %copy-done.12, bf16[2,528,256]{2,1,0:T(8,128)(2,1)} %copy-done.13, ...), custom_call_target="tpu_custom_call" | custom-call | tf_op jit(solution)/shard_map/normalize/pallas_call | solution.py:114
  95.5 5.8 %project.1 = (bf16[512,128]{1,0:T(8,128)(2,1)}, bf16[512,256]{1,0:T(8,128)(2,1)}) custom-call(s32[8]{0:T(128)} %stack.180.idx.tok_idx, bf16[16,512,256]{2,1,0:T(8,128)(2,1)} %get-tuple-element.37.normed.n0.n1, bf16[2,512,256]{2,1,0:T(8,128)(2,1)} %pack_weights.1.refs_0_.refs_8_, bf16[2,512,256]{2,1,0:T(8,128)(2,1)} %copy-done.4, ...), custom_call_target="tpu_custom_call" | custom-call | tf_op jit(solution)/shard_map/project/pallas_call | solution.py:142
  103.2 3.9 %collective-permute-start.17 = (bf16[512,256]{1,0:T(8,128)(2,1)}, bf16[512,256]{1,0:T(8,128)(2,1)S(1)}, u32[]{:S(2)}, u32[]{:S(2)}) collective-permute-start(bf16[512,256]{1,0:T(8,128)(2,1)} %get-tuple-element.39.refs_0_.kv), channel_id=1, source_target_pairs={{0,4},{2,6},{4,0},{6,2},{1,5},{3,7},{5,1},{7,3},{8,12},{10,14},{12... | collective-permute-start | bytes 786440 | tf_op jit(solution)/shard_map/ppermute | solution.py:30
  117.2 5.3 %upstream.1 = (bf16[512,128]{1,0:T(8,128)(2,1)}, bf16[16,512,256]{2,1,0:T(8,128)(2,1)}, bf16[16,128,256]{2,1,0:T(8,128)(2,1)}) custom-call(s32[16]{0:T(128)} %stack.171.idx, s32[8]{0:T(128)} %stack.180.idx.tok_idx, bf16[2,512,256]{2,1,0:T(8,128)(2,1)} %pad_maximum_fusion.1.refs_0_, bf16[2,512,256]{2,1,0:T(8,128)(2,1)} %copy-done.19, ...), custom_call_target="tpu_custom_call" | custom-call | tf_op jit(solution)/shard_map/upstream/pallas_call | solution.py:192
  125.5 6.0 %forward.1 = (bf16[512,128]{1,0:T(8,128)(2,1)}, bf16[128,512]{1,0:T(8,128)(2,1)}, f32[1,512]{1,0:T(1,128)}, bf16[4096,256]{1,0:T(8,128)(2,1)}) custom-call(s32[8]{0:T(128)} %stack.180.idx.tok_idx, s32[1,512]{1,0:T(1,128)} %add_maximum_fusion.limit, bf16[512,128]{1,0:T(8,128)(2,1)} %get-tuple-element.38.q, bf16[512,256]{1,0:T(8,128)(2,1)} %get-tuple-element.39.refs_0_.kv, ...), custom_call_target="tpu_custom_call" | custom-call | tf_op jit(solution)/shard_map/forward/pallas_call | solution.py:256
  131.5 8.5 %backward.1 = (bf16[512,128]{1,0:T(8,128)(2,1)}, bf16[4096,256]{1,0:T(8,128)(2,1)}) custom-call(s32[1,512]{1,0:T(1,128)} %add_maximum_fusion.limit, f32[1,512]{1,0:T(1,128)} %get-tuple-element.42.lse, bf16[512,128]{1,0:T(8,128)(2,1)} %get-tuple-element.38.q, bf16[4096,256]{1,0:T(8,128)(2,1)} %get-tuple-element.43.kv, bf16[512,128]{1,0:T(8,128)(2,1)} %get-tuple-element.44.da, ...), custom_call_target="tpu_custom_call" | custom-call | tf_op jit(solution)/shard_map/backward/pallas_call | solution.py:286
  140.1 5.1 %all-to-all-start.1 = ((bf16[8,512,256]{2,1,0:T(8,128)(2,1)}), bf16[8,512,256]{2,1,0:T(8,128)(2,1)S(1)}, u32[]{:S(2)}, u32[]{:S(2)}) async-start(bf16[8,512,256]{2,1,0:T(8,128)(2,1)} %bitcast.54), calls=%async_computation.1 | async-start | bytes 4194304 | tf_op jit(solution)/shard_map/all_to_all | solution.py:53
  145.1 3.7 %order_weights.1 = (bf16[8,384,256]{2,1,0:T(8,128)(2,1)}, bf16[8,384,256]{2,1,0:T(8,128)(2,1)}) custom-call(s32[8]{0:T(128)} %stack.180.idx.tok_idx, s32[1]{0:T(128)} %bitcast.50.core, bf16[2,512,256]{2,1,0:T(8,128)(2,1)} %pack_weights.1.refs_0_.refs_8_, bf16[2,512,256]{2,1,0:T(8,128)(2,1)} %copy-done.4, bf16[2,512,256]{2,1,0:T(8,128)(2,1)} %copy-done.5, ...), custom_call_target="tpu_custom_call" | custom-call | tf_op jit(solution)/shard_map/order_weights/pallas_call | solution.py:162
  149.5 3.5 %weight_grad.1.w0.w1 = bf16[16,128,256]{2,1,0:T(8,128)(2,1)} custom-call(bf16[128,512]{1,0:T(8,128)(2,1)} %get-tuple-element.45.att_t.left, bf16[16,512,256]{2,1,0:T(8,128)(2,1)} %get-tuple-element.48.right), custom_call_target="tpu_custom_call" | custom-call | tf_op jit(solution)/shard_map/weight_grad/pallas_call | solution.py:432
  153.0 20.3 %all-to-all-done.1.dkv = bf16[8,512,256]{2,1,0:T(8,128)(2,1)S(1)} async-done(((bf16[8,512,256]{2,1,0:T(8,128)(2,1)}), bf16[8,512,256]{2,1,0:T(8,128)(2,1)S(1)}, u32[]{:S(2)}, u32[]{:S(2)}) %all-to-all-start.1) | async-done | bytes 2097184 | tf_op jit(solution)/shard_map/all_to_all | solution.py:53
  174.6 9.5 %gradients.1 = (bf16[512,384]{1,0:T(8,128)(2,1)}, f32[8,512]{1,0:T(8,128)}, bf16[2,2,512,256]{3,2,1,0:T(8,128)(2,1)}, bf16[2,2,512,256]{3,2,1,0:T(8,128)(2,1)}, ...) custom-call(s32[8]{0:T(128)} %stack.205.idx, ...), custom_call_target="tpu_custom_call" | custom-call | tf_op jit(solution)/shard_map/gradients/pallas_call | solution.py:369
  187.5 3.0 %collective-permute-done.22 = bf16[512,128]{1,0:T(8,128)(2,1)S(1)} collective-permute-done((bf16[512,128]{1,0:T(8,128)(2,1)S(1)}, bf16[512,128]{1,0:T(8,128)(2,1)S(1)}, u32[]{:S(2)}, u32[]{:S(2)}) %collective-permute-start.22) | collective-permute-done | bytes 131104 | tf_op jit(solution)/shard_map/ppermute | solution.py:26
  197.2 5.7 %input_grad.1 = (bf16[2,528,256]{2,1,0:T(8,128)(2,1)}, bf16[2,528,256]{2,1,0:T(8,128)(2,1)}, bf16[2,528,256]{2,1,0:T(8,128)(2,1)}, bf16[2,528,256]{2,1,0:T(8,128)(2,1)}) custom-call(s32[8]{0:T(128)} %stack.198.idx, bf16[512,384]{1,0:T(8,128)(2,1)} %get-tuple-element.49.g, bf16[512,384]{1,0:T(8,128)(2,1)} %copy-done.23, ...), custom_call_target="tpu_custom_call" | custom-call | tf_op jit(solution)/shard_map/input_grad/pallas_call | solution.py:416
  203.0 3.3 %collective-permute-start.42 = (bf16[2,528,256]{2,1,0:T(8,128)(2,1)}, bf16[2,528,256]{2,1,0:T(8,128)(2,1)}, u32[]{:S(2)}, u32[]{:S(2)}) collective-permute-start(bf16[2,528,256]{2,1,0:T(8,128)(2,1)} %get-tuple-element.55), channel_id=1, source_target_pairs={{0,64},{32,96},{64,0},{96,32},{1,65},{33,97},{65,1},{97,33},{2,66}... | collective-permute-start | bytes 1622024 | tf_op jit(solution)/shard_map/ppermute | solution.py:30
  207.2 4.3 %all-to-all-start = ((bf16[16,128,256]{2,1,0:T(8,128)(2,1)}), bf16[16,128,256]{2,1,0:T(8,128)(2,1)S(1)}, u32[]{:S(2)}, u32[]{:S(2)}) async-start(bf16[16,128,256]{2,1,0:T(8,128)(2,1)} %get-tuple-element.41), calls=%async_computation | async-start | bytes 2097152 | tf_op jit(solution)/shard_map/all_to_all | solution.py:53
  211.5 19.6 %collective-permute-done.41.refs_1_ = bf16[2,528,256]{2,1,0:T(8,128)(2,1)} collective-permute-done((bf16[2,528,256]{2,1,0:T(8,128)(2,1)}, bf16[2,528,256]{2,1,0:T(8,128)(2,1)}, u32[]{:S(2)}, u32[]{:S(2)}) %collective-permute-start.41) | collective-permute-done | bytes 540704 | tf_op jit(solution)/shard_map/ppermute | solution.py:30
  238.2 3.1 %line_sum.1 = (f32[512,256]{1,0:T(8,128)}, f32[8,256]{1,0:T(8,128)}, bf16[528,256]{1,0:T(8,128)(2,1)}, f32[8,2,2,256]{3,2,1,0:T(2,128)}) custom-call(s32[1]{0:T(128)} %bitcast.34.side, bf16[2,528,256]{2,1,0:T(8,128)(2,1)} %get-tuple-element.53.refs_0_, bf16[2,528,256]{2,1,0:T(8,128)(2,1)} %collective-permute-done.41.refs_1_, ...), custom_call_target="tpu_custom_call" | custom-call | tf_op jit(solution)/shard_map/line_sum/pallas_call | solution.py:471
  241.3 5.6 %collective-permute-done.25.refs_3_ = bf16[2,512,128]{2,1,0:T(8,128)(2,1)} collective-permute-done((bf16[2,512,128]{2,1,0:T(8,128)(2,1)S(1)}, bf16[2,512,128]{2,1,0:T(8,128)(2,1)}, u32[]{:S(2)}, u32[]{:S(2)}) %collective-permute-start.25) | collective-permute-done | bytes 262176 | tf_op jit(solution)/shard_map/ppermute | solution.py:30
  249.7 3.5 %all-to-all-start.2 = ((f32[16,2,256]{2,1,0:T(2,128)}), f32[16,2,256]{2,1,0:T(2,128)S(1)}, u32[]{:S(2)}, u32[]{:S(2)}) async-start(f32[16,2,256]{2,1,0:T(2,128)} %bitcast.61), calls=%async_computation.2 | async-start | bytes 65536 | tf_op jit(solution)/shard_map/all_to_all | solution.py:53
  254.6 4.7 %output.1 = bf16[512,256]{1,0:T(8,128)(2,1)} custom-call(s32[16]{0:T(128)} %stack.171.idx, bf16[2,512,128]{2,1,0:T(8,128)(2,1)} %copy-done.18, bf16[2,512,128]{2,1,0:T(8,128)(2,1)} %copy-done.25, bf16[2,512,128]{2,1,0:T(8,128)(2,1)} %collective-permute-done.24.refs_2_, bf16[2,512,128]{2,1,0:T(8,128)(2,1)} %collective-permute-done.25.refs_3_, ...), custom_call_target="tpu_custom_call" | custom-call | tf_op jit(solution)/shard_map/output/pallas_call | solution.py:518
  266.5 2.7 sum_weights.1
  (188 shorter events, 72.8 us)
Async XLA Ops:
  2.6 29.9 %collective-permute-start.11 = (bf16[2,512,256]{2,1,0:T(8,128)(2,1)}, bf16[2,512,256]{2,1,0:T(8,128)(2,1)S(1)}, u32[]{:S(2)}, u32[]{:S(2)}) collective-permute-start(bf16[2,512,256]{2,1,0:T(8,128)(2,1)} %pack_weights.1.refs_0_.refs_8_), channel_id=1, source_target_pairs={{0,1},{1,0},{2,3},{3,2},{4,5},{5,4},{6,7},{7,6},{8,9},{9,8},{10,11... | collective-permute-start | bytes 1572872 | tf_op jit(solution)/shard_map/ppermute | solution.py:26
  5.9 28.4 %collective-permute-start.10 = (bf16[2,512,256]{2,1,0:T(8,128)(2,1)}, bf16[2,512,256]{2,1,0:T(8,128)(2,1)S(1)}, u32[]{:S(2)}, u32[]{:S(2)}) collective-permute-start(bf16[2,512,256]{2,1,0:T(8,128)(2,1)} %pack_weights.1.refs_0_.refs_8_), channel_id=1, source_target_pairs={{0,4},{2,6},{4,0},{6,2},{1,5},{3,7},{5,1},{7,3},{8,12},{10,14},{12... | collective-permute-start | bytes 1572872 | tf_op jit(solution)/shard_map/ppermute | solution.py:30
  9.8 24.9 %collective-permute-start.8 = (bf16[2,512,256]{2,1,0:T(8,128)(2,1)}, bf16[2,512,256]{2,1,0:T(8,128)(2,1)S(1)}, u32[]{:S(2)}, u32[]{:S(2)}) collective-permute-start(bf16[2,512,256]{2,1,0:T(8,128)(2,1)} %pack_weights.1.refs_0_.refs_8_), channel_id=1, source_target_pairs={{0,2},{2,4},{4,6},{6,0},{1,3},{3,5},{5,7},{7,1},{8,10},{10,12},{12... | collective-permute-start | bytes 1572872 | tf_op jit(solution)/shard_map/ppermute | solution.py:30
  10.8 14.4 %collective-permute-start.30 = (bf16[512,256]{1,0:T(8,128)(2,1)}, bf16[512,256]{1,0:T(8,128)(2,1)S(1)}, u32[]{:S(2)}, u32[]{:S(2)}) collective-permute-start(bf16[512,256]{1,0:T(8,128)(2,1)} %param.13), channel_id=1, source_target_pairs={{0,16},{16,0},{1,17},{17,1},{2,18},{18,2},{3,19},{19,3},{4,20},{20... | collective-permute-start | bytes 786440 | tf_op jit(solution)/shard_map/ppermute | solution.py:26
  13.3 17.7 %collective-permute-start = (bf16[528,256]{1,0:T(8,128)(2,1)S(1)}, bf16[528,256]{1,0:T(8,128)(2,1)S(1)}, u32[]{:S(2)}, u32[]{:S(2)}) collective-permute-start(bf16[528,256]{1,0:T(8,128)(2,1)S(1)} %concatenate.6), channel_id=1, source_target_pairs={{0,16},{16,0},{1,17},{17,1},{2,18},{18,2},{3,19},{19,3},{4,20},{20... | collective-permute-start | bytes 811016 | tf_op jit(solution)/shard_map/ppermute | solution.py:26
  31.0 16.2 %collective-permute-start.31 = (bf16[2,512,256]{2,1,0:T(8,128)(2,1)}, bf16[2,512,256]{2,1,0:T(8,128)(2,1)S(1)}, u32[]{:S(2)}, u32[]{:S(2)}) collective-permute-start(bf16[2,512,256]{2,1,0:T(8,128)(2,1)} %pad_maximum_fusion.1.refs_0_), channel_id=1, source_target_pairs={{0,32},{32,64},{64,96},{96,0},{1,33},{33,65},{65,97},{97,1},{2,34}... | collective-permute-start | bytes 1572872 | tf_op jit(solution)/shard_map/ppermute | solution.py:30
  32.5 25.3 %collective-permute-start.32 = (bf16[2,512,256]{2,1,0:T(8,128)(2,1)}, bf16[2,512,256]{2,1,0:T(8,128)(2,1)}, u32[]{:S(2)}, u32[]{:S(2)}) collective-permute-start(bf16[2,512,256]{2,1,0:T(8,128)(2,1)} %pad_maximum_fusion.1.refs_0_), channel_id=1, source_target_pairs={{0,96},{32,0},{64,32},{96,64},{1,97},{33,1},{65,33},{97,65},{2,98}... | collective-permute-start | bytes 1572872 | tf_op jit(solution)/shard_map/ppermute | solution.py:30
  34.4 37.5 %collective-permute-start.1 = (bf16[2,528,256]{2,1,0:T(8,128)(2,1)S(1)}, bf16[2,528,256]{2,1,0:T(8,128)(2,1)S(1)}, u32[]{:S(2)}, u32[]{:S(2)}) collective-permute-start(bf16[2,528,256]{2,1,0:T(8,128)(2,1)S(1)} %pad_maximum_fusion.refs_0_.refs_8_.refs_5_), channel_id=1, source_target_pairs={{0,32},{32,64},{64,96},{96,0},{1,33},{33,65},{65,97},{97,1},{2,34}... | collective-permute-start | bytes 1622024 | tf_op jit(solution)/shard_map/ppermute | solution.py:30
  34.7 36.4 %collective-permute-start.33 = (bf16[2,512,256]{2,1,0:T(8,128)(2,1)}, bf16[2,512,256]{2,1,0:T(8,128)(2,1)}, u32[]{:S(2)}, u32[]{:S(2)}) collective-permute-start(bf16[2,512,256]{2,1,0:T(8,128)(2,1)} %pad_maximum_fusion.1.refs_0_), channel_id=1, source_target_pairs={{0,64},{32,96},{64,0},{96,32},{1,65},{33,97},{65,1},{97,33},{2,66}... | collective-permute-start | bytes 1572872 | tf_op jit(solution)/shard_map/ppermute | solution.py:30
  38.7 35.7 %collective-permute-start.2 = (bf16[2,528,256]{2,1,0:T(8,128)(2,1)S(1)}, bf16[2,528,256]{2,1,0:T(8,128)(2,1)S(1)}, u32[]{:S(2)}, u32[]{:S(2)}) collective-permute-start(bf16[2,528,256]{2,1,0:T(8,128)(2,1)S(1)} %pad_maximum_fusion.refs_0_.refs_8_.refs_5_), channel_id=1, source_target_pairs={{0,96},{32,0},{64,32},{96,64},{1,97},{33,1},{65,33},{97,65},{2,98}... | collective-permute-start | bytes 1622024 | tf_op jit(solution)/shard_map/ppermute | solution.py:30
  47.2 32.2 %collective-permute-start.3 = (bf16[2,528,256]{2,1,0:T(8,128)(2,1)S(1)}, bf16[2,528,256]{2,1,0:T(8,128)(2,1)S(1)}, u32[]{:S(2)}, u32[]{:S(2)}) collective-permute-start(bf16[2,528,256]{2,1,0:T(8,128)(2,1)S(1)} %pad_maximum_fusion.refs_0_.refs_8_.refs_5_), channel_id=1, source_target_pairs={{0,64},{32,96},{64,0},{96,32},{1,65},{33,97},{65,1},{97,33},{2,66}... | collective-permute-start | bytes 1622024 | tf_op jit(solution)/shard_map/ppermute | solution.py:30
  57.9 21.6 %collective-permute-start.4 = (bf16[2,528,256]{2,1,0:T(8,128)(2,1)S(1)}, bf16[2,528,256]{2,1,0:T(8,128)(2,1)S(1)}, u32[]{:S(2)}, u32[]{:S(2)}) collective-permute-start(bf16[2,528,256]{2,1,0:T(8,128)(2,1)S(1)} %pad_maximum_fusion.refs_0_.refs_8_.refs_5_), channel_id=1, source_target_pairs={{0,8},{8,0},{1,9},{9,1},{2,10},{10,2},{3,11},{11,3},{4,12},{12,4},... | collective-permute-start | bytes 1622024 | tf_op jit(solution)/shard_map/ppermute | solution.py:26
  84.1 19.2 %collective-permute-start.34 = (bf16[2,512,256]{2,1,0:T(8,128)(2,1)}, bf16[2,512,256]{2,1,0:T(8,128)(2,1)}, u32[]{:S(2)}, u32[]{:S(2)}) collective-permute-start(bf16[2,512,256]{2,1,0:T(8,128)(2,1)} %pad_maximum_fusion.1.refs_0_), channel_id=1, source_target_pairs={{0,8},{8,0},{1,9},{9,1},{2,10},{10,2},{3,11},{11,3},{4,12},{12,4},... | collective-permute-start | bytes 1572872 | tf_op jit(solution)/shard_map/ppermute | solution.py:26
  84.9 22.3 %collective-permute-start.35 = (bf16[2,512,256]{2,1,0:T(8,128)(2,1)S(1)}, bf16[2,512,256]{2,1,0:T(8,128)(2,1)}, u32[]{:S(2)}, u32[]{:S(2)}) collective-permute-start(bf16[2,512,256]{2,1,0:T(8,128)(2,1)S(1)} %collective-permute-done.31.refs_1_), channel_id=1, source_target_pairs={{0,8},{8,0},{1,9},{9,1},{2,10},{10,2},{3,11},{11,3},{4,12},{12,4},... | collective-permute-start | bytes 1572872 | tf_op jit(solution)/shard_map/ppermute | solution.py:26
  85.0 23.2 %collective-permute-start.36 = (bf16[2,512,256]{2,1,0:T(8,128)(2,1)}, bf16[2,512,256]{2,1,0:T(8,128)(2,1)}, u32[]{:S(2)}, u32[]{:S(2)}) collective-permute-start(bf16[2,512,256]{2,1,0:T(8,128)(2,1)} %collective-permute-done.32.refs_2_), channel_id=1, source_target_pairs={{0,8},{8,0},{1,9},{9,1},{2,10},{10,2},{3,11},{11,3},{4,12},{12,4},... | collective-permute-start | bytes 1572872 | tf_op jit(solution)/shard_map/ppermute | solution.py:26
  85.6 26.9 %collective-permute-start.37 = (bf16[2,512,256]{2,1,0:T(8,128)(2,1)}, bf16[2,512,256]{2,1,0:T(8,128)(2,1)}, u32[]{:S(2)}, u32[]{:S(2)}) collective-permute-start(bf16[2,512,256]{2,1,0:T(8,128)(2,1)} %collective-permute-done.33.refs_3_), channel_id=1, source_target_pairs={{0,8},{8,0},{1,9},{9,1},{2,10},{10,2},{3,11},{11,3},{4,12},{12,4},... | collective-permute-start | bytes 1572872 | tf_op jit(solution)/shard_map/ppermute | solution.py:26
  107.1 15.4 %collective-permute-start.15 = (bf16[512,256]{1,0:T(8,128)(2,1)}, bf16[512,256]{1,0:T(8,128)(2,1)S(1)}, u32[]{:S(2)}, u32[]{:S(2)}) collective-permute-start(bf16[512,256]{1,0:T(8,128)(2,1)} %get-tuple-element.39.refs_0_.kv), channel_id=1, source_target_pairs={{0,2},{2,4},{4,6},{6,0},{1,3},{3,5},{5,7},{7,1},{8,10},{10,12},{12... | collective-permute-start | bytes 786440 | tf_op jit(solution)/shard_map/ppermute | solution.py:30
  140.1 33.2 %all-to-all-start.1 = ((bf16[8,512,256]{2,1,0:T(8,128)(2,1)}), bf16[8,512,256]{2,1,0:T(8,128)(2,1)S(1)}, u32[]{:S(2)}, u32[]{:S(2)}) async-start(bf16[8,512,256]{2,1,0:T(8,128)(2,1)} %bitcast.54), calls=%async_computation.1 | async-start | bytes 4194304 | tf_op jit(solution)/shard_map/all_to_all | solution.py:53
  148.8 42.8 %collective-permute-start.39 = (bf16[8,384,256]{2,1,0:T(8,128)(2,1)}, bf16[8,384,256]{2,1,0:T(8,128)(2,1)}, u32[]{:S(2)}, u32[]{:S(2)}) collective-permute-start(bf16[8,384,256]{2,1,0:T(8,128)(2,1)} %get-tuple-element.51), channel_id=1, source_target_pairs={{0,8},{8,0},{1,9},{9,1},{2,10},{10,2},{3,11},{11,3},{4,12},{12,4},... | collective-permute-start | bytes 4718600 | tf_op jit(solution)/shard_map/ppermute | solution.py:26
  185.5 20.8 %collective-permute-start.47 = (bf16[2,512,256]{2,1,0:T(8,128)(2,1)}, bf16[2,512,256]{2,1,0:T(8,128)(2,1)S(1)}, u32[]{:S(2)}, u32[]{:S(2)}) collective-permute-start(bf16[2,512,256]{2,1,0:T(8,128)(2,1)} %get-tuple-element.65), channel_id=1, source_target_pairs={{0,1},{1,0},{2,3},{3,2},{4,5},{5,4},{6,7},{7,6},{8,9},{9,8},{10,11... | collective-permute-start | bytes 1572872 | tf_op jit(solution)/shard_map/ppermute | solution.py:26
  186.9 44.3 %collective-permute-start.45 = (bf16[2,2,512,256]{3,2,1,0:T(8,128)(2,1)}, bf16[2,2,512,256]{3,2,1,0:T(8,128)(2,1)S(1)}, u32[]{:S(2)}, u32[]{:S(2)}) collective-permute-start(bf16[2,2,512,256]{3,2,1,0:T(8,128)(2,1)} %get-tuple-element.62), channel_id=1, source_target_pairs={{0,2},{2,4},{4,6},{6,0},{1,3},{3,5},{5,7},{7,1},{8,10},{10,12},{12... | collective-permute-start | bytes 3145736 | tf_op jit(solution)/shard_map/ppermute | solution.py:30
  190.5 40.8 %collective-permute-start.46 = (bf16[2,2,512,256]{3,2,1,0:T(8,128)(2,1)}, bf16[2,2,512,256]{3,2,1,0:T(8,128)(2,1)S(1)}, u32[]{:S(2)}, u32[]{:S(2)}) collective-permute-start(bf16[2,2,512,256]{3,2,1,0:T(8,128)(2,1)} %get-tuple-element.63), channel_id=1, source_target_pairs={{0,6},{2,0},{4,2},{6,4},{1,7},{3,1},{5,3},{7,5},{8,14},{10,8},{12,... | collective-permute-start | bytes 3145736 | tf_op jit(solution)/shard_map/ppermute | solution.py:30
  203.0 28.1 %collective-permute-start.41 = (bf16[2,528,256]{2,1,0:T(8,128)(2,1)}, bf16[2,528,256]{2,1,0:T(8,128)(2,1)}, u32[]{:S(2)}, u32[]{:S(2)}) collective-permute-start(bf16[2,528,256]{2,1,0:T(8,128)(2,1)} %get-tuple-element.54), channel_id=1, source_target_pairs={{0,32},{32,64},{64,96},{96,0},{1,33},{33,65},{65,97},{97,1},{2,34}... | collective-permute-start | bytes 1622024 | tf_op jit(solution)/shard_map/ppermute | solution.py:30
  203.0 33.1 %collective-permute-start.42 = (bf16[2,528,256]{2,1,0:T(8,128)(2,1)}, bf16[2,528,256]{2,1,0:T(8,128)(2,1)}, u32[]{:S(2)}, u32[]{:S(2)}) collective-permute-start(bf16[2,528,256]{2,1,0:T(8,128)(2,1)} %get-tuple-element.55), channel_id=1, source_target_pairs={{0,64},{32,96},{64,0},{96,32},{1,65},{33,97},{65,1},{97,33},{2,66}... | collective-permute-start | bytes 1622024 | tf_op jit(solution)/shard_map/ppermute | solution.py:30
  206.4 30.4 %collective-permute-start.43 = (bf16[2,528,256]{2,1,0:T(8,128)(2,1)}, bf16[2,528,256]{2,1,0:T(8,128)(2,1)}, u32[]{:S(2)}, u32[]{:S(2)}) collective-permute-start(bf16[2,528,256]{2,1,0:T(8,128)(2,1)} %get-tuple-element.56), channel_id=1, source_target_pairs={{0,96},{32,0},{64,32},{96,64},{1,97},{33,1},{65,33},{97,65},{2,98}... | collective-permute-start | bytes 1622024 | tf_op jit(solution)/shard_map/ppermute | solution.py:30
  207.2 42.6 %all-to-all-start = ((bf16[16,128,256]{2,1,0:T(8,128)(2,1)}), bf16[16,128,256]{2,1,0:T(8,128)(2,1)S(1)}, u32[]{:S(2)}, u32[]{:S(2)}) async-start(bf16[16,128,256]{2,1,0:T(8,128)(2,1)} %get-tuple-element.41), calls=%async_computation | async-start | bytes 2097152 | tf_op jit(solution)/shard_map/all_to_all | solution.py:53
  231.1 15.8 %collective-permute-start.25 = (bf16[2,512,128]{2,1,0:T(8,128)(2,1)S(1)}, bf16[2,512,128]{2,1,0:T(8,128)(2,1)}, u32[]{:S(2)}, u32[]{:S(2)}) collective-permute-start(bf16[2,512,128]{2,1,0:T(8,128)(2,1)S(1)} %pad_maximum_fusion.2.refs_0_), channel_id=1, source_target_pairs={{0,64},{32,96},{64,0},{96,32},{1,65},{33,97},{65,1},{97,33},{2,66}... | collective-permute-start | bytes 786440 | tf_op jit(solution)/shard_map/ppermute | solution.py:30
  231.3 17.0 %collective-permute-start.26 = (bf16[2,512,128]{2,1,0:T(8,128)(2,1)S(1)}, bf16[2,512,128]{2,1,0:T(8,128)(2,1)S(1)}, u32[]{:S(2)}, u32[]{:S(2)}) collective-permute-start(bf16[2,512,128]{2,1,0:T(8,128)(2,1)S(1)} %pad_maximum_fusion.2.refs_0_), channel_id=1, source_target_pairs={{0,8},{8,0},{1,9},{9,1},{2,10},{10,2},{3,11},{11,3},{4,12},{12,4},... | collective-permute-start | bytes 786440 | tf_op jit(solution)/shard_map/ppermute | solution.py:26
  231.4 16.9 %collective-permute-start.27 = (bf16[2,512,128]{2,1,0:T(8,128)(2,1)}, bf16[2,512,128]{2,1,0:T(8,128)(2,1)S(1)}, u32[]{:S(2)}, u32[]{:S(2)}) collective-permute-start(bf16[2,512,128]{2,1,0:T(8,128)(2,1)} %copy-done.25), channel_id=1, source_target_pairs={{0,8},{8,0},{1,9},{9,1},{2,10},{10,2},{3,11},{11,3},{4,12},{12,4},... | collective-permute-start | bytes 786440 | tf_op jit(solution)/shard_map/ppermute | solution.py:26
  236.1 28.8 %collective-permute-start.48 = (bf16[2,512,256]{2,1,0:T(8,128)(2,1)}, bf16[2,512,256]{2,1,0:T(8,128)(2,1)S(1)}, u32[]{:S(2)}, u32[]{:S(2)}) collective-permute-start(bf16[2,512,256]{2,1,0:T(8,128)(2,1)} %add_blocks.2), channel_id=1, source_target_pairs={{0,4},{2,6},{4,0},{6,2},{1,5},{3,7},{5,1},{7,3},{8,12},{10,14},{12... | collective-permute-start | bytes 1572872 | tf_op jit(solution)/shard_map/ppermute | solution.py:30
  236.8 28.1 %collective-permute-start.49 = (bf16[2,512,256]{2,1,0:T(8,128)(2,1)}, bf16[2,512,256]{2,1,0:T(8,128)(2,1)S(1)}, u32[]{:S(2)}, u32[]{:S(2)}) collective-permute-start(bf16[2,512,256]{2,1,0:T(8,128)(2,1)} %add_blocks.3), channel_id=1, source_target_pairs={{0,1},{1,0},{2,3},{3,2},{4,5},{5,4},{6,7},{7,6},{8,9},{9,8},{10,11... | collective-permute-start | bytes 1572872 | tf_op jit(solution)/shard_map/ppermute | solution.py:26
  246.9 14.8 %collective-permute-start.44 = (bf16[528,256]{1,0:T(8,128)(2,1)}, bf16[528,256]{1,0:T(8,128)(2,1)S(1)}, u32[]{:S(2)}, u32[]{:S(2)}) collective-permute-start(bf16[528,256]{1,0:T(8,128)(2,1)} %get-tuple-element.60), channel_id=1, source_target_pairs={{0,16},{16,0},{1,17},{17,1},{2,18},{18,2},{3,19},{19,3},{4,20},{20... | collective-permute-start | bytes 811016 | tf_op jit(solution)/shard_map/ppermute | solution.py:26
  (62 other events, 784.9 us)
